TPU v7x, 128 devices: a whole 4x4x4 slice. The times are simulated.
128 devices in a mesh: row: 32 (over y, x, core), col: 4 (over z).
Axes of the slice: x: 4, y: 4, z: 4, core: 2. Of those that a mesh axis runs over, the one named last changes fastest.
Arguments:
- velocity: float32 [512, 512, 2048], P(None, 'row', 'col'), may hold values from -6 to 6
- symbol_x: float32 [512], replicated, may hold values from 0.3 to 3
- symbol_y: float32 [512], replicated, may hold values from 0.3 to 3
- symbol_z: float32 [2048], replicated, may hold values from 0.3 to 3
Outputs:
- coefficients: float32 [512, 512, 2048], P('row', 'col')
All inputs are finite; a program needn't handle non-finite values.
Results may differ from a plain program's by a relative error of at most 0.000076.
Values sent between devices are 32-bit elements; how exact they have to be, the bound alone decides.
No kernel may reach another device: no remote copies, remote signals or barrier semaphores. Data moves between devices by JAX's collectives and lax.ppermute only.
A program may use at most 192 MiB of HBM per device.

v0:
```python
import jax
import jax.numpy as jnp
from jax import lax
from jax.sharding import PartitionSpec as P


def cut_along(x, dim, devices):
    dims = x.shape
    parts = x.reshape(*dims[:dim], devices, dims[dim] // devices, *dims[dim + 1 :])
    return jnp.moveaxis(parts, dim, 0)


def cut_rows(length, count):
    lap = length // count
    if lap >= 8:
        lap -= lap % 8
    return [lap * k for k in range(1, count)]


def joined_along(parts, dim):
    parts = jnp.moveaxis(parts, 0, dim)
    dims = parts.shape
    return parts.reshape(*dims[:dim], dims[dim] * dims[dim + 1], *dims[dim + 2 :])


def exchange_in_pieces(x, axis, pieces, split_dim, concat_dim):
    parts = cut_along(x, split_dim, lax.axis_size(axis))
    widest = max(range(1, max(2, parts.ndim - 1)), key=lambda d: parts.shape[d])
    finished = []
    for share in jnp.split(parts, cut_rows(parts.shape[widest], pieces), axis=widest):
        if share.size:
            finished.append(lax.all_to_all(share, axis, split_axis=0, concat_axis=0, tiled=True))
    return joined_along(jnp.concatenate(finished, axis=widest), concat_dim)


def mode_table(count):
    rank = jnp.arange(count)
    angle = 2.0 * jnp.pi / count * (rank[:, None] * rank[None, :] % count).astype(jnp.float32)
    return (jnp.cos(angle) + jnp.sin(angle)) * count ** (-0.5)


def along_dim(values, dim):
    moved = jnp.tensordot(
        values, mode_table(values.shape[dim]), axes=([dim], [0]), precision=lax.Precision.HIGHEST
    )
    return jnp.moveaxis(moved, -1, dim)


def local(velocity, symbol_x, symbol_y, symbol_z):
    part_values = velocity
    part_values = along_dim(part_values, 0)
    part_values = lax.all_to_all(part_values, "row", split_axis=0, concat_axis=1, tiled=True)
    part_values = along_dim(part_values, 1)
    pencil_values = part_values
    pencil_values = exchange_in_pieces(pencil_values, "col", 2, 1, 2)
    pencil_values = along_dim(pencil_values, 2)
    share_x = pencil_values.shape[0]
    part_x = lax.dynamic_slice_in_dim(symbol_x, lax.axis_index("row") * share_x, share_x)
    share_y = pencil_values.shape[1]
    part_y = lax.dynamic_slice_in_dim(symbol_y, lax.axis_index("col") * share_y, share_y)
    symbol = part_x[:, None, None] + part_y[None, :, None] + symbol_z[None, None, :]
    pencil_values = pencil_values * ((1.0 - 0.2 * symbol) / (1.0 + 0.2 * symbol))
    return pencil_values


def solution(mesh):
    placed = (P(None, "row", "col"), P(), P(), P())
    return jax.shard_map(
        local, mesh=mesh, in_specs=placed, out_specs=P("row", "col", None), check_vma=False
    )
```

profile of v0, /device:TPU:0, one launch (start us, length us, event | category | flops | bytes accessed | tf_op | source)
XLA Modules:
  0.0 663.7 jit_solution(2667797766476617710)
XLA Ops:
  0.0 4.2 fusion.53
  4.2 38.2 %fusion.5 = f32[512,16,512]{2,0,1:T(8,128)S(1)} fusion(f32[512,16,512]{2,1,0:T(8,128)} %param.4, f32[512,512,1]{0,1,2:T(8,128)S(1)} %fusion.53), kind=kOutput, calls=%fused_computation.10 | convolution fusion | flops 25769803776 | bytes 34603008 | tf_op jit(solution)/shard_map/dot_general | solution.py:43
  42.4 17.2 %copy.9 = f32[512,16,512]{2,1,0:T(8,128)S(1)} copy(f32[512,16,512]{2,0,1:T(8,128)S(1)} %fusion.5) | data formatting | bytes 33554432 | tf_op jit(solution)/shard_map/dot_general | solution.py:43
  59.6 193.0 %all_to_all.28 = f32[512,16,512]{2,1,0:T(8,128)S(1)} all-to-all(f32[512,16,512]{2,1,0:T(8,128)S(1)} %copy.9), channel_id=1, replica_groups=mesh['row'=32,'col'=4] {'row'}, dimensions={0} | all-to-all | bytes 33554432 | tf_op jit(solution)/shard_map/all_to_all | solution.py:52
  252.6 6.4 copy.10
  259.0 56.4 %fusion.25 = f32[16,512,512]{1,2,0:T(8,128)} fusion(f32[16,512,512]{2,1,0:T(8,128)} %bitcast.37), kind=kOutput, calls=%fused_computation.31 | convolution fusion | flops 25773998080 | bytes 33554432 | tf_op jit(solution)/shard_map/dot_general | solution.py:43
  315.4 6.9 %copy.18 = f32[16,4,128,512]{3,2,0,1:T(8,128)S(1)} copy(f32[16,4,128,512]{3,2,1,0:T(8,128)} %bitcast.38) | data formatting | bytes 33554432 | tf_op jit(solution)/shard_map/reshape | solution.py:9
  322.3 6.9 %fusion.46 = (f32[4,16,64,512]{3,2,1,0:T(8,128)}, f32[4,16,64,512]{3,2,1,0:T(8,128)}) fusion(f32[4,16,128,512]{3,2,1,0:T(8,128)S(1)} %bitcast.35), kind=kLoop, calls=%fused_computation.54 | loop fusion | bytes 33554432 | tf_op jit(solution)/shard_map/split | solution.py:30
  329.3 102.6 %all_to_all.29 = f32[4,16,64,512]{3,2,1,0:T(8,128)} all-to-all(f32[4,16,64,512]{3,2,1,0:T(8,128)} %get-tuple-element.5), channel_id=1, replica_groups=mesh['row'=32,'col'=4] {'col'}, dimensions={0} | all-to-all | bytes 16777216 | tf_op jit(solution)/shard_map/all_to_all | solution.py:32
  431.9 5.6 all-to-all-start.2
  437.5 0.8 dynamic_slice.7
  438.3 0.8 dynamic_slice.6
  439.0 0.1 broadcast_add_fusion
  439.1 67.7 %fusion.4.clone.4 = f32[2048,2048,1]{1,0,2:T(8,128)} fusion(), kind=kLoop, calls=%fused_computation.8.clone.clone.clone.1 | loop fusion | flops 67108864 | bytes 16777216 | tf_op jit(solution)/shard_map/mul | solution.py:62
  506.8 24.4 %all-to-all-done.2 = f32[4,16,64,512]{3,2,1,0:T(8,128)} async-done(((f32[4,16,64,512]{3,2,1,0:T(8,128)}), f32[4,16,64,512]{3,2,1,0:T(8,128)}, u32[]{:S(2)}, u32[]{:S(2)}) %all-to-all-start.2) | async-done | bytes 8388640 | tf_op jit(solution)/shard_map/all_to_all | solution.py:32
  531.2 6.9 %maximum_bitcast_fusion = f32[4,16,16,8,512]{4,3,2,1,0:T(8,128)S(1)} fusion(f32[4,16,64,512]{3,2,1,0:T(8,128)} %all-to-all-done.2, f32[4,16,64,512]{3,2,1,0:T(8,128)} %all_to_all.29), kind=kLoop, calls=%fused_computation.6 | loop fusion | flops 4194304 | bytes 33554432
  538.1 0.0 copy-start
  538.1 6.2 copy.13
  544.4 0.0 copy-done
  544.4 119.0 %divide_multiply_fusion = f32[16,128,2048]{2,1,0:T(8,128)} fusion(f32[2048]{0:T(1024)S(1)} %copy-done, f32[16,128]{1,0:T(8,128)S(1)} %broadcast_add_fusion, f32[16,128,2048]{2,1,0:T(8,128)} %bitcast.39, f32[2048,2048,1]{1,0,2:T(8,128)} %fusion.4.clone.4), kind=kOutput, calls=%fused_computation.12 | convolution fusion | flops 103104380928 | bytes 50348032 | tf_op jit(solution)/shard_map/dot_general | solution.py:43
Async XLA Ops:
  431.9 99.3 %all-to-all-start.2 = ((f32[4,16,64,512]{3,2,1,0:T(8,128)}), f32[4,16,64,512]{3,2,1,0:T(8,128)}, u32[]{:S(2)}, u32[]{:S(2)}) async-start(f32[4,16,64,512]{3,2,1,0:T(8,128)} %get-tuple-element.6), calls=%async_computation.2 | async-start | bytes 16777216 | tf_op jit(solution)/shard_map/all_to_all | solution.py:32
  538.1 6.2 copy-start
where the time goes:
time: 668 us; the launch traced here: 664 us
  blocking collectives  296 us (44%)
  matrix products  214 us (32%)
  other arithmetic  78.8 us (12%)
  local copies, waits for them, and re-layouts  45.2 us (7%)
  waiting for transfers between devices  24.4 us (4%)
    dot_general x3, matrix products, along_dim(): jnp.tensordot(values, mode_table(values.shape[dim]), axes=([dim], [0]), p...  214 us
    all_to_all x1, blocking collectives, local(): lax.all_to_all(part_values, 'row', split_axis=0, concat_axis=1, tiled=True)  193 us
    all_to_all x1, blocking collectives, exchange_in_pieces(): lax.all_to_all(share, axis, split_axis=0, concat_axis=0, tiled=True)  103 us
    mul x1, other arithmetic, local(): pencil_values * ((1.0 - 0.2 * symbol) / (1.0 + 0.2 * symbol))  67.7 us
    all_to_all x1, waiting for transfers between devices, exchange_in_pieces(): lax.all_to_all(share, axis, split_axis=0, concat_axis=0, tiled=True)  24.4 us
    dot_general x1, local copies, waits for them, and re-layouts, along_dim(): jnp.tensordot(values, mode_table(values.shape[dim]), axes=([dim], [0]), p...  17.2 us
  transfers between devices with their start and end apart: 1, of which 1 were waited for; matrix products, arithmetic and copies ran while one was open for 10% of the time, Pallas kernels for 0%

commit v1 on v0

v1 whole, which is shorter than its diff:
```python
import functools

import jax
import jax.numpy as jnp
import numpy as np
from jax import lax
from jax.experimental import pallas as pl
from jax.experimental.pallas import tpu as pltpu
from jax.sharding import PartitionSpec as P

SIZES = (2, 4, 4, 3, 2, 1)
STARTS = (8, 0, 4, 12, 10, 15)
Z_COLS = 512
VMEM = 60 * 2**20


def halves(x):
    high = x.astype(jnp.bfloat16)
    low = (x - high.astype(jnp.float32)).astype(jnp.bfloat16)
    return high, low


def mm(a, b):
    return lax.dot_general(a, b, (((1,), (0,)), ((), ())), preferred_element_type=jnp.float32)


def mm3(table, x):
    n = table.shape[0] // 2
    high, low = halves(x)
    both = mm(table, high)
    return both[:n] + both[n:] + mm(table[:n], low)


def split_table(table):
    high = lax.reduce_precision(table, 8, 7)
    low = table - high
    return high.astype(jnp.bfloat16), low.astype(jnp.bfloat16)


def stacked(table):
    return jnp.concatenate(split_table(table), axis=0)


def small_table(rank, count):
    turns = (rank[:, None] * jnp.arange(count)[None, :] % count).astype(jnp.float32)
    return jnp.cos(2.0 * jnp.pi / count * turns - jnp.pi / 4) * (2.0 / count) ** 0.5


def x_kernel(ys, group, a_ref, v_ref, *o_refs):
    xs = v_ref.shape[0] // ys
    a = a_ref[...]

    def body(s, _):
        y = s * group
        lines = [v_ref[pl.ds(y + k, xs, stride=ys), :] for k in range(group)]
        out = mm3(a, jnp.concatenate(lines, axis=1))
        first = 0
        for o_ref in o_refs:
            modes = o_ref.shape[0] // ys
            for k in range(group):
                o_ref[pl.ds(y + k, modes, stride=ys), :] = out[first : first + modes, 128 * k : 128 * (k + 1)]
            first += modes
        return 0

    lax.fori_loop(0, ys // group, body, 0)


def x_modes(velocity, table, shares):
    xs, ys, zs = velocity.shape
    modes = table.shape[0] // 2
    flat = velocity.reshape(xs * ys, zs)
    group = 4 if modes < 256 else 2
    return pl.pallas_call(
        functools.partial(x_kernel, ys, group),
        grid=(zs // 128,),
        in_specs=[
            pl.BlockSpec((2 * modes, xs), lambda i: (0, 0)),
            pl.BlockSpec((xs * ys, 128), lambda i: (0, i)),
        ],
        out_specs=[pl.BlockSpec((m * ys, 128), lambda i: (0, i)) for m in shares],
        out_shape=[jax.ShapeDtypeStruct((m * ys, zs), jnp.float32) for m in shares],
        compiler_params=pltpu.CompilerParams(vmem_limit_bytes=VMEM),
        cost_estimate=pl.CostEstimate(flops=6 * modes * xs * ys * zs, bytes_accessed=4 * xs * ys * zs, transcendentals=0),
    )(table, flat)


def y_kernel(a_ref, v_ref, *o_refs):
    blocks, _, ys, width = v_ref.shape
    n = blocks * ys
    out = mm3(a_ref[...], v_ref[...].reshape(n, width))
    share = n // len(o_refs)
    for d, o_ref in enumerate(o_refs):
        o_ref[0] = out[d * share : (d + 1) * share]


def y_modes(values, table, parts):
    blocks, planes, ys, zs = values.shape
    n = blocks * ys
    width = 256
    return pl.pallas_call(
        y_kernel,
        grid=(planes, zs // width),
        in_specs=[
            pl.BlockSpec((2 * n, n), lambda i, k: (0, 0)),
            pl.BlockSpec((blocks, 1, ys, width), lambda i, k: (0, i, 0, k)),
        ],
        out_specs=[pl.BlockSpec((1, n // parts, width), lambda i, k: (i, 0, k))] * parts,
        out_shape=[jax.ShapeDtypeStruct((planes, n // parts, zs), jnp.float32)] * parts,
        compiler_params=pltpu.CompilerParams(vmem_limit_bytes=VMEM),
        cost_estimate=pl.CostEstimate(flops=6 * n * n * zs * planes, bytes_accessed=8 * n * zs * planes, transcendentals=0),
    )(table, values)


def table_kernel(cos_ref, sin_ref, plus_ref, minus_ref, high_ref, low_ref):
    inner = plus_ref.shape[0]
    lines = high_ref.shape[0] // inner
    plus, minus = plus_ref[...], minus_ref[...]
    for k in range(lines):
        i = pl.program_id(0) * lines + k
        cos, sin = cos_ref[pl.ds(i, 1), :], sin_ref[pl.ds(i, 1), :]
        high, low = halves(cos * plus + sin * minus)
        high_ref[k * inner : (k + 1) * inner] = high
        low_ref[k * inner : (k + 1) * inner] = low


def wide_table(outer, inner, count):
    rank = jnp.arange(count)
    unit = 2.0 * jnp.pi / count
    a = unit * (outer[:, None] * rank[None, :] % count).astype(jnp.float32)
    b = unit * (inner[:, None] * rank[None, :] % count).astype(jnp.float32)
    scale = count ** (-0.5)
    cos_b, sin_b = jnp.cos(b), jnp.sin(b)
    lines = pl.BlockSpec((len(outer), count), lambda i: (0, 0))
    whole = pl.BlockSpec((len(inner), count), lambda i: (0, 0))
    block = pl.BlockSpec((4 * len(inner), count), lambda i: (i, 0))
    return pl.pallas_call(
        table_kernel,
        grid=(len(outer) // 4,),
        in_specs=[lines, lines, whole, whole],
        out_specs=[block, block],
        out_shape=[jax.ShapeDtypeStruct((count, count), jnp.bfloat16)] * 2,
        compiler_params=pltpu.CompilerParams(vmem_limit_bytes=VMEM),
        cost_estimate=pl.CostEstimate(flops=10**10, bytes_accessed=4 * count * count, transcendentals=0),
    )(jnp.cos(a) * scale, jnp.sin(a) * scale, cos_b + sin_b, cos_b - sin_b)


def z_kernel(parts, *refs):
    v_refs, (h_ref, l_ref, sxy_ref, sz_ref) = refs[:parts], refs[parts : parts + 4]
    o_ref, high_s, low_s = refs[-3:]
    planes, share, zs = v_refs[0].shape
    rows = planes * share
    pair = pl.program_id(1)

    @pl.when(pl.program_id(0) == 0)
    def _():
        for p, v_ref in enumerate(v_refs):
            high, low = halves(v_ref[...].reshape(rows, zs))
            high_s[pair, :, p * zs : (p + 1) * zs] = high
            low_s[pair, :, p * zs : (p + 1) * zs] = low

    high = high_s[pair]
    hr = h_ref[...]
    out = mm(high, hr) + mm(low_s[pair], hr) + mm(high, l_ref[...])
    sxy = sxy_ref[...]
    for c in range(0, out.shape[1], 128):
        step = 0.2 * (sxy + sz_ref[:, c : c + 128])
        done = out[:, c : c + 128] * ((1.0 - step) / (1.0 + step))
        o_ref[:, :, c : c + 128] = done.reshape(planes, share, 128)


def z_modes(values, tables, sxy, symbol_z, start, total, previous):
    parts = len(values)
    planes, share, zs = values[0].shape
    n = parts * zs
    group = planes
    rows = group * share
    pairs = planes // group
    first = start // group
    assert start % group == 0
    cols = Z_COLS
    operands = [*values, *tables, sxy, symbol_z]
    in_specs = [
        pl.BlockSpec((group, share, zs), lambda i, k: (jnp.where(i == 0, k, pairs - 1), 0, 0))
    ] * parts + [
        pl.BlockSpec((n, cols), lambda i, k: (0, i)),
        pl.BlockSpec((n, cols), lambda i, k: (0, i)),
        pl.BlockSpec((rows, 128), lambda i, k: (first + k, 0)),
        pl.BlockSpec((1, cols), lambda i, k: (0, i)),
    ]
    aliases = {}
    if previous is not None:
        aliases = {len(operands): 0}
        operands.append(previous)
        in_specs.append(pl.BlockSpec(memory_space=pl.ANY))
    return pl.pallas_call(
        functools.partial(z_kernel, parts),
        grid=(n // cols, pairs),
        in_specs=in_specs,
        out_specs=pl.BlockSpec((group, share, cols), lambda i, k: (first + k, 0, i)),
        out_shape=jax.ShapeDtypeStruct((total, share, n), jnp.float32),
        scratch_shapes=[pltpu.VMEM((pairs, rows, n), jnp.bfloat16)] * 2,
        input_output_aliases=aliases,
        compiler_params=pltpu.CompilerParams(vmem_limit_bytes=VMEM),
        cost_estimate=pl.CostEstimate(flops=6 * planes * share * n * n, bytes_accessed=4 * n * n + 8 * planes * share * n, transcendentals=0),
    )(*operands)


def local(velocity, symbol_x, symbol_y, symbol_z):
    xs, ys, zs = velocity.shape
    rows, cols = lax.axis_size("row"), lax.axis_size("col")
    me = lax.axis_index("col")
    planes = xs // rows
    all_y, all_z = ys * rows, zs * cols
    share_y = all_y // cols
    part_x = lax.dynamic_slice_in_dim(symbol_x, lax.axis_index("row") * planes, planes)
    part_y = lax.dynamic_slice_in_dim(symbol_y, me * share_y, share_y)
    sxy = jnp.broadcast_to((part_x[:, None] + part_y[None, :])[..., None], (planes, share_y, 128))
    sxy = sxy.reshape(planes * share_y, 128)
    symbol_z = symbol_z.reshape(1, -1)

    y_rank = (jnp.arange(all_y) + me * share_y) % all_y
    y_table = stacked(small_table(y_rank, all_y))
    low_count = 64
    outer = jnp.arange(all_z // low_count) * low_count
    outer = (me + cols - outer // zs) % cols * zs + outer % zs
    z_tables = wide_table(outer, jnp.arange(low_count), all_z)

    x_parts = []
    for pick in (range(1), range(1, len(SIZES))):
        mode = np.concatenate(
            [(np.arange(rows)[:, None] * planes + STARTS[j] + np.arange(SIZES[j])).reshape(-1) for j in pick]
        )
        x_table = stacked(small_table(jnp.asarray(mode, jnp.int32), xs))
        x_parts += x_modes(velocity, x_table, [rows * SIZES[j] for j in pick])

    out = None
    for j, (size, start) in enumerate(zip(SIZES, STARTS)):
        part = x_parts[j].reshape(rows, size, ys, zs)
        part = lax.all_to_all(part, "row", split_axis=0, concat_axis=0, tiled=True)
        part = y_modes(part, y_table, cols)
        part = [part[0]] + [
            lax.ppermute(part[d], "col", [(i, (i + d) % cols) for i in range(cols)]) for d in range(1, cols)
        ]
        out = z_modes(part, z_tables, sxy, symbol_z, start, planes, out)
    return out


def solution(mesh):
    placed = (P(None, "row", "col"), P(), P(), P())
    return jax.shard_map(local, mesh=mesh, in_specs=placed, out_specs=P("row", "col", None), check_vma=False)
```

time: 668 us -> 466 us (0.70)
  matrix products: 214 us -> 0 us
  Pallas kernels: 0 us -> 179 us
  blocking collectives: 296 us -> 164 us
  starting transfers between devices: 5.63 us -> 72.9 us
  other arithmetic: 78.8 us -> 17.4 us
  local copies, waits for them, and re-layouts: 45.2 us -> 7.02 us
    dot_general x3 -> x0, matrix products: 214 us -> none  [along_dim(): jnp.tensordot(values, mode_table(values.shape[dim]), axes=([dim], [0]), p...]
    pallas_call x0 -> x15, Pallas kernels: none -> 179 us  [the longest x6 89.8 us: z_modes(): pl.pallas_call(functools.partial(z_kernel, parts), grid=(n // cols, pairs...]
    all_to_all x2 -> x4, blocking collectives: 296 us -> 164 us  [local(): part = lax.all_to_all(part, 'row', split_axis=0, concat_axis=0, tiled=True)]
    mul x1, other arithmetic: 67.7 us -> 1.93 us  [wide_table(): jnp.sin(a) * scale]
    ppermute x0 -> x18, starting transfers between devices: none -> 60.6 us  [local(): lax.ppermute(part[d], 'col', [(i, (i + d) % cols) for i in range(cols)])]
    all_to_all x1 -> x2, waiting for transfers between devices: 24.4 us -> 2.78 us  [local(): part = lax.all_to_all(part, 'row', split_axis=0, concat_axis=0, tiled=True)]
    ppermute x0 -> x18, waiting for transfers between devices: none -> 21.5 us  [local(): lax.ppermute(part[d], 'col', [(i, (i + d) % cols) for i in range(cols)])]
    dot_general x1 -> x0, local copies, waits for them, and re-layouts: 17.2 us -> none  [along_dim(): jnp.tensordot(values, mode_table(values.shape[dim]), axes=([dim], [0]), p...]
  transfers between devices with their start and end apart: 1 -> 20, of which waited for: 1 -> 7; matrix products, arithmetic and copies ran while one was open for 10% -> 3% of each run, Pallas kernels for 0% -> 30%
where the time goes in v1:
time: 466 us; the launch traced here: 464 us
  Pallas kernels  179 us (38%)
  blocking collectives  164 us (35%)
  starting transfers between devices  72.9 us (16%)
  waiting for transfers between devices  24.3 us (5%)
  other arithmetic  17.4 us (4%)
  local copies, waits for them, and re-layouts  7.02 us (2%)
    all_to_all x4, blocking collectives, local(): part = lax.all_to_all(part, 'row', split_axis=0, concat_axis=0, tiled=True)  164 us
    pallas_call x6, Pallas kernels, z_modes(): pl.pallas_call(functools.partial(z_kernel, parts), grid=(n // cols, pairs...  89.8 us
    ppermute x18, starting transfers between devices, local(): lax.ppermute(part[d], 'col', [(i, (i + d) % cols) for i in range(cols)])  60.6 us
    pallas_call x2, Pallas kernels, x_modes(): pl.pallas_call(functools.partial(x_kernel, ys, group), grid=(zs // 128,),...  41.7 us
    pallas_call x6, Pallas kernels, y_modes(): pl.pallas_call(y_kernel, grid=(planes, zs // width), in_specs=[pl.BlockSp...  38.2 us
    ppermute x18, waiting for transfers between devices, local(): lax.ppermute(part[d], 'col', [(i, (i + d) % cols) for i in range(cols)])  21.5 us
    all_to_all x2, starting transfers between devices, local(): part = lax.all_to_all(part, 'row', split_axis=0, concat_axis=0, tiled=True)  12.3 us
    convert_element_type x3, other arithmetic, split_table(): return (high.astype(jnp.bfloat16), low.astype(jnp.bfloat16))  9.65 us
  transfers between devices with their start and end apart: 20, of which 7 were waited for; matrix products, arithmetic and copies ran while one was open for 3% of the time, Pallas kernels for 30%

profile of v1, /device:TPU:0, one launch (start us, length us, event | category | flops | bytes accessed | tf_op | source)
XLA Modules:
  0.0 464.4 jit_solution(15094515447942923667)
XLA Ops:
  0.0 4.6 reduce-precision_convert_fusion.1
  4.6 1.0 pad_maximum_fusion.1.a_ref
  5.7 28.6 %shard_map.64 = (f32[2048,512]{1,0:T(8,128)}, f32[2048,512]{1,0:T(8,128)}, f32[1536,512]{1,0:T(8,128)}, f32[1024,512]{1,0:T(8,128)}, f32[512,512]{1,0:T(8,128)}) custom-call(bf16[896,512]{1,0:T(8,128)(2,1)} %pad_maximum_fusion.1.a_ref, f32[8192,512]{1,0:T(8,128)} %bitcast.11), custom_call_target="tpu_custom_call" | custom-call | flops 11274289152 | bytes 16777216 | tf_op jit(solution)/shard_map/pallas_call | solution.py:73
  34.2 7.4 %all-to-all-start = ((f32[32,1,16,512]{3,2,1,0:T(8,128)}), f32[32,1,16,512]{3,2,1,0:T(8,128)S(1)}, u32[]{:S(2)}, u32[]{:S(2)}) async-start(f32[32,1,16,512]{3,2,1,0:T(8,128)} %bitcast.18), calls=%async_computation | async-start | bytes 2097152 | tf_op jit(solution)/shard_map/all_to_all | solution.py:239
  42.9 13.2 %shard_map.71 = f32[1024,512]{1,0:T(8,128)} custom-call(bf16[128,512]{1,0:T(8,128)(2,1)} %pad_maximum_fusion.2.a_ref, f32[8192,512]{1,0:T(8,128)} %bitcast.12), custom_call_target="tpu_custom_call" | custom-call | flops 1610612736 | bytes 16777216 | tf_op jit(solution)/shard_map/pallas_call | solution.py:73
  56.1 2.8 all-to-all-done.v_ref
  58.9 33.4 %all_to_all.30.v_ref = f32[32,2,16,512]{3,2,1,0:T(8,128)} all-to-all(f32[32,2,16,512]{3,2,1,0:T(8,128)} %bitcast.13), channel_id=1, replica_groups=mesh['row'=32,'col'=4] {'row'}, dimensions={0} | all-to-all | bytes 4194304 | tf_op jit(solution)/shard_map/all_to_all | solution.py:239
  92.3 32.1 %all_to_all.31.v_ref = f32[32,2,16,512]{3,2,1,0:T(8,128)} all-to-all(f32[32,2,16,512]{3,2,1,0:T(8,128)S(1)} %bitcast.17), channel_id=1, replica_groups=mesh['row'=32,'col'=4] {'row'}, dimensions={0} | all-to-all | bytes 4194304 | tf_op jit(solution)/shard_map/all_to_all | solution.py:239
  124.4 43.6 %all_to_all.32.v_ref = f32[32,3,16,512]{3,2,1,0:T(8,128)} all-to-all(f32[32,3,16,512]{3,2,1,0:T(8,128)S(1)} %bitcast.16), channel_id=1, replica_groups=mesh['row'=32,'col'=4] {'row'}, dimensions={0} | all-to-all | bytes 6291456 | tf_op jit(solution)/shard_map/all_to_all | solution.py:239
  168.1 54.6 %all_to_all.33.v_ref = f32[32,4,16,512]{3,2,1,0:T(8,128)} all-to-all(f32[32,4,16,512]{3,2,1,0:T(8,128)S(1)} %bitcast.15), channel_id=1, replica_groups=mesh['row'=32,'col'=4] {'row'}, dimensions={0} | all-to-all | bytes 8388608 | tf_op jit(solution)/shard_map/all_to_all | solution.py:239
  222.7 4.9 %all-to-all-start.3 = ((f32[32,4,16,512]{3,2,1,0:T(8,128)}), f32[32,4,16,512]{3,2,1,0:T(8,128)}, u32[]{:S(2)}, u32[]{:S(2)}) async-start(f32[32,4,16,512]{3,2,1,0:T(8,128)} %bitcast.14), calls=%async_computation.3 | async-start | bytes 8388608 | tf_op jit(solution)/shard_map/all_to_all | solution.py:239
  229.2 4.4 reduce-precision_convert_fusion
  233.6 1.0 pad_maximum_fusion.a_ref
  234.7 3.0 fusion.31
  237.7 1.9 sine_multiply_fusion
  239.7 9.0 %shard_map.66 = (bf16[2048,2048]{1,0:T(8,128)(2,1)}, bf16[2048,2048]{1,0:T(8,128)(2,1)}) custom-call(f32[32,2048]{1,0:T(8,128)} %get-tuple-element.74.cos_ref, f32[32,2048]{1,0:T(8,128)} %get-tuple-element.73.sin_ref, f32[64,2048]{1,0:T(8,128)} %get-tuple-element.76.plus_ref, f32[64,2048]{1,0:T(8,128)} %get-tuple-element.75.minus_ref), custom_call_target="tpu_custom_call" | custom-call | flops 10000000000 | bytes 16777216 | tf_op jit(solution)/shard_map/pallas_call | solution.py:136
  248.7 5.1 %shard_map.72 = (f32[2,128,512]{2,1,0:T(8,128)}, f32[2,128,512]{2,1,0:T(8,128)}, f32[2,128,512]{2,1,0:T(8,128)}, f32[2,128,512]{2,1,0:T(8,128)}) custom-call(bf16[1024,512]{1,0:T(8,128)(2,1)} %pad_maximum_fusion.a_ref, f32[32,2,16,512]{3,2,1,0:T(8,128)} %all_to_all.30.v_ref), custom_call_target="tpu_custom_call" | custom-call | flops 1610612736 | bytes 4194304 | tf_op jit(solution)/shard_map/pallas_call | solution.py:100
  253.9 1.9 collective-permute-start.15
  255.8 3.6 collective-permute-start.16
  259.4 1.0 collective-permute-start.17
  260.4 3.3 shard_map.65
  263.7 1.0 collective-permute-start
  265.2 5.1 %shard_map.67 = (f32[2,128,512]{2,1,0:T(8,128)}, f32[2,128,512]{2,1,0:T(8,128)}, f32[2,128,512]{2,1,0:T(8,128)}, f32[2,128,512]{2,1,0:T(8,128)}) custom-call(bf16[1024,512]{1,0:T(8,128)(2,1)} %pad_maximum_fusion.a_ref, f32[32,2,16,512]{3,2,1,0:T(8,128)} %all_to_all.31.v_ref), custom_call_target="tpu_custom_call" | custom-call | flops 1610612736 | bytes 4194304 | tf_op jit(solution)/shard_map/pallas_call | solution.py:100
  270.4 8.8 %shard_map.70 = (f32[4,128,512]{2,1,0:T(8,128)}, f32[4,128,512]{2,1,0:T(8,128)}, f32[4,128,512]{2,1,0:T(8,128)}, f32[4,128,512]{2,1,0:T(8,128)}) custom-call(bf16[1024,512]{1,0:T(8,128)(2,1)} %pad_maximum_fusion.a_ref, f32[32,4,16,512]{3,2,1,0:T(8,128)} %all_to_all.33.v_ref), custom_call_target="tpu_custom_call" | custom-call | flops 3221225472 | bytes 8388608 | tf_op jit(solution)/shard_map/pallas_call | solution.py:100
  279.1 2.7 collective-permute-start.12
  281.8 1.8 collective-permute-done.16.refs_2_
  284.9 0.8 copy-done.12
  285.7 2.6 collective-permute-start.14
  288.3 1.3 broadcast_in_dim.2.refs_6_
  289.6 12.6 %shard_map.73.refs_8_ = f32[16,128,2048]{2,1,0:T(8,128)} custom-call(f32[2,128,512]{2,1,0:T(8,128)} %get-tuple-element.63.refs_0_, f32[2,128,512]{2,1,0:T(8,128)} %copy-done.10, f32[2,128,512]{2,1,0:T(8,128)} %copy-done.11, f32[2,128,512]{2,1,0:T(8,128)} %copy-done.12, bf16[2048,2048]{1,0:T(8,128)(2,1)} %get-tuple-element.41.refs_4_, ...), custom_call_target="tpu_custom_call" | custom-call | flops 6442450944 | bytes 20971520 | tf_op jit(solution)/shard_map/pallas_call | solution.py:195
  302.2 7.0 %shard_map.68 = (f32[3,128,512]{2,1,0:T(8,128)}, f32[3,128,512]{2,1,0:T(8,128)}, f32[3,128,512]{2,1,0:T(8,128)}, f32[3,128,512]{2,1,0:T(8,128)}) custom-call(bf16[1024,512]{1,0:T(8,128)(2,1)} %pad_maximum_fusion.a_ref, f32[32,3,16,512]{3,2,1,0:T(8,128)} %all_to_all.32.v_ref), custom_call_target="tpu_custom_call" | custom-call | flops 2415919104 | bytes 6291456 | tf_op jit(solution)/shard_map/pallas_call | solution.py:100
  309.2 8.8 %shard_map.69 = (f32[4,128,512]{2,1,0:T(8,128)}, f32[4,128,512]{2,1,0:T(8,128)}, f32[4,128,512]{2,1,0:T(8,128)}, f32[4,128,512]{2,1,0:T(8,128)}) custom-call(bf16[1024,512]{1,0:T(8,128)(2,1)} %pad_maximum_fusion.a_ref, f32[32,4,16,512]{3,2,1,0:T(8,128)} %all-to-all-done.3.v_ref), custom_call_target="tpu_custom_call" | custom-call | flops 3221225472 | bytes 8388608 | tf_op jit(solution)/shard_map/pallas_call | solution.py:100
  318.0 18.4 %collective-permute-start.9 = (f32[4,128,512]{2,1,0:T(8,128)}, f32[4,128,512]{2,1,0:T(8,128)}, u32[]{:S(2)}, u32[]{:S(2)}) collective-permute-start(f32[4,128,512]{2,1,0:T(8,128)} %get-tuple-element.55), channel_id=1, source_target_pairs={{0,1},{1,2},{2,3},{3,0},{4,5},{5,6},{6,7},{7,4},{8,9},{9,10},{10,1... | collective-permute-start | bytes 3145736 | tf_op jit(solution)/shard_map/ppermute | solution.py:242
  336.4 3.5 collective-permute-done.13.refs_2_
  339.9 2.0 collective-permute-start.11
  341.9 19.5 %shard_map.74.refs_8_ = f32[16,128,2048]{2,1,0:T(8,128)} custom-call(f32[4,128,512]{2,1,0:T(8,128)} %get-tuple-element.59.refs_0_, f32[4,128,512]{2,1,0:T(8,128)} %copy-done.3, f32[4,128,512]{2,1,0:T(8,128)} %copy-done.4, f32[4,128,512]{2,1,0:T(8,128)} %copy-done.5, bf16[2048,2048]{1,0:T(8,128)(2,1)} %get-tuple-element.41.refs_4_, ...), custom_call_target="tpu_custom_call", output_to_operand_aliasing={{}: (8, {})} | custom-call | flops 12884901888 | bytes 25165824 | tf_op jit(solution)/shard_map/pallas_call | solution.py:195
  361.5 2.0 collective-permute-done.9.refs_1_
  363.5 15.9 %collective-permute-start.6 = (f32[3,128,512]{2,1,0:T(8,128)}, f32[3,128,512]{2,1,0:T(8,128)S(1)}, u32[]{:S(2)}, u32[]{:S(2)}) collective-permute-start(f32[3,128,512]{2,1,0:T(8,128)} %get-tuple-element.50), channel_id=1, source_target_pairs={{0,1},{1,2},{2,3},{3,0},{4,5},{5,6},{6,7},{7,4},{8,9},{9,10},{10,1... | collective-permute-start | bytes 2359304 | tf_op jit(solution)/shard_map/ppermute | solution.py:242
  379.4 6.7 %collective-permute-done.10.refs_2_ = f32[4,128,512]{2,1,0:T(8,128)} collective-permute-done((f32[4,128,512]{2,1,0:T(8,128)}, f32[4,128,512]{2,1,0:T(8,128)}, u32[]{:S(2)}, u32[]{:S(2)}) %collective-permute-start.10) | collective-permute-done | bytes 1048608 | tf_op jit(solution)/shard_map/ppermute | solution.py:242
  386.8 1.9 collective-permute-start.8
  388.7 19.5 %shard_map.75.refs_8_ = f32[16,128,2048]{2,1,0:T(8,128)} custom-call(f32[4,128,512]{2,1,0:T(8,128)} %get-tuple-element.54.refs_0_, f32[4,128,512]{2,1,0:T(8,128)} %collective-permute-done.9.refs_1_, f32[4,128,512]{2,1,0:T(8,128)} %collective-permute-done.10.refs_2_, f32[4,128,512]{2,1,0:T(8,128)} %collective-permute-done.11.refs_3_, ...), custom_call_target="tpu_custom_call", output_to_operand_aliasing={{}: (8, {})} | custom-call | flops 12884901888 | bytes 25165824 | tf_op jit(solution)/shard_map/pallas_call | solution.py:195
  408.2 4.8 %collective-permute-start.3 = (f32[2,128,512]{2,1,0:T(8,128)}, f32[2,128,512]{2,1,0:T(8,128)S(1)}, u32[]{:S(2)}, u32[]{:S(2)}) collective-permute-start(f32[2,128,512]{2,1,0:T(8,128)} %get-tuple-element.45), channel_id=1, source_target_pairs={{0,1},{1,2},{2,3},{3,0},{4,5},{5,6},{6,7},{7,4},{8,9},{9,10},{10,1... | collective-permute-start | bytes 1572872 | tf_op jit(solution)/shard_map/ppermute | solution.py:242
  413.0 6.8 %collective-permute-done.7.refs_2_ = f32[3,128,512]{2,1,0:T(8,128)S(1)} collective-permute-done((f32[3,128,512]{2,1,0:T(8,128)}, f32[3,128,512]{2,1,0:T(8,128)S(1)}, u32[]{:S(2)}, u32[]{:S(2)}) %collective-permute-start.7) | collective-permute-done | bytes 786464 | tf_op jit(solution)/shard_map/ppermute | solution.py:242
  421.3 15.7 %shard_map.76.refs_8_ = f32[16,128,2048]{2,1,0:T(8,128)} custom-call(f32[3,128,512]{2,1,0:T(8,128)} %get-tuple-element.49.refs_0_, f32[3,128,512]{2,1,0:T(8,128)} %copy-done.7, f32[3,128,512]{2,1,0:T(8,128)} %copy-done.8, f32[3,128,512]{2,1,0:T(8,128)} %copy-done.9, bf16[2048,2048]{1,0:T(8,128)(2,1)} %get-tuple-element.41.refs_4_, ...), custom_call_target="tpu_custom_call", output_to_operand_aliasing={{}: (8, {})} | custom-call | flops 9663676416 | bytes 23068672 | tf_op jit(solution)/shard_map/pallas_call | solution.py:195
  437.0 2.7 collective-permute-start.2
  440.2 0.8 copy-done.14
  441.2 12.6 %shard_map.77.refs_8_ = f32[16,128,2048]{2,1,0:T(8,128)} custom-call(f32[2,128,512]{2,1,0:T(8,128)} %get-tuple-element.44.refs_0_, f32[2,128,512]{2,1,0:T(8,128)} %copy-done.13, f32[2,128,512]{2,1,0:T(8,128)} %copy-done.14, f32[2,128,512]{2,1,0:T(8,128)} %copy-done.15, bf16[2048,2048]{1,0:T(8,128)(2,1)} %get-tuple-element.41.refs_4_, ...), custom_call_target="tpu_custom_call", output_to_operand_aliasing={{}: (8, {})} | custom-call | flops 6442450944 | bytes 20971520 | tf_op jit(solution)/shard_map/pallas_call | solution.py:195
  454.5 9.9 %shard_map.78 = f32[16,128,2048]{2,1,0:T(8,128)} custom-call(f32[1,128,512]{2,1,0:T(8,128)} %get-tuple-element.37.refs_0_, f32[1,128,512]{2,1,0:T(8,128)} %collective-permute-done.refs_1_, f32[1,128,512]{2,1,0:T(8,128)} %collective-permute-done.1.refs_2_, f32[1,128,512]{2,1,0:T(8,128)} %copy-done.16, ...), custom_call_target="tpu_custom_call", output_to_operand_aliasing={{}: (8, {})} | custom-call | flops 3221225472 | bytes 18874368 | tf_op jit(solution)/shard_map/pallas_call | solution.py:195
  (62 shorter events, 8.2 us)
Async XLA Ops:
  5.7 36.0 %copy-start.17 = (s32[64]{0:T(128)S(1)}, s32[64]{0:T(128)}, u32[]{:S(2)}) copy-start(s32[64]{0:T(128)} %constant.134.clone) | copy-start | bytes 772
  34.2 24.7 %all-to-all-start = ((f32[32,1,16,512]{3,2,1,0:T(8,128)}), f32[32,1,16,512]{3,2,1,0:T(8,128)S(1)}, u32[]{:S(2)}, u32[]{:S(2)}) async-start(f32[32,1,16,512]{3,2,1,0:T(8,128)} %bitcast.18), calls=%async_computation | async-start | bytes 2097152 | tf_op jit(solution)/shard_map/all_to_all | solution.py:239
  56.1 36.2 %copy-start.2 = (f32[1024,512]{1,0:T(8,128)S(1)}, f32[1024,512]{1,0:T(8,128)}, u32[]{:S(2)}) copy-start(f32[1024,512]{1,0:T(8,128)} %get-tuple-element.43) | copy-start | bytes 6291460
  58.9 65.6 %copy-start.6 = (f32[32,1,16,512]{3,2,1,0:T(8,128)}, f32[32,1,16,512]{3,2,1,0:T(8,128)S(1)}, u32[]{:S(2)}) copy-start(f32[32,1,16,512]{3,2,1,0:T(8,128)S(1)} %all-to-all-done.v_ref) | copy-start | bytes 3145732
  58.9 65.6 %copy-start.1 = (f32[1536,512]{1,0:T(8,128)S(1)}, f32[1536,512]{1,0:T(8,128)}, u32[]{:S(2)}) copy-start(f32[1536,512]{1,0:T(8,128)} %get-tuple-element.48) | copy-start | bytes 9437188
  124.4 43.6 %copy-start = (f32[2048,512]{1,0:T(8,128)S(1)}, f32[2048,512]{1,0:T(8,128)}, u32[]{:S(2)}) copy-start(f32[2048,512]{1,0:T(8,128)} %get-tuple-element.58) | copy-start | bytes 12582916
  222.7 86.5 %all-to-all-start.3 = ((f32[32,4,16,512]{3,2,1,0:T(8,128)}), f32[32,4,16,512]{3,2,1,0:T(8,128)}, u32[]{:S(2)}, u32[]{:S(2)}) async-start(f32[32,4,16,512]{3,2,1,0:T(8,128)} %bitcast.14), calls=%async_computation.3 | async-start | bytes 8388608 | tf_op jit(solution)/shard_map/all_to_all | solution.py:239
  253.9 25.3 %collective-permute-start.15 = (f32[2,128,512]{2,1,0:T(8,128)}, f32[2,128,512]{2,1,0:T(8,128)S(1)}, u32[]{:S(2)}, u32[]{:S(2)}) collective-permute-start(f32[2,128,512]{2,1,0:T(8,128)} %get-tuple-element.64), channel_id=1, source_target_pairs={{0,1},{1,2},{2,3},{3,0},{4,5},{5,6},{6,7},{7,4},{8,9},{9,10},{10,1... | collective-permute-start | bytes 1572872 | tf_op jit(solution)/shard_map/ppermute | solution.py:242
  255.8 27.8 %collective-permute-start.16 = (f32[2,128,512]{2,1,0:T(8,128)}, f32[2,128,512]{2,1,0:T(8,128)S(1)}, u32[]{:S(2)}, u32[]{:S(2)}) collective-permute-start(f32[2,128,512]{2,1,0:T(8,128)} %get-tuple-element.65), channel_id=1, source_target_pairs={{0,2},{1,3},{2,0},{3,1},{4,6},{5,7},{6,4},{7,5},{8,10},{9,11},{10,... | collective-permute-start | bytes 1572872 | tf_op jit(solution)/shard_map/ppermute | solution.py:242
  259.4 25.5 %collective-permute-start.17 = (f32[2,128,512]{2,1,0:T(8,128)}, f32[2,128,512]{2,1,0:T(8,128)S(1)}, u32[]{:S(2)}, u32[]{:S(2)}) collective-permute-start(f32[2,128,512]{2,1,0:T(8,128)} %get-tuple-element.66), channel_id=1, source_target_pairs={{0,3},{1,0},{2,1},{3,2},{4,7},{5,4},{6,5},{7,6},{8,11},{9,8},{10,9... | collective-permute-start | bytes 1572872 | tf_op jit(solution)/shard_map/ppermute | solution.py:242
  263.7 190.1 %collective-permute-start = (f32[1,128,512]{2,1,0:T(8,128)}, f32[1,128,512]{2,1,0:T(8,128)}, u32[]{:S(2)}, u32[]{:S(2)}) collective-permute-start(f32[1,128,512]{2,1,0:T(8,128)} %get-tuple-element.38), channel_id=1, source_target_pairs={{0,1},{1,2},{2,3},{3,0},{4,5},{5,6},{6,7},{7,4},{8,9},{9,10},{10,1... | collective-permute-start | bytes 786440 | tf_op jit(solution)/shard_map/ppermute | solution.py:242
  264.7 189.1 %collective-permute-start.1 = (f32[1,128,512]{2,1,0:T(8,128)}, f32[1,128,512]{2,1,0:T(8,128)}, u32[]{:S(2)}, u32[]{:S(2)}) collective-permute-start(f32[1,128,512]{2,1,0:T(8,128)} %get-tuple-element.39), channel_id=1, source_target_pairs={{0,2},{1,3},{2,0},{3,1},{4,6},{5,7},{6,4},{7,5},{8,10},{9,11},{10,... | collective-permute-start | bytes 786440 | tf_op jit(solution)/shard_map/ppermute | solution.py:242
  279.1 10.4 %copy-start.10 = (f32[2,128,512]{2,1,0:T(8,128)}, f32[2,128,512]{2,1,0:T(8,128)S(1)}, u32[]{:S(2)}) copy-start(f32[2,128,512]{2,1,0:T(8,128)S(1)} %collective-permute-done.15.refs_1_) | copy-start | bytes 1572868
  279.1 38.9 %collective-permute-start.12 = (f32[4,128,512]{2,1,0:T(8,128)}, f32[4,128,512]{2,1,0:T(8,128)S(1)}, u32[]{:S(2)}, u32[]{:S(2)}) collective-permute-start(f32[4,128,512]{2,1,0:T(8,128)} %get-tuple-element.60), channel_id=1, source_target_pairs={{0,1},{1,2},{2,3},{3,0},{4,5},{5,6},{6,7},{7,4},{8,9},{9,10},{10,1... | collective-permute-start | bytes 3145736 | tf_op jit(solution)/shard_map/ppermute | solution.py:242
  283.6 0.8 copy-start.11
  284.4 55.5 %collective-permute-start.13 = (f32[4,128,512]{2,1,0:T(8,128)}, f32[4,128,512]{2,1,0:T(8,128)S(1)}, u32[]{:S(2)}, u32[]{:S(2)}) collective-permute-start(f32[4,128,512]{2,1,0:T(8,128)} %get-tuple-element.61), channel_id=1, source_target_pairs={{0,2},{1,3},{2,0},{3,1},{4,6},{5,7},{6,4},{7,5},{8,10},{9,11},{10,... | collective-permute-start | bytes 3145736 | tf_op jit(solution)/shard_map/ppermute | solution.py:242
  284.9 0.8 copy-start.12
  285.7 54.2 %collective-permute-start.14 = (f32[4,128,512]{2,1,0:T(8,128)}, f32[4,128,512]{2,1,0:T(8,128)S(1)}, u32[]{:S(2)}, u32[]{:S(2)}) collective-permute-start(f32[4,128,512]{2,1,0:T(8,128)} %get-tuple-element.62), channel_id=1, source_target_pairs={{0,3},{1,0},{2,1},{3,2},{4,7},{5,4},{6,5},{7,6},{8,11},{9,8},{10,9... | collective-permute-start | bytes 3145736 | tf_op jit(solution)/shard_map/ppermute | solution.py:242
  318.0 23.9 %copy-start.3 = (f32[4,128,512]{2,1,0:T(8,128)}, f32[4,128,512]{2,1,0:T(8,128)S(1)}, u32[]{:S(2)}) copy-start(f32[4,128,512]{2,1,0:T(8,128)S(1)} %collective-permute-done.12.refs_1_) | copy-start | bytes 3145732
  318.0 45.5 %collective-permute-start.9 = (f32[4,128,512]{2,1,0:T(8,128)}, f32[4,128,512]{2,1,0:T(8,128)}, u32[]{:S(2)}, u32[]{:S(2)}) collective-permute-start(f32[4,128,512]{2,1,0:T(8,128)} %get-tuple-element.55), channel_id=1, source_target_pairs={{0,1},{1,2},{2,3},{3,0},{4,5},{5,6},{6,7},{7,4},{8,9},{9,10},{10,1... | collective-permute-start | bytes 3145736 | tf_op jit(solution)/shard_map/ppermute | solution.py:242
  339.9 2.0 copy-start.4
  339.9 46.2 %collective-permute-start.10 = (f32[4,128,512]{2,1,0:T(8,128)}, f32[4,128,512]{2,1,0:T(8,128)}, u32[]{:S(2)}, u32[]{:S(2)}) collective-permute-start(f32[4,128,512]{2,1,0:T(8,128)} %get-tuple-element.56), channel_id=1, source_target_pairs={{0,2},{1,3},{2,0},{3,1},{4,6},{5,7},{6,4},{7,5},{8,10},{9,11},{10,... | collective-permute-start | bytes 3145736 | tf_op jit(solution)/shard_map/ppermute | solution.py:242
  339.9 2.0 copy-start.5
  339.9 46.8 %collective-permute-start.11 = (f32[4,128,512]{2,1,0:T(8,128)}, f32[4,128,512]{2,1,0:T(8,128)}, u32[]{:S(2)}, u32[]{:S(2)}) collective-permute-start(f32[4,128,512]{2,1,0:T(8,128)} %get-tuple-element.57), channel_id=1, source_target_pairs={{0,3},{1,0},{2,1},{3,2},{4,7},{5,4},{6,5},{7,6},{8,11},{9,8},{10,9... | collective-permute-start | bytes 3145736 | tf_op jit(solution)/shard_map/ppermute | solution.py:242
  363.5 44.7 %collective-permute-start.6 = (f32[3,128,512]{2,1,0:T(8,128)}, f32[3,128,512]{2,1,0:T(8,128)S(1)}, u32[]{:S(2)}, u32[]{:S(2)}) collective-permute-start(f32[3,128,512]{2,1,0:T(8,128)} %get-tuple-element.50), channel_id=1, source_target_pairs={{0,1},{1,2},{2,3},{3,0},{4,5},{5,6},{6,7},{7,4},{8,9},{9,10},{10,1... | collective-permute-start | bytes 2359304 | tf_op jit(solution)/shard_map/ppermute | solution.py:242
  386.1 33.6 %collective-permute-start.7 = (f32[3,128,512]{2,1,0:T(8,128)}, f32[3,128,512]{2,1,0:T(8,128)S(1)}, u32[]{:S(2)}, u32[]{:S(2)}) collective-permute-start(f32[3,128,512]{2,1,0:T(8,128)} %get-tuple-element.51), channel_id=1, source_target_pairs={{0,2},{1,3},{2,0},{3,1},{4,6},{5,7},{6,4},{7,5},{8,10},{9,11},{10,... | collective-permute-start | bytes 2359304 | tf_op jit(solution)/shard_map/ppermute | solution.py:242
  386.8 33.6 %collective-permute-start.8 = (f32[3,128,512]{2,1,0:T(8,128)}, f32[3,128,512]{2,1,0:T(8,128)S(1)}, u32[]{:S(2)}, u32[]{:S(2)}) collective-permute-start(f32[3,128,512]{2,1,0:T(8,128)} %get-tuple-element.52), channel_id=1, source_target_pairs={{0,3},{1,0},{2,1},{3,2},{4,7},{5,4},{6,5},{7,6},{8,11},{9,8},{10,9... | collective-permute-start | bytes 2359304 | tf_op jit(solution)/shard_map/ppermute | solution.py:242
  408.2 12.2 %copy-start.7 = (f32[3,128,512]{2,1,0:T(8,128)}, f32[3,128,512]{2,1,0:T(8,128)S(1)}, u32[]{:S(2)}) copy-start(f32[3,128,512]{2,1,0:T(8,128)S(1)} %collective-permute-done.6.refs_1_) | copy-start | bytes 2359300
  408.2 28.7 %collective-permute-start.3 = (f32[2,128,512]{2,1,0:T(8,128)}, f32[2,128,512]{2,1,0:T(8,128)S(1)}, u32[]{:S(2)}, u32[]{:S(2)}) collective-permute-start(f32[2,128,512]{2,1,0:T(8,128)} %get-tuple-element.45), channel_id=1, source_target_pairs={{0,1},{1,2},{2,3},{3,0},{4,5},{5,6},{6,7},{7,4},{8,9},{9,10},{10,1... | collective-permute-start | bytes 1572872 | tf_op jit(solution)/shard_map/ppermute | solution.py:242
  419.8 0.9 copy-start.8
  419.8 20.4 %collective-permute-start.4 = (f32[2,128,512]{2,1,0:T(8,128)}, f32[2,128,512]{2,1,0:T(8,128)S(1)}, u32[]{:S(2)}, u32[]{:S(2)}) collective-permute-start(f32[2,128,512]{2,1,0:T(8,128)} %get-tuple-element.46), channel_id=1, source_target_pairs={{0,2},{1,3},{2,0},{3,1},{4,6},{5,7},{6,4},{7,5},{8,10},{9,11},{10,... | collective-permute-start | bytes 1572872 | tf_op jit(solution)/shard_map/ppermute | solution.py:242
  420.4 0.9 copy-start.9
  420.4 19.8 %collective-permute-start.5 = (f32[2,128,512]{2,1,0:T(8,128)}, f32[2,128,512]{2,1,0:T(8,128)S(1)}, u32[]{:S(2)}, u32[]{:S(2)}) collective-permute-start(f32[2,128,512]{2,1,0:T(8,128)} %get-tuple-element.47), channel_id=1, source_target_pairs={{0,3},{1,0},{2,1},{3,2},{4,7},{5,4},{6,5},{7,6},{8,11},{9,8},{10,9... | collective-permute-start | bytes 1572872 | tf_op jit(solution)/shard_map/ppermute | solution.py:242
  437.0 3.3 copy-start.13
  437.0 16.9 %collective-permute-start.2 = (f32[1,128,512]{2,1,0:T(8,128)}, f32[1,128,512]{2,1,0:T(8,128)S(1)}, u32[]{:S(2)}, u32[]{:S(2)}) collective-permute-start(f32[1,128,512]{2,1,0:T(8,128)} %get-tuple-element.40), channel_id=1, source_target_pairs={{0,3},{1,0},{2,1},{3,2},{4,7},{5,4},{6,5},{7,6},{8,11},{9,8},{10,9... | collective-permute-start | bytes 786440 | tf_op jit(solution)/shard_map/ppermute | solution.py:242
  440.2 0.8 copy-start.14
  440.2 1.0 copy-start.15
  453.8 0.7 copy-start.16

commit v2 on v1

--- a/solution.py
+++ b/solution.py
@@ -8,10 +8,12 @@
 from jax.experimental.pallas import tpu as pltpu
 from jax.sharding import PartitionSpec as P
 
-SIZES = (2, 4, 4, 3, 2, 1)
-STARTS = (8, 0, 4, 12, 10, 15)
+SIZES = (3, 4, 4, 3, 2)
+STARTS = (0, 8, 12, 3, 6)
 Z_COLS = 512
-VMEM = 60 * 2**20
+X_FORM = ((4, 2), (4, 2))
+Y_WIDTH = 512
+VMEM = 67043328
 
 
 def halves(x):
@@ -46,42 +48,44 @@
     return jnp.cos(2.0 * jnp.pi / count * turns - jnp.pi / 4) * (2.0 / count) ** 0.5
 
 
-def x_kernel(ys, group, a_ref, v_ref, *o_refs):
-    xs = v_ref.shape[0] // ys
+def x_kernel(group, unroll, a_ref, v_ref, *o_refs):
+    xs, _, tile, lanes = v_ref.shape
+    v_ref = v_ref.reshape(xs * tile, lanes)
+    o_refs = [o_ref.reshape(o_ref.shape[0] * tile, lanes) for o_ref in o_refs]
     a = a_ref[...]
 
     def body(s, _):
         y = s * group
-        lines = [v_ref[pl.ds(y + k, xs, stride=ys), :] for k in range(group)]
+        lines = [v_ref[pl.ds(y + k, xs, stride=tile), :] for k in range(group)]
         out = mm3(a, jnp.concatenate(lines, axis=1))
         first = 0
         for o_ref in o_refs:
-            modes = o_ref.shape[0] // ys
+            modes = o_ref.shape[0] // tile
             for k in range(group):
-                o_ref[pl.ds(y + k, modes, stride=ys), :] = out[first : first + modes, 128 * k : 128 * (k + 1)]
+                o_ref[pl.ds(y + k, modes, stride=tile), :] = out[first : first + modes, lanes * k : lanes * (k + 1)]
             first += modes
         return 0
 
-    lax.fori_loop(0, ys // group, body, 0)
+    lax.fori_loop(0, tile // group, body, 0, unroll=unroll)
 
 
 def x_modes(velocity, table, shares):
     xs, ys, zs = velocity.shape
     modes = table.shape[0] // 2
-    flat = velocity.reshape(xs * ys, zs)
-    group = 4 if modes < 256 else 2
-    return pl.pallas_call(
-        functools.partial(x_kernel, ys, group),
-        grid=(zs // 128,),
+    tile = 8
+    group, unroll = X_FORM[modes < 256]
+    return pl.pallas_call(
+        functools.partial(x_kernel, group, unroll),
+        grid=(zs // 128, ys // tile),
         in_specs=[
-            pl.BlockSpec((2 * modes, xs), lambda i: (0, 0)),
-            pl.BlockSpec((xs * ys, 128), lambda i: (0, i)),
+            pl.BlockSpec((2 * modes, xs), lambda i, k: (0, 0)),
+            pl.BlockSpec((xs, 1, tile, 128), lambda i, k: (0, k, 0, i)),
         ],
-        out_specs=[pl.BlockSpec((m * ys, 128), lambda i: (0, i)) for m in shares],
-        out_shape=[jax.ShapeDtypeStruct((m * ys, zs), jnp.float32) for m in shares],
+        out_specs=[pl.BlockSpec((m, 1, tile, 128), lambda i, k: (0, k, 0, i)) for m in shares],
+        out_shape=[jax.ShapeDtypeStruct((m, ys // tile, tile, zs), jnp.float32) for m in shares],
         compiler_params=pltpu.CompilerParams(vmem_limit_bytes=VMEM),
         cost_estimate=pl.CostEstimate(flops=6 * modes * xs * ys * zs, bytes_accessed=4 * xs * ys * zs, transcendentals=0),
-    )(table, flat)
+    )(table, velocity.reshape(xs, ys // tile, tile, zs))
 
 
 def y_kernel(a_ref, v_ref, *o_refs):
@@ -96,7 +100,7 @@
 def y_modes(values, table, parts):
     blocks, planes, ys, zs = values.shape
     n = blocks * ys
-    width = 256
+    width = Y_WIDTH
     return pl.pallas_call(
         y_kernel,
         grid=(planes, zs // width),

time: 466 us -> 454 us (0.974)
  waiting for transfers between devices: 24.3 us -> 106 us
  blocking collectives: 164 us -> 87.9 us
  Pallas kernels: 179 us -> 153 us
  starting transfers between devices: 72.9 us -> 83.1 us
    all_to_all x4 -> x2, blocking collectives: 164 us -> 87.9 us  [local(): part = lax.all_to_all(part, 'row', split_axis=0, concat_axis=0, tiled=True)]
    all_to_all x2 -> x3, waiting for transfers between devices: 2.78 us -> 67.9 us  [local(): part = lax.all_to_all(part, 'row', split_axis=0, concat_axis=0, tiled=True)]
    ppermute x18 -> x15, waiting for transfers between devices: 21.5 us -> 37.7 us  [local(): lax.ppermute(part[d], 'col', [(i, (i + d) % cols) for i in range(cols)])]
    pallas_call x2, Pallas kernels: 41.7 us -> 30.1 us  [x_modes(): pl.pallas_call(functools.partial(x_kernel, group, unroll), grid=(zs // 12...]
    pallas_call x6 -> x5, Pallas kernels: 38.2 us -> 30.3 us  [y_modes(): pl.pallas_call(y_kernel, grid=(planes, zs // width), in_specs=[pl.BlockSp...]
    pallas_call x6 -> x5, Pallas kernels: 89.8 us -> 83 us  [z_modes(): pl.pallas_call(functools.partial(z_kernel, parts), grid=(n // cols, pairs...]
    all_to_all x2 -> x3, starting transfers between devices: 12.3 us -> 17.4 us  [local(): part = lax.all_to_all(part, 'row', split_axis=0, concat_axis=0, tiled=True)]
    ppermute x18 -> x15, starting transfers between devices: 60.6 us -> 65.7 us  [local(): lax.ppermute(part[d], 'col', [(i, (i + d) % cols) for i in range(cols)])]
  transfers between devices with their start and end apart: 20 -> 18, of which waited for: 7 -> 8; matrix products, arithmetic and copies ran while one was open for 3% -> 4% of each run, Pallas kernels for 30% -> 27%
where the time goes in v2:
time: 454 us; the launch traced here: 453 us
  Pallas kernels  153 us (34%)
  waiting for transfers between devices  106 us (23%)
  blocking collectives  87.9 us (19%)
  starting transfers between devices  83.1 us (18%)
  other arithmetic  18.5 us (4%)
  local copies, waits for them, and re-layouts  5.22 us (1%)
    all_to_all x2, blocking collectives, local(): part = lax.all_to_all(part, 'row', split_axis=0, concat_axis=0, tiled=True)  87.9 us
    pallas_call x5, Pallas kernels, z_modes(): pl.pallas_call(functools.partial(z_kernel, parts), grid=(n // cols, pairs...  83 us
    all_to_all x3, waiting for transfers between devices, local(): part = lax.all_to_all(part, 'row', split_axis=0, concat_axis=0, tiled=True)  67.9 us
    ppermute x15, starting transfers between devices, local(): lax.ppermute(part[d], 'col', [(i, (i + d) % cols) for i in range(cols)])  65.7 us
    ppermute x15, waiting for transfers between devices, local(): lax.ppermute(part[d], 'col', [(i, (i + d) % cols) for i in range(cols)])  37.7 us
    pallas_call x5, Pallas kernels, y_modes(): pl.pallas_call(y_kernel, grid=(planes, zs // width), in_specs=[pl.BlockSp...  30.3 us
    pallas_call x2, Pallas kernels, x_modes(): pl.pallas_call(functools.partial(x_kernel, group, unroll), grid=(zs // 12...  30.1 us
    all_to_all x3, starting transfers between devices, local(): part = lax.all_to_all(part, 'row', split_axis=0, concat_axis=0, tiled=True)  17.4 us
  transfers between devices with their start and end apart: 18, of which 8 were waited for; matrix products, arithmetic and copies ran while one was open for 4% of the time, Pallas kernels for 27%

profile of v2, /device:TPU:0, one launch (start us, length us, event | category | flops | bytes accessed | tf_op | source)
XLA Modules:
  0.0 452.9 jit_solution(9359767936392501839)
XLA Ops:
  0.0 4.2 reduce-precision_convert_fusion.1
  4.2 1.0 pad_maximum_fusion.1.a_ref
  5.2 18.1 %shard_map.64 = (f32[128,2,8,512]{3,2,1,0:T(8,128)}, f32[128,2,8,512]{3,2,1,0:T(8,128)}, f32[96,2,8,512]{3,2,1,0:T(8,128)}, f32[64,2,8,512]{3,2,1,0:T(8,128)}) custom-call(bf16[832,512]{1,0:T(8,128)(2,1)} %pad_maximum_fusion.1.a_ref, f32[512,2,8,512]{3,2,1,0:T(8,128)} %bitcast.10), custom_call_target="tpu_custom_call" | custom-call | flops 10468982784 | bytes 16777216 | tf_op jit(solution)/shard_map/pallas_call | solution.py:77
  23.4 7.7 %all-to-all-start = ((f32[32,2,16,512]{3,2,1,0:T(8,128)}), f32[32,2,16,512]{3,2,1,0:T(8,128)}, u32[]{:S(2)}, u32[]{:S(2)}) async-start(f32[32,2,16,512]{3,2,1,0:T(8,128)} %bitcast.16), calls=%async_computation | async-start | bytes 4194304 | tf_op jit(solution)/shard_map/all_to_all | solution.py:243
  31.1 0.8 reduce-precision_convert_fusion.2
  31.9 0.7 pad_maximum_fusion.2.a_ref
  32.6 12.0 %shard_map.70 = f32[96,2,8,512]{3,2,1,0:T(8,128)} custom-call(bf16[192,512]{1,0:T(8,128)(2,1)} %pad_maximum_fusion.2.a_ref, f32[512,2,8,512]{3,2,1,0:T(8,128)} %bitcast.11), custom_call_target="tpu_custom_call" | custom-call | flops 2415919104 | bytes 16777216 | tf_op jit(solution)/shard_map/pallas_call | solution.py:77
  44.6 16.5 %all-to-all-done.v_ref = f32[32,2,16,512]{3,2,1,0:T(8,128)} async-done(((f32[32,2,16,512]{3,2,1,0:T(8,128)}), f32[32,2,16,512]{3,2,1,0:T(8,128)}, u32[]{:S(2)}, u32[]{:S(2)}) %all-to-all-start) | async-done | bytes 2097184 | tf_op jit(solution)/shard_map/all_to_all | solution.py:243
  61.1 44.5 %all_to_all.25.v_ref = f32[32,3,16,512]{3,2,1,0:T(8,128)} all-to-all(f32[32,3,16,512]{3,2,1,0:T(8,128)} %bitcast.12), channel_id=1, replica_groups=mesh['row'=32,'col'=4] {'row'}, dimensions={0} | all-to-all | bytes 6291456 | tf_op jit(solution)/shard_map/all_to_all | solution.py:243
  105.6 43.4 %all_to_all.26.v_ref = f32[32,3,16,512]{3,2,1,0:T(8,128)} all-to-all(f32[32,3,16,512]{3,2,1,0:T(8,128)S(1)} %bitcast.15), channel_id=1, replica_groups=mesh['row'=32,'col'=4] {'row'}, dimensions={0} | all-to-all | bytes 6291456 | tf_op jit(solution)/shard_map/all_to_all | solution.py:243
  149.0 4.9 %all-to-all-start.3 = ((f32[32,4,16,512]{3,2,1,0:T(8,128)}), f32[32,4,16,512]{3,2,1,0:T(8,128)}, u32[]{:S(2)}, u32[]{:S(2)}) async-start(f32[32,4,16,512]{3,2,1,0:T(8,128)} %bitcast.14), calls=%async_computation.3 | async-start | bytes 8388608 | tf_op jit(solution)/shard_map/all_to_all | solution.py:243
  153.8 1.3 dynamic_slice.7
  155.1 1.2 dynamic_slice.6
  156.4 51.4 %all-to-all-done.3.v_ref = f32[32,4,16,512]{3,2,1,0:T(8,128)} async-done(((f32[32,4,16,512]{3,2,1,0:T(8,128)}), f32[32,4,16,512]{3,2,1,0:T(8,128)}, u32[]{:S(2)}, u32[]{:S(2)}) %all-to-all-start.3) | async-done | bytes 4194336 | tf_op jit(solution)/shard_map/all_to_all | solution.py:243
  207.8 4.9 %all-to-all-start.2 = ((f32[32,4,16,512]{3,2,1,0:T(8,128)}), f32[32,4,16,512]{3,2,1,0:T(8,128)}, u32[]{:S(2)}, u32[]{:S(2)}) async-start(f32[32,4,16,512]{3,2,1,0:T(8,128)} %bitcast.13), calls=%async_computation.2 | async-start | bytes 8388608 | tf_op jit(solution)/shard_map/all_to_all | solution.py:243
  212.7 4.4 reduce-precision_convert_fusion
  217.1 1.1 pad_maximum_fusion.a_ref
  218.2 3.0 fusion.31
  221.2 2.0 sine_multiply_fusion
  223.1 9.1 %shard_map.66 = (bf16[2048,2048]{1,0:T(8,128)(2,1)}, bf16[2048,2048]{1,0:T(8,128)(2,1)}) custom-call(f32[32,2048]{1,0:T(8,128)} %get-tuple-element.64.cos_ref, f32[32,2048]{1,0:T(8,128)} %get-tuple-element.63.sin_ref, f32[64,2048]{1,0:T(8,128)} %get-tuple-element.66.plus_ref, f32[64,2048]{1,0:T(8,128)} %get-tuple-element.65.minus_ref), custom_call_target="tpu_custom_call" | custom-call | flops 10000000000 | bytes 16777216 | tf_op jit(solution)/shard_map/pallas_call | solution.py:140
  232.3 5.9 %shard_map.71 = (f32[3,128,512]{2,1,0:T(8,128)}, f32[3,128,512]{2,1,0:T(8,128)}, f32[3,128,512]{2,1,0:T(8,128)}, f32[3,128,512]{2,1,0:T(8,128)}) custom-call(bf16[1024,512]{1,0:T(8,128)(2,1)} %pad_maximum_fusion.a_ref, f32[32,3,16,512]{3,2,1,0:T(8,128)} %all_to_all.25.v_ref), custom_call_target="tpu_custom_call" | custom-call | flops 2415919104 | bytes 6291456 | tf_op jit(solution)/shard_map/pallas_call | solution.py:104
  238.1 1.9 collective-permute-start.12
  240.1 3.6 collective-permute-start.13
  243.6 1.0 collective-permute-start.14
  245.3 1.2 bitcast_add_fusion
  246.5 4.4 shard_map.65
  250.9 1.0 collective-permute-start
  252.4 5.9 %shard_map.67 = (f32[3,128,512]{2,1,0:T(8,128)}, f32[3,128,512]{2,1,0:T(8,128)}, f32[3,128,512]{2,1,0:T(8,128)}, f32[3,128,512]{2,1,0:T(8,128)}) custom-call(bf16[1024,512]{1,0:T(8,128)(2,1)} %pad_maximum_fusion.a_ref, f32[32,3,16,512]{3,2,1,0:T(8,128)} %all_to_all.26.v_ref), custom_call_target="tpu_custom_call" | custom-call | flops 2415919104 | bytes 6291456 | tf_op jit(solution)/shard_map/pallas_call | solution.py:104
  258.3 7.1 %shard_map.69 = (f32[4,128,512]{2,1,0:T(8,128)}, f32[4,128,512]{2,1,0:T(8,128)}, f32[4,128,512]{2,1,0:T(8,128)}, f32[4,128,512]{2,1,0:T(8,128)}) custom-call(bf16[1024,512]{1,0:T(8,128)(2,1)} %pad_maximum_fusion.a_ref, f32[32,4,16,512]{3,2,1,0:T(8,128)} %all-to-all-done.3.v_ref), custom_call_target="tpu_custom_call" | custom-call | flops 3221225472 | bytes 8388608 | tf_op jit(solution)/shard_map/pallas_call | solution.py:104
  265.4 11.6 %collective-permute-start.9 = (f32[4,128,512]{2,1,0:T(8,128)}, f32[4,128,512]{2,1,0:T(8,128)}, u32[]{:S(2)}, u32[]{:S(2)}) collective-permute-start(f32[4,128,512]{2,1,0:T(8,128)} %get-tuple-element.50), channel_id=1, source_target_pairs={{0,1},{1,2},{2,3},{3,0},{4,5},{5,6},{6,7},{7,4},{8,9},{9,10},{10,1... | collective-permute-start | bytes 3145736 | tf_op jit(solution)/shard_map/ppermute | solution.py:246
  276.9 2.3 collective-permute-done.13.refs_2_
  279.6 2.6 collective-permute-start.11
  282.3 2.1 broadcast_in_dim.2.refs_6_
  284.3 15.7 %shard_map.72.refs_8_ = f32[16,128,2048]{2,1,0:T(8,128)} custom-call(f32[3,128,512]{2,1,0:T(8,128)} %get-tuple-element.53.refs_0_, f32[3,128,512]{2,1,0:T(8,128)} %collective-permute-done.12.refs_1_, f32[3,128,512]{2,1,0:T(8,128)} %collective-permute-done.13.refs_2_, f32[3,128,512]{2,1,0:T(8,128)} %collective-permute-done.14.refs_3_, ...), custom_call_target="tpu_custom_call" | custom-call | flops 9663676416 | bytes 23068672 | tf_op jit(solution)/shard_map/pallas_call | solution.py:199
  300.0 7.0 %shard_map.68 = (f32[4,128,512]{2,1,0:T(8,128)}, f32[4,128,512]{2,1,0:T(8,128)}, f32[4,128,512]{2,1,0:T(8,128)}, f32[4,128,512]{2,1,0:T(8,128)}) custom-call(bf16[1024,512]{1,0:T(8,128)(2,1)} %pad_maximum_fusion.a_ref, f32[32,4,16,512]{3,2,1,0:T(8,128)} %all-to-all-done.2.v_ref), custom_call_target="tpu_custom_call" | custom-call | flops 3221225472 | bytes 8388608 | tf_op jit(solution)/shard_map/pallas_call | solution.py:104
  307.0 15.1 %collective-permute-done.9.refs_1_ = f32[4,128,512]{2,1,0:T(8,128)} collective-permute-done((f32[4,128,512]{2,1,0:T(8,128)}, f32[4,128,512]{2,1,0:T(8,128)}, u32[]{:S(2)}, u32[]{:S(2)}) %collective-permute-start.9) | collective-permute-done | bytes 1048608 | tf_op jit(solution)/shard_map/ppermute | solution.py:246
  322.1 21.0 %collective-permute-start.6 = (f32[4,128,512]{2,1,0:T(8,128)}, f32[4,128,512]{2,1,0:T(8,128)}, u32[]{:S(2)}, u32[]{:S(2)}) collective-permute-start(f32[4,128,512]{2,1,0:T(8,128)} %get-tuple-element.45), channel_id=1, source_target_pairs={{0,1},{1,2},{2,3},{3,0},{4,5},{5,6},{6,7},{7,4},{8,9},{9,10},{10,1... | collective-permute-start | bytes 3145736 | tf_op jit(solution)/shard_map/ppermute | solution.py:246
  343.0 3.7 collective-permute-done.10.refs_2_
  346.8 1.9 collective-permute-start.8
  348.7 19.5 %shard_map.73.refs_8_ = f32[16,128,2048]{2,1,0:T(8,128)} custom-call(f32[4,128,512]{2,1,0:T(8,128)} %get-tuple-element.49.refs_0_, f32[4,128,512]{2,1,0:T(8,128)} %collective-permute-done.9.refs_1_, f32[4,128,512]{2,1,0:T(8,128)} %collective-permute-done.10.refs_2_, f32[4,128,512]{2,1,0:T(8,128)} %collective-permute-done.11.refs_3_, ...), custom_call_target="tpu_custom_call", output_to_operand_aliasing={{}: (8, {})} | custom-call | flops 12884901888 | bytes 25165824 | tf_op jit(solution)/shard_map/pallas_call | solution.py:199
  368.2 2.1 collective-permute-done.6.refs_1_
  370.3 16.1 %collective-permute-start.3 = (f32[3,128,512]{2,1,0:T(8,128)}, f32[3,128,512]{2,1,0:T(8,128)}, u32[]{:S(2)}, u32[]{:S(2)}) collective-permute-start(f32[3,128,512]{2,1,0:T(8,128)} %get-tuple-element.40), channel_id=1, source_target_pairs={{0,1},{1,2},{2,3},{3,0},{4,5},{5,6},{6,7},{7,4},{8,9},{9,10},{10,1... | collective-permute-start | bytes 2359304 | tf_op jit(solution)/shard_map/ppermute | solution.py:246
  386.4 6.5 %collective-permute-done.7.refs_2_ = f32[4,128,512]{2,1,0:T(8,128)} collective-permute-done((f32[4,128,512]{2,1,0:T(8,128)}, f32[4,128,512]{2,1,0:T(8,128)}, u32[]{:S(2)}, u32[]{:S(2)}) %collective-permute-start.7) | collective-permute-done | bytes 1048608 | tf_op jit(solution)/shard_map/ppermute | solution.py:246
  393.4 19.5 %shard_map.74.refs_8_ = f32[16,128,2048]{2,1,0:T(8,128)} custom-call(f32[4,128,512]{2,1,0:T(8,128)} %get-tuple-element.44.refs_0_, f32[4,128,512]{2,1,0:T(8,128)} %collective-permute-done.6.refs_1_, f32[4,128,512]{2,1,0:T(8,128)} %collective-permute-done.7.refs_2_, f32[4,128,512]{2,1,0:T(8,128)} %collective-permute-done.8.refs_3_, ...), custom_call_target="tpu_custom_call", output_to_operand_aliasing={{}: (8, {})} | custom-call | flops 12884901888 | bytes 25165824 | tf_op jit(solution)/shard_map/pallas_call | solution.py:199
  413.0 3.6 collective-permute-start.2
  416.6 8.0 %collective-permute-done.4.refs_2_ = f32[3,128,512]{2,1,0:T(8,128)} collective-permute-done((f32[3,128,512]{2,1,0:T(8,128)}, f32[3,128,512]{2,1,0:T(8,128)}, u32[]{:S(2)}, u32[]{:S(2)}) %collective-permute-start.4) | collective-permute-done | bytes 786464 | tf_op jit(solution)/shard_map/ppermute | solution.py:246
  424.6 15.7 %shard_map.75.refs_8_ = f32[16,128,2048]{2,1,0:T(8,128)} custom-call(f32[3,128,512]{2,1,0:T(8,128)} %get-tuple-element.39.refs_0_, f32[3,128,512]{2,1,0:T(8,128)} %collective-permute-done.3.refs_1_, f32[3,128,512]{2,1,0:T(8,128)} %collective-permute-done.4.refs_2_, f32[3,128,512]{2,1,0:T(8,128)} %collective-permute-done.5.refs_3_, ...), custom_call_target="tpu_custom_call", output_to_operand_aliasing={{}: (8, {})} | custom-call | flops 9663676416 | bytes 23068672 | tf_op jit(solution)/shard_map/pallas_call | solution.py:199
  440.3 12.6 %shard_map.76 = f32[16,128,2048]{2,1,0:T(8,128)} custom-call(f32[2,128,512]{2,1,0:T(8,128)} %get-tuple-element.32.refs_0_, f32[2,128,512]{2,1,0:T(8,128)} %collective-permute-done.refs_1_, f32[2,128,512]{2,1,0:T(8,128)} %collective-permute-done.1.refs_2_, f32[2,128,512]{2,1,0:T(8,128)} %collective-permute-done.2.refs_3_, ...), custom_call_target="tpu_custom_call", output_to_operand_aliasing={{}: (8, {})} | custom-call | flops 6442450944 | bytes 20971520 | tf_op jit(solution)/shard_map/pallas_call | solution.py:199
  (22 shorter events, 2.0 us)
Async XLA Ops:
  23.4 7.7 %copy-start.1 = (s32[96]{0:T(128)S(1)}, s32[96]{0:T(128)}, u32[]{:S(2)}) copy-start(s32[96]{0:T(128)} %constant.134.clone) | copy-start | bytes 1156
  23.4 37.7 %all-to-all-start = ((f32[32,2,16,512]{3,2,1,0:T(8,128)}), f32[32,2,16,512]{3,2,1,0:T(8,128)}, u32[]{:S(2)}, u32[]{:S(2)}) async-start(f32[32,2,16,512]{3,2,1,0:T(8,128)} %bitcast.16), calls=%async_computation | async-start | bytes 4194304 | tf_op jit(solution)/shard_map/all_to_all | solution.py:243
  44.6 61.0 %copy-start = (f32[96,2,8,512]{3,2,1,0:T(8,128)S(1)}, f32[96,2,8,512]{3,2,1,0:T(8,128)}, u32[]{:S(2)}) copy-start(f32[96,2,8,512]{3,2,1,0:T(8,128)} %get-tuple-element.38) | copy-start | bytes 9437188
  149.0 58.8 %all-to-all-start.3 = ((f32[32,4,16,512]{3,2,1,0:T(8,128)}), f32[32,4,16,512]{3,2,1,0:T(8,128)}, u32[]{:S(2)}, u32[]{:S(2)}) async-start(f32[32,4,16,512]{3,2,1,0:T(8,128)} %bitcast.14), calls=%async_computation.3 | async-start | bytes 8388608 | tf_op jit(solution)/shard_map/all_to_all | solution.py:243
  207.8 92.2 %all-to-all-start.2 = ((f32[32,4,16,512]{3,2,1,0:T(8,128)}), f32[32,4,16,512]{3,2,1,0:T(8,128)}, u32[]{:S(2)}, u32[]{:S(2)}) async-start(f32[32,4,16,512]{3,2,1,0:T(8,128)} %bitcast.13), calls=%async_computation.2 | async-start | bytes 8388608 | tf_op jit(solution)/shard_map/all_to_all | solution.py:243
  238.1 27.2 %collective-permute-start.12 = (f32[3,128,512]{2,1,0:T(8,128)}, f32[3,128,512]{2,1,0:T(8,128)}, u32[]{:S(2)}, u32[]{:S(2)}) collective-permute-start(f32[3,128,512]{2,1,0:T(8,128)} %get-tuple-element.54), channel_id=1, source_target_pairs={{0,1},{1,2},{2,3},{3,0},{4,5},{5,6},{6,7},{7,4},{8,9},{9,10},{10,1... | collective-permute-start | bytes 2359304 | tf_op jit(solution)/shard_map/ppermute | solution.py:246
  240.1 39.2 %collective-permute-start.13 = (f32[3,128,512]{2,1,0:T(8,128)}, f32[3,128,512]{2,1,0:T(8,128)}, u32[]{:S(2)}, u32[]{:S(2)}) collective-permute-start(f32[3,128,512]{2,1,0:T(8,128)} %get-tuple-element.55), channel_id=1, source_target_pairs={{0,2},{1,3},{2,0},{3,1},{4,6},{5,7},{6,4},{7,5},{8,10},{9,11},{10,... | collective-permute-start | bytes 2359304 | tf_op jit(solution)/shard_map/ppermute | solution.py:246
  243.6 36.0 %collective-permute-start.14 = (f32[3,128,512]{2,1,0:T(8,128)}, f32[3,128,512]{2,1,0:T(8,128)}, u32[]{:S(2)}, u32[]{:S(2)}) collective-permute-start(f32[3,128,512]{2,1,0:T(8,128)} %get-tuple-element.56), channel_id=1, source_target_pairs={{0,3},{1,0},{2,1},{3,2},{4,7},{5,4},{6,5},{7,6},{8,11},{9,8},{10,9... | collective-permute-start | bytes 2359304 | tf_op jit(solution)/shard_map/ppermute | solution.py:246
  250.9 189.3 %collective-permute-start = (f32[2,128,512]{2,1,0:T(8,128)}, f32[2,128,512]{2,1,0:T(8,128)}, u32[]{:S(2)}, u32[]{:S(2)}) collective-permute-start(f32[2,128,512]{2,1,0:T(8,128)} %get-tuple-element.33), channel_id=1, source_target_pairs={{0,1},{1,2},{2,3},{3,0},{4,5},{5,6},{6,7},{7,4},{8,9},{9,10},{10,1... | collective-permute-start | bytes 1572872 | tf_op jit(solution)/shard_map/ppermute | solution.py:246
  251.9 188.3 %collective-permute-start.1 = (f32[2,128,512]{2,1,0:T(8,128)}, f32[2,128,512]{2,1,0:T(8,128)}, u32[]{:S(2)}, u32[]{:S(2)}) collective-permute-start(f32[2,128,512]{2,1,0:T(8,128)} %get-tuple-element.34), channel_id=1, source_target_pairs={{0,2},{1,3},{2,0},{3,1},{4,6},{5,7},{6,4},{7,5},{8,10},{9,11},{10,... | collective-permute-start | bytes 1572872 | tf_op jit(solution)/shard_map/ppermute | solution.py:246
  265.4 56.7 %collective-permute-start.9 = (f32[4,128,512]{2,1,0:T(8,128)}, f32[4,128,512]{2,1,0:T(8,128)}, u32[]{:S(2)}, u32[]{:S(2)}) collective-permute-start(f32[4,128,512]{2,1,0:T(8,128)} %get-tuple-element.50), channel_id=1, source_target_pairs={{0,1},{1,2},{2,3},{3,0},{4,5},{5,6},{6,7},{7,4},{8,9},{9,10},{10,1... | collective-permute-start | bytes 3145736 | tf_op jit(solution)/shard_map/ppermute | solution.py:246
  279.2 67.5 %collective-permute-start.10 = (f32[4,128,512]{2,1,0:T(8,128)}, f32[4,128,512]{2,1,0:T(8,128)}, u32[]{:S(2)}, u32[]{:S(2)}) collective-permute-start(f32[4,128,512]{2,1,0:T(8,128)} %get-tuple-element.51), channel_id=1, source_target_pairs={{0,2},{1,3},{2,0},{3,1},{4,6},{5,7},{6,4},{7,5},{8,10},{9,11},{10,... | collective-permute-start | bytes 3145736 | tf_op jit(solution)/shard_map/ppermute | solution.py:246
  279.6 67.1 %collective-permute-start.11 = (f32[4,128,512]{2,1,0:T(8,128)}, f32[4,128,512]{2,1,0:T(8,128)}, u32[]{:S(2)}, u32[]{:S(2)}) collective-permute-start(f32[4,128,512]{2,1,0:T(8,128)} %get-tuple-element.52), channel_id=1, source_target_pairs={{0,3},{1,0},{2,1},{3,2},{4,7},{5,4},{6,5},{7,6},{8,11},{9,8},{10,9... | collective-permute-start | bytes 3145736 | tf_op jit(solution)/shard_map/ppermute | solution.py:246
  322.1 48.2 %collective-permute-start.6 = (f32[4,128,512]{2,1,0:T(8,128)}, f32[4,128,512]{2,1,0:T(8,128)}, u32[]{:S(2)}, u32[]{:S(2)}) collective-permute-start(f32[4,128,512]{2,1,0:T(8,128)} %get-tuple-element.45), channel_id=1, source_target_pairs={{0,1},{1,2},{2,3},{3,0},{4,5},{5,6},{6,7},{7,4},{8,9},{9,10},{10,1... | collective-permute-start | bytes 3145736 | tf_op jit(solution)/shard_map/ppermute | solution.py:246
  346.7 46.2 %collective-permute-start.7 = (f32[4,128,512]{2,1,0:T(8,128)}, f32[4,128,512]{2,1,0:T(8,128)}, u32[]{:S(2)}, u32[]{:S(2)}) collective-permute-start(f32[4,128,512]{2,1,0:T(8,128)} %get-tuple-element.46), channel_id=1, source_target_pairs={{0,2},{1,3},{2,0},{3,1},{4,6},{5,7},{6,4},{7,5},{8,10},{9,11},{10,... | collective-permute-start | bytes 3145736 | tf_op jit(solution)/shard_map/ppermute | solution.py:246
  346.8 46.7 %collective-permute-start.8 = (f32[4,128,512]{2,1,0:T(8,128)}, f32[4,128,512]{2,1,0:T(8,128)}, u32[]{:S(2)}, u32[]{:S(2)}) collective-permute-start(f32[4,128,512]{2,1,0:T(8,128)} %get-tuple-element.47), channel_id=1, source_target_pairs={{0,3},{1,0},{2,1},{3,2},{4,7},{5,4},{6,5},{7,6},{8,11},{9,8},{10,9... | collective-permute-start | bytes 3145736 | tf_op jit(solution)/shard_map/ppermute | solution.py:246
  370.3 42.6 %collective-permute-start.3 = (f32[3,128,512]{2,1,0:T(8,128)}, f32[3,128,512]{2,1,0:T(8,128)}, u32[]{:S(2)}, u32[]{:S(2)}) collective-permute-start(f32[3,128,512]{2,1,0:T(8,128)} %get-tuple-element.40), channel_id=1, source_target_pairs={{0,1},{1,2},{2,3},{3,0},{4,5},{5,6},{6,7},{7,4},{8,9},{9,10},{10,1... | collective-permute-start | bytes 2359304 | tf_op jit(solution)/shard_map/ppermute | solution.py:246
  392.9 31.7 %collective-permute-start.4 = (f32[3,128,512]{2,1,0:T(8,128)}, f32[3,128,512]{2,1,0:T(8,128)}, u32[]{:S(2)}, u32[]{:S(2)}) collective-permute-start(f32[3,128,512]{2,1,0:T(8,128)} %get-tuple-element.41), channel_id=1, source_target_pairs={{0,2},{1,3},{2,0},{3,1},{4,6},{5,7},{6,4},{7,5},{8,10},{9,11},{10,... | collective-permute-start | bytes 2359304 | tf_op jit(solution)/shard_map/ppermute | solution.py:246
  393.4 31.1 %collective-permute-start.5 = (f32[3,128,512]{2,1,0:T(8,128)}, f32[3,128,512]{2,1,0:T(8,128)}, u32[]{:S(2)}, u32[]{:S(2)}) collective-permute-start(f32[3,128,512]{2,1,0:T(8,128)} %get-tuple-element.42), channel_id=1, source_target_pairs={{0,3},{1,0},{2,1},{3,2},{4,7},{5,4},{6,5},{7,6},{8,11},{9,8},{10,9... | collective-permute-start | bytes 2359304 | tf_op jit(solution)/shard_map/ppermute | solution.py:246
  413.0 27.3 %collective-permute-start.2 = (f32[2,128,512]{2,1,0:T(8,128)}, f32[2,128,512]{2,1,0:T(8,128)}, u32[]{:S(2)}, u32[]{:S(2)}) collective-permute-start(f32[2,128,512]{2,1,0:T(8,128)} %get-tuple-element.35), channel_id=1, source_target_pairs={{0,3},{1,0},{2,1},{3,2},{4,7},{5,4},{6,5},{7,6},{8,11},{9,8},{10,9... | collective-permute-start | bytes 1572872 | tf_op jit(solution)/shard_map/ppermute | solution.py:246

commit v3 on v2

--- a/solution.py
+++ b/solution.py
@@ -11,6 +11,7 @@
 SIZES = (3, 4, 4, 3, 2)
 STARTS = (0, 8, 12, 3, 6)
 Z_COLS = 512
+SPLIT = 2
 X_FORM = ((4, 2), (4, 2))
 Y_WIDTH = 512
 VMEM = 67043328
@@ -41,6 +42,14 @@
 
 def stacked(table):
     return jnp.concatenate(split_table(table), axis=0)
+
+
+def stacked_once(rank, count):
+    both = jnp.concatenate([rank, rank])
+    table = small_table(both, count)
+    high = lax.reduce_precision(table, 8, 7)
+    row = lax.broadcasted_iota(jnp.int32, table.shape, 0)
+    return jnp.where(row < len(rank), high, table - high).astype(jnp.bfloat16)
 
 
 def small_table(rank, count):
@@ -148,64 +157,71 @@
     )(jnp.cos(a) * scale, jnp.sin(a) * scale, cos_b + sin_b, cos_b - sin_b)
 
 
-def z_kernel(parts, *refs):
+def z_kernel(parts, summed, final, *refs):
     v_refs, (h_ref, l_ref, sxy_ref, sz_ref) = refs[:parts], refs[parts : parts + 4]
+    sum_ref = refs[parts + 4] if summed else None
     o_ref, high_s, low_s = refs[-3:]
     planes, share, zs = v_refs[0].shape
     rows = planes * share
-    pair = pl.program_id(1)
 
     @pl.when(pl.program_id(0) == 0)
     def _():
         for p, v_ref in enumerate(v_refs):
             high, low = halves(v_ref[...].reshape(rows, zs))
-            high_s[pair, :, p * zs : (p + 1) * zs] = high
-            low_s[pair, :, p * zs : (p + 1) * zs] = low
-
-    high = high_s[pair]
+            high_s[:, p * zs : (p + 1) * zs] = high
+            low_s[:, p * zs : (p + 1) * zs] = low
+
+    high = high_s[...]
     hr = h_ref[...]
-    out = mm(high, hr) + mm(low_s[pair], hr) + mm(high, l_ref[...])
+    out = mm(high, hr) + mm(low_s[...], hr) + mm(high, l_ref[...])
+    cols = out.shape[1]
+    if summed:
+        out = out + sum_ref[...].reshape(rows, cols)
+    if not final:
+        o_ref[...] = out.reshape(planes, share, cols)
+        return
     sxy = sxy_ref[...]
-    for c in range(0, out.shape[1], 128):
+    for c in range(0, cols, 128):
         step = 0.2 * (sxy + sz_ref[:, c : c + 128])
         done = out[:, c : c + 128] * ((1.0 - step) / (1.0 + step))
         o_ref[:, :, c : c + 128] = done.reshape(planes, share, 128)
 
 
-def z_modes(values, tables, sxy, symbol_z, start, total, previous):
-    parts = len(values)
+def z_modes(values, part, tables, sxy, symbol_z, start, total, previous, summed=None, final=True):
     planes, share, zs = values[0].shape
-    n = parts * zs
-    group = planes
-    rows = group * share
-    pairs = planes // group
-    first = start // group
-    assert start % group == 0
+    depth = len(values) * zs
+    n = tables[0].shape[0]
+    rows = planes * share
+    first = start // planes
+    assert start % planes == 0 and part % len(values) == 0
+    block = part // len(values)
     cols = Z_COLS
     operands = [*values, *tables, sxy, symbol_z]
-    in_specs = [
-        pl.BlockSpec((group, share, zs), lambda i, k: (jnp.where(i == 0, k, pairs - 1), 0, 0))
-    ] * parts + [
-        pl.BlockSpec((n, cols), lambda i, k: (0, i)),
-        pl.BlockSpec((n, cols), lambda i, k: (0, i)),
-        pl.BlockSpec((rows, 128), lambda i, k: (first + k, 0)),
-        pl.BlockSpec((1, cols), lambda i, k: (0, i)),
+    in_specs = [pl.BlockSpec((planes, share, zs), lambda i: (0, 0, 0))] * len(values) + [
+        pl.BlockSpec((depth, cols), lambda i: (block, i)),
+        pl.BlockSpec((depth, cols), lambda i: (block, i)),
+        pl.BlockSpec((rows, 128), lambda i: (first, 0)),
+        pl.BlockSpec((1, cols), lambda i: (0, i)),
     ]
+    if summed is not None:
+        operands.append(summed)
+        in_specs.append(pl.BlockSpec((planes, share, cols), lambda i: (0, 0, i)))
     aliases = {}
-    if previous is not None:
+    if final and previous is not None:
         aliases = {len(operands): 0}
         operands.append(previous)
         in_specs.append(pl.BlockSpec(memory_space=pl.ANY))
-    return pl.pallas_call(
-        functools.partial(z_kernel, parts),
-        grid=(n // cols, pairs),
+    place = first if final else 0
+    return pl.pallas_call(
+        functools.partial(z_kernel, len(values), summed is not None, final),
+        grid=(n // cols,),
         in_specs=in_specs,
-        out_specs=pl.BlockSpec((group, share, cols), lambda i, k: (first + k, 0, i)),
-        out_shape=jax.ShapeDtypeStruct((total, share, n), jnp.float32),
-        scratch_shapes=[pltpu.VMEM((pairs, rows, n), jnp.bfloat16)] * 2,
+        out_specs=pl.BlockSpec((planes, share, cols), lambda i: (place, 0, i)),
+        out_shape=jax.ShapeDtypeStruct((total if final else planes, share, n), jnp.float32),
+        scratch_shapes=[pltpu.VMEM((rows, depth), jnp.bfloat16)] * 2,
         input_output_aliases=aliases,
         compiler_params=pltpu.CompilerParams(vmem_limit_bytes=VMEM),
-        cost_estimate=pl.CostEstimate(flops=6 * planes * share * n * n, bytes_accessed=4 * n * n + 8 * planes * share * n, transcendentals=0),
+        cost_estimate=pl.CostEstimate(flops=6 * rows * depth * n, bytes_accessed=4 * depth * n + 8 * rows * n, transcendentals=0),
     )(*operands)
 
 
@@ -226,15 +242,18 @@
     y_table = stacked(small_table(y_rank, all_y))
     low_count = 64
     outer = jnp.arange(all_z // low_count) * low_count
-    outer = (me + cols - outer // zs) % cols * zs + outer % zs
+    hop = outer // zs
+    hop = jnp.where(hop < 2, hop, 5 - hop)
+    outer = (me + cols - hop) % cols * zs + outer % zs
     z_tables = wide_table(outer, jnp.arange(low_count), all_z)
 
     x_parts = []
-    for pick in (range(1), range(1, len(SIZES))):
+    for name, pick in (("x0", range(1)), ("x1", range(1, len(SIZES)))):
         mode = np.concatenate(
             [(np.arange(rows)[:, None] * planes + STARTS[j] + np.arange(SIZES[j])).reshape(-1) for j in pick]
         )
-        x_table = stacked(small_table(jnp.asarray(mode, jnp.int32), xs))
+        mode = jnp.asarray(mode, jnp.int32)
+        x_table = stacked_once(mode, xs) if name == "x0" else stacked(small_table(mode, xs))
         x_parts += x_modes(velocity, x_table, [rows * SIZES[j] for j in pick])
 
     out = None
@@ -242,10 +261,15 @@
         part = x_parts[j].reshape(rows, size, ys, zs)
         part = lax.all_to_all(part, "row", split_axis=0, concat_axis=0, tiled=True)
         part = y_modes(part, y_table, cols)
-        part = [part[0]] + [
-            lax.ppermute(part[d], "col", [(i, (i + d) % cols) for i in range(cols)]) for d in range(1, cols)
-        ]
-        out = z_modes(part, z_tables, sxy, symbol_z, start, planes, out)
+        moved = [part[0]]
+        for d in (1, 3, 2):
+            moved.append(lax.ppermute(part[d], "col", [(i, (i + d) % cols) for i in range(cols)]))
+        rest = (z_tables, sxy, symbol_z, start, planes, out)
+        if j < len(SIZES) - SPLIT:
+            out = z_modes(moved, 0, *rest)
+        else:
+            early = z_modes(moved[:3], 0, *rest, final=False)
+            out = z_modes(moved[3:], 3, *rest, summed=early)
     return out
 
 

time: 454 us -> 446 us (0.982)
  starting transfers between devices: 83.1 us -> 41.5 us
  waiting for transfers between devices: 106 us -> 132 us
  Pallas kernels: 153 us -> 161 us
    ppermute x15, starting transfers between devices: 65.7 us -> 24.1 us  [local(): lax.ppermute(part[d], 'col', [(i, (i + d) % cols) for i in range(cols)])]
    ppermute x15, waiting for transfers between devices: 37.7 us -> 72.4 us  [local(): lax.ppermute(part[d], 'col', [(i, (i + d) % cols) for i in range(cols)])]
    all_to_all x3, waiting for transfers between devices: 67.9 us -> 59.2 us  [local(): part = lax.all_to_all(part, 'row', split_axis=0, concat_axis=0, tiled=True)]
    pallas_call x5 -> x7, Pallas kernels: 83 us -> 91.3 us  [z_modes(): pl.pallas_call(functools.partial(z_kernel, len(values), summed is not Non...]
    convert_element_type x3 -> x2, other arithmetic: 9.47 us -> 8.63 us  [split_table(): return (high.astype(jnp.bfloat16), low.astype(jnp.bfloat16))]
  transfers between devices with their start and end apart: 18 -> 18, of which waited for: 8 -> 8; matrix products, arithmetic and copies ran while one was open for 4% -> 4% of each run, Pallas kernels for 27% -> 31%
where the time goes in v3:
time: 446 us; the launch traced here: 444 us
  Pallas kernels  161 us (36%)
  waiting for transfers between devices  132 us (30%)
  blocking collectives  88.1 us (20%)
  starting transfers between devices  41.5 us (9%)
  other arithmetic  18.6 us (4%)
    pallas_call x7, Pallas kernels, z_modes(): pl.pallas_call(functools.partial(z_kernel, len(values), summed is not Non...  91.3 us
    all_to_all x2, blocking collectives, local(): part = lax.all_to_all(part, 'row', split_axis=0, concat_axis=0, tiled=True)  88.1 us
    ppermute x15, waiting for transfers between devices, local(): lax.ppermute(part[d], 'col', [(i, (i + d) % cols) for i in range(cols)])  72.4 us
    all_to_all x3, waiting for transfers between devices, local(): part = lax.all_to_all(part, 'row', split_axis=0, concat_axis=0, tiled=True)  59.2 us
    pallas_call x5, Pallas kernels, y_modes(): pl.pallas_call(y_kernel, grid=(planes, zs // width), in_specs=[pl.BlockSp...  30.3 us
    pallas_call x2, Pallas kernels, x_modes(): pl.pallas_call(functools.partial(x_kernel, group, unroll), grid=(zs // 12...  30.1 us
    ppermute x15, starting transfers between devices, local(): lax.ppermute(part[d], 'col', [(i, (i + d) % cols) for i in range(cols)])  24.1 us
    all_to_all x3, starting transfers between devices, local(): part = lax.all_to_all(part, 'row', split_axis=0, concat_axis=0, tiled=True)  17.4 us
  transfers between devices with their start and end apart: 18, of which 8 were waited for; matrix products, arithmetic and copies ran while one was open for 4% of the time, Pallas kernels for 31%

profile of v3, /device:TPU:0, one launch (start us, length us, event | category | flops | bytes accessed | tf_op | source)
XLA Modules:
  0.0 444.3 jit_solution(3487627819340378702)
XLA Ops:
  0.0 4.2 reduce-precision_convert_fusion.1
  4.2 1.0 pad_maximum_fusion.1.a_ref
  5.2 18.1 %shard_map.64 = (f32[128,2,8,512]{3,2,1,0:T(8,128)}, f32[128,2,8,512]{3,2,1,0:T(8,128)}, f32[96,2,8,512]{3,2,1,0:T(8,128)}, f32[64,2,8,512]{3,2,1,0:T(8,128)}) custom-call(bf16[832,512]{1,0:T(8,128)(2,1)} %pad_maximum_fusion.1.a_ref, f32[512,2,8,512]{3,2,1,0:T(8,128)} %bitcast.10), custom_call_target="tpu_custom_call" | custom-call | flops 10468982784 | bytes 16777216 | tf_op jit(solution)/shard_map/pallas_call | solution.py:86
  23.3 7.7 %all-to-all-start = ((f32[32,2,16,512]{3,2,1,0:T(8,128)}), f32[32,2,16,512]{3,2,1,0:T(8,128)}, u32[]{:S(2)}, u32[]{:S(2)}) async-start(f32[32,2,16,512]{3,2,1,0:T(8,128)} %bitcast.16), calls=%async_computation | async-start | bytes 4194304 | tf_op jit(solution)/shard_map/all_to_all | solution.py:262
  31.0 2.3 fusion.32.a_ref
  33.3 12.0 %shard_map.72 = f32[96,2,8,512]{3,2,1,0:T(8,128)} custom-call(bf16[192,512]{1,0:T(8,128)(2,1)} %fusion.32.a_ref, f32[512,2,8,512]{3,2,1,0:T(8,128)} %bitcast.11), custom_call_target="tpu_custom_call" | custom-call | flops 2415919104 | bytes 16777216 | tf_op jit(solution)/shard_map/pallas_call | solution.py:86
  45.3 15.7 %all-to-all-done.v_ref = f32[32,2,16,512]{3,2,1,0:T(8,128)} async-done(((f32[32,2,16,512]{3,2,1,0:T(8,128)}), f32[32,2,16,512]{3,2,1,0:T(8,128)}, u32[]{:S(2)}, u32[]{:S(2)}) %all-to-all-start) | async-done | bytes 2097184 | tf_op jit(solution)/shard_map/all_to_all | solution.py:262
  61.0 44.7 %all_to_all.25.v_ref = f32[32,3,16,512]{3,2,1,0:T(8,128)} all-to-all(f32[32,3,16,512]{3,2,1,0:T(8,128)} %bitcast.12), channel_id=1, replica_groups=mesh['row'=32,'col'=4] {'row'}, dimensions={0} | all-to-all | bytes 6291456 | tf_op jit(solution)/shard_map/all_to_all | solution.py:262
  105.7 43.4 %all_to_all.26.v_ref = f32[32,3,16,512]{3,2,1,0:T(8,128)} all-to-all(f32[32,3,16,512]{3,2,1,0:T(8,128)S(1)} %bitcast.15), channel_id=1, replica_groups=mesh['row'=32,'col'=4] {'row'}, dimensions={0} | all-to-all | bytes 6291456 | tf_op jit(solution)/shard_map/all_to_all | solution.py:262
  149.1 4.9 %all-to-all-start.3 = ((f32[32,4,16,512]{3,2,1,0:T(8,128)}), f32[32,4,16,512]{3,2,1,0:T(8,128)}, u32[]{:S(2)}, u32[]{:S(2)}) async-start(f32[32,4,16,512]{3,2,1,0:T(8,128)} %bitcast.14), calls=%async_computation.3 | async-start | bytes 8388608 | tf_op jit(solution)/shard_map/all_to_all | solution.py:262
  154.0 4.4 reduce-precision_convert_fusion
  158.5 1.0 pad_maximum_fusion.a_ref
  159.5 3.0 fusion.41
  162.5 1.9 sine_multiply_fusion
  164.5 43.5 %all-to-all-done.3.v_ref = f32[32,4,16,512]{3,2,1,0:T(8,128)} async-done(((f32[32,4,16,512]{3,2,1,0:T(8,128)}), f32[32,4,16,512]{3,2,1,0:T(8,128)}, u32[]{:S(2)}, u32[]{:S(2)}) %all-to-all-start.3) | async-done | bytes 4194336 | tf_op jit(solution)/shard_map/all_to_all | solution.py:262
  207.9 4.9 %all-to-all-start.2 = ((f32[32,4,16,512]{3,2,1,0:T(8,128)}), f32[32,4,16,512]{3,2,1,0:T(8,128)}, u32[]{:S(2)}, u32[]{:S(2)}) async-start(f32[32,4,16,512]{3,2,1,0:T(8,128)} %bitcast.13), calls=%async_computation.2 | async-start | bytes 8388608 | tf_op jit(solution)/shard_map/all_to_all | solution.py:262
  212.8 4.5 %shard_map.65 = (f32[2,128,512]{2,1,0:T(8,128)}, f32[2,128,512]{2,1,0:T(8,128)}, f32[2,128,512]{2,1,0:T(8,128)}, f32[2,128,512]{2,1,0:T(8,128)}) custom-call(bf16[1024,512]{1,0:T(8,128)(2,1)} %pad_maximum_fusion.a_ref, f32[32,2,16,512]{3,2,1,0:T(8,128)} %all-to-all-done.v_ref), custom_call_target="tpu_custom_call" | custom-call | flops 1610612736 | bytes 4194304 | tf_op jit(solution)/shard_map/pallas_call | solution.py:113
  217.3 1.9 collective-permute-start.1
  219.2 2.3 collective-permute-start.2
  221.5 9.2 %shard_map.66 = (bf16[2048,2048]{1,0:T(8,128)(2,1)}, bf16[2048,2048]{1,0:T(8,128)(2,1)}) custom-call(f32[32,2048]{1,0:T(8,128)} %get-tuple-element.62.cos_ref, f32[32,2048]{1,0:T(8,128)} %get-tuple-element.61.sin_ref, f32[64,2048]{1,0:T(8,128)} %get-tuple-element.64.plus_ref, f32[64,2048]{1,0:T(8,128)} %get-tuple-element.63.minus_ref), custom_call_target="tpu_custom_call" | custom-call | flops 10000000000 | bytes 16777216 | tf_op jit(solution)/shard_map/pallas_call | solution.py:149
  230.7 0.8 dynamic_slice.7
  231.5 0.8 dynamic_slice.6
  232.2 0.7 bitcast_add_fusion
  232.9 5.9 %shard_map.73 = (f32[3,128,512]{2,1,0:T(8,128)}, f32[3,128,512]{2,1,0:T(8,128)}, f32[3,128,512]{2,1,0:T(8,128)}, f32[3,128,512]{2,1,0:T(8,128)}) custom-call(bf16[1024,512]{1,0:T(8,128)(2,1)} %pad_maximum_fusion.a_ref, f32[32,3,16,512]{3,2,1,0:T(8,128)} %all_to_all.25.v_ref), custom_call_target="tpu_custom_call" | custom-call | flops 2415919104 | bytes 6291456 | tf_op jit(solution)/shard_map/pallas_call | solution.py:113
  238.8 3.2 collective-permute-start.13
  242.5 2.0 broadcast_in_dim.2.refs_5_.refs_6_.refs_3_
  244.5 10.4 %shard_map.67.refs_5_ = f32[2,128,2048]{2,1,0:T(8,128)} custom-call(f32[2,128,512]{2,1,0:T(8,128)} %get-tuple-element.35.refs_0_, f32[2,128,512]{2,1,0:T(8,128)} %collective-permute-done.1.refs_1_, f32[2,128,512]{2,1,0:T(8,128)} %collective-permute-done.2.refs_2_, bf16[2048,2048]{1,0:T(8,128)(2,1)} %get-tuple-element.33.refs_3_.refs_4_.refs_1_, ...), custom_call_target="tpu_custom_call" | custom-call | flops 4831838208 | bytes 16777216 | tf_op jit(solution)/shard_map/pallas_call | solution.py:215
  254.9 5.9 %shard_map.68 = (f32[3,128,512]{2,1,0:T(8,128)}, f32[3,128,512]{2,1,0:T(8,128)}, f32[3,128,512]{2,1,0:T(8,128)}, f32[3,128,512]{2,1,0:T(8,128)}) custom-call(bf16[1024,512]{1,0:T(8,128)(2,1)} %pad_maximum_fusion.a_ref, f32[32,3,16,512]{3,2,1,0:T(8,128)} %all_to_all.26.v_ref), custom_call_target="tpu_custom_call" | custom-call | flops 2415919104 | bytes 6291456 | tf_op jit(solution)/shard_map/pallas_call | solution.py:113
  260.8 1.0 collective-permute-start.4
  261.8 2.2 collective-permute-start.5
  264.1 7.0 %shard_map.71 = (f32[4,128,512]{2,1,0:T(8,128)}, f32[4,128,512]{2,1,0:T(8,128)}, f32[4,128,512]{2,1,0:T(8,128)}, f32[4,128,512]{2,1,0:T(8,128)}) custom-call(bf16[1024,512]{1,0:T(8,128)(2,1)} %pad_maximum_fusion.a_ref, f32[32,4,16,512]{3,2,1,0:T(8,128)} %all-to-all-done.3.v_ref), custom_call_target="tpu_custom_call" | custom-call | flops 3221225472 | bytes 8388608 | tf_op jit(solution)/shard_map/pallas_call | solution.py:113
  271.1 4.4 collective-permute-done.12.refs_1_
  275.4 1.6 collective-permute-done.13.refs_2_
  277.0 0.6 collective-permute-done.14.refs_3_
  277.7 3.9 collective-permute-start.9
  281.6 15.7 %shard_map.74.refs_8_ = f32[16,128,2048]{2,1,0:T(8,128)} custom-call(f32[3,128,512]{2,1,0:T(8,128)} %get-tuple-element.53.refs_0_, f32[3,128,512]{2,1,0:T(8,128)} %collective-permute-done.12.refs_1_, f32[3,128,512]{2,1,0:T(8,128)} %collective-permute-done.13.refs_2_, f32[3,128,512]{2,1,0:T(8,128)} %collective-permute-done.14.refs_3_, ...), custom_call_target="tpu_custom_call" | custom-call | flops 9663676416 | bytes 23068672 | tf_op jit(solution)/shard_map/pallas_call | solution.py:215
  297.3 17.4 %collective-permute-done.4.refs_1_ = f32[3,128,512]{2,1,0:T(8,128)} collective-permute-done((f32[3,128,512]{2,1,0:T(8,128)}, f32[3,128,512]{2,1,0:T(8,128)}, u32[]{:S(2)}, u32[]{:S(2)}) %collective-permute-start.4) | collective-permute-done | bytes 786464 | tf_op jit(solution)/shard_map/ppermute | solution.py:266
  314.7 3.5 collective-permute-start.3
  318.3 12.6 %shard_map.69.refs_5_ = f32[3,128,2048]{2,1,0:T(8,128)} custom-call(f32[3,128,512]{2,1,0:T(8,128)} %get-tuple-element.40.refs_0_, f32[3,128,512]{2,1,0:T(8,128)} %collective-permute-done.4.refs_1_, f32[3,128,512]{2,1,0:T(8,128)} %collective-permute-done.5.refs_2_, bf16[2048,2048]{1,0:T(8,128)(2,1)} %get-tuple-element.33.refs_3_.refs_4_.refs_1_, ...), custom_call_target="tpu_custom_call" | custom-call | flops 7247757312 | bytes 18874368 | tf_op jit(solution)/shard_map/pallas_call | solution.py:215
  330.9 7.0 %shard_map.70 = (f32[4,128,512]{2,1,0:T(8,128)}, f32[4,128,512]{2,1,0:T(8,128)}, f32[4,128,512]{2,1,0:T(8,128)}, f32[4,128,512]{2,1,0:T(8,128)}) custom-call(bf16[1024,512]{1,0:T(8,128)(2,1)} %pad_maximum_fusion.a_ref, f32[32,4,16,512]{3,2,1,0:T(8,128)} %all-to-all-done.2.v_ref), custom_call_target="tpu_custom_call" | custom-call | flops 3221225472 | bytes 8388608 | tf_op jit(solution)/shard_map/pallas_call | solution.py:113
  337.9 29.0 %collective-permute-done.10.refs_2_ = f32[4,128,512]{2,1,0:T(8,128)} collective-permute-done((f32[4,128,512]{2,1,0:T(8,128)}, f32[4,128,512]{2,1,0:T(8,128)}, u32[]{:S(2)}, u32[]{:S(2)}) %collective-permute-start.10) | collective-permute-done | bytes 1048608 | tf_op jit(solution)/shard_map/ppermute | solution.py:266
  366.9 3.7 collective-permute-start.7
  370.6 1.8 collective-permute-start.8
  372.3 19.5 %shard_map.75.refs_8_ = f32[16,128,2048]{2,1,0:T(8,128)} custom-call(f32[4,128,512]{2,1,0:T(8,128)} %get-tuple-element.49.refs_0_, f32[4,128,512]{2,1,0:T(8,128)} %collective-permute-done.9.refs_1_, f32[4,128,512]{2,1,0:T(8,128)} %collective-permute-done.10.refs_2_, f32[4,128,512]{2,1,0:T(8,128)} %collective-permute-done.11.refs_3_, ...), custom_call_target="tpu_custom_call", output_to_operand_aliasing={{}: (8, {})} | custom-call | flops 12884901888 | bytes 25165824 | tf_op jit(solution)/shard_map/pallas_call | solution.py:215
  391.8 19.4 %collective-permute-done.6.refs_1_ = f32[4,128,512]{2,1,0:T(8,128)} collective-permute-done((f32[4,128,512]{2,1,0:T(8,128)}, f32[4,128,512]{2,1,0:T(8,128)}, u32[]{:S(2)}, u32[]{:S(2)}) %collective-permute-start.6) | collective-permute-done | bytes 1048608 | tf_op jit(solution)/shard_map/ppermute | solution.py:266
  411.3 19.5 %shard_map.76.refs_6_ = f32[16,128,2048]{2,1,0:T(8,128)} custom-call(f32[4,128,512]{2,1,0:T(8,128)} %get-tuple-element.44.refs_0_, f32[4,128,512]{2,1,0:T(8,128)} %collective-permute-done.6.refs_1_, f32[4,128,512]{2,1,0:T(8,128)} %collective-permute-done.7.refs_2_, f32[4,128,512]{2,1,0:T(8,128)} %collective-permute-done.8.refs_3_, ...), custom_call_target="tpu_custom_call", output_to_operand_aliasing={{}: (8, {})} | custom-call | flops 12884901888 | bytes 25165824 | tf_op jit(solution)/shard_map/pallas_call | solution.py:215
  430.8 7.4 %shard_map.77.refs_6_ = f32[16,128,2048]{2,1,0:T(8,128)} custom-call(f32[3,128,512]{2,1,0:T(8,128)} %collective-permute-done.3.refs_0_, bf16[2048,2048]{1,0:T(8,128)(2,1)} %get-tuple-element.33.refs_3_.refs_4_.refs_1_, bf16[2048,2048]{1,0:T(8,128)(2,1)} %get-tuple-element.34.refs_4_.refs_5_.refs_2_, ...), custom_call_target="tpu_custom_call", output_to_operand_aliasing={{}: (6, {})} | custom-call | flops 2415919104 | bytes 10485760 | tf_op jit(solution)/shard_map/pallas_call | solution.py:215
  438.2 6.2 %shard_map.78 = f32[16,128,2048]{2,1,0:T(8,128)} custom-call(f32[2,128,512]{2,1,0:T(8,128)} %collective-permute-done.refs_0_, bf16[2048,2048]{1,0:T(8,128)(2,1)} %get-tuple-element.33.refs_3_.refs_4_.refs_1_, bf16[2048,2048]{1,0:T(8,128)(2,1)} %get-tuple-element.34.refs_4_.refs_5_.refs_2_, ...), custom_call_target="tpu_custom_call", output_to_operand_aliasing={{}: (6, {})} | custom-call | flops 1610612736 | bytes 8388608 | tf_op jit(solution)/shard_map/pallas_call | solution.py:215
  (24 shorter events, 0.6 us)
Async XLA Ops:
  23.3 7.7 %copy-start.1 = (s32[192]{0:T(256)S(1)}, s32[192]{0:T(256)}, u32[]{:S(2)}) copy-start(s32[192]{0:T(256)} %constant.143) | copy-start | bytes 2308
  23.3 37.7 %all-to-all-start = ((f32[32,2,16,512]{3,2,1,0:T(8,128)}), f32[32,2,16,512]{3,2,1,0:T(8,128)}, u32[]{:S(2)}, u32[]{:S(2)}) async-start(f32[32,2,16,512]{3,2,1,0:T(8,128)} %bitcast.16), calls=%async_computation | async-start | bytes 4194304 | tf_op jit(solution)/shard_map/all_to_all | solution.py:262
  61.0 44.7 %copy-start = (f32[96,2,8,512]{3,2,1,0:T(8,128)S(1)}, f32[96,2,8,512]{3,2,1,0:T(8,128)}, u32[]{:S(2)}) copy-start(f32[96,2,8,512]{3,2,1,0:T(8,128)} %get-tuple-element.38) | copy-start | bytes 9437188
  149.1 58.8 %all-to-all-start.3 = ((f32[32,4,16,512]{3,2,1,0:T(8,128)}), f32[32,4,16,512]{3,2,1,0:T(8,128)}, u32[]{:S(2)}, u32[]{:S(2)}) async-start(f32[32,4,16,512]{3,2,1,0:T(8,128)} %bitcast.14), calls=%async_computation.3 | async-start | bytes 8388608 | tf_op jit(solution)/shard_map/all_to_all | solution.py:262
  207.9 123.0 %all-to-all-start.2 = ((f32[32,4,16,512]{3,2,1,0:T(8,128)}), f32[32,4,16,512]{3,2,1,0:T(8,128)}, u32[]{:S(2)}, u32[]{:S(2)}) async-start(f32[32,4,16,512]{3,2,1,0:T(8,128)} %bitcast.13), calls=%async_computation.2 | async-start | bytes 8388608 | tf_op jit(solution)/shard_map/all_to_all | solution.py:262
  217.3 25.2 %collective-permute-start.1 = (f32[2,128,512]{2,1,0:T(8,128)}, f32[2,128,512]{2,1,0:T(8,128)}, u32[]{:S(2)}, u32[]{:S(2)}) collective-permute-start(f32[2,128,512]{2,1,0:T(8,128)} %get-tuple-element.36), channel_id=1, source_target_pairs={{0,1},{1,2},{2,3},{3,0},{4,5},{5,6},{6,7},{7,4},{8,9},{9,10},{10,1... | collective-permute-start | bytes 1572872 | tf_op jit(solution)/shard_map/ppermute | solution.py:266
  219.2 23.3 %collective-permute-start.2 = (f32[2,128,512]{2,1,0:T(8,128)}, f32[2,128,512]{2,1,0:T(8,128)}, u32[]{:S(2)}, u32[]{:S(2)}) collective-permute-start(f32[2,128,512]{2,1,0:T(8,128)} %get-tuple-element.37), channel_id=1, source_target_pairs={{0,3},{1,0},{2,1},{3,2},{4,7},{5,4},{6,5},{7,6},{8,11},{9,8},{10,9... | collective-permute-start | bytes 1572872 | tf_op jit(solution)/shard_map/ppermute | solution.py:266
  238.8 36.7 %collective-permute-start.12 = (f32[3,128,512]{2,1,0:T(8,128)}, f32[3,128,512]{2,1,0:T(8,128)}, u32[]{:S(2)}, u32[]{:S(2)}) collective-permute-start(f32[3,128,512]{2,1,0:T(8,128)} %get-tuple-element.54), channel_id=1, source_target_pairs={{0,1},{1,2},{2,3},{3,0},{4,5},{5,6},{6,7},{7,4},{8,9},{9,10},{10,1... | collective-permute-start | bytes 2359304 | tf_op jit(solution)/shard_map/ppermute | solution.py:266
  238.8 38.2 %collective-permute-start.13 = (f32[3,128,512]{2,1,0:T(8,128)}, f32[3,128,512]{2,1,0:T(8,128)}, u32[]{:S(2)}, u32[]{:S(2)}) collective-permute-start(f32[3,128,512]{2,1,0:T(8,128)} %get-tuple-element.55), channel_id=1, source_target_pairs={{0,3},{1,0},{2,1},{3,2},{4,7},{5,4},{6,5},{7,6},{8,11},{9,8},{10,9... | collective-permute-start | bytes 2359304 | tf_op jit(solution)/shard_map/ppermute | solution.py:266
  242.0 35.6 %collective-permute-start.14 = (f32[3,128,512]{2,1,0:T(8,128)}, f32[3,128,512]{2,1,0:T(8,128)}, u32[]{:S(2)}, u32[]{:S(2)}) collective-permute-start(f32[3,128,512]{2,1,0:T(8,128)} %get-tuple-element.56), channel_id=1, source_target_pairs={{0,2},{1,3},{2,0},{3,1},{4,6},{5,7},{6,4},{7,5},{8,10},{9,11},{10,... | collective-permute-start | bytes 2359304 | tf_op jit(solution)/shard_map/ppermute | solution.py:266
  260.8 53.9 %collective-permute-start.4 = (f32[3,128,512]{2,1,0:T(8,128)}, f32[3,128,512]{2,1,0:T(8,128)}, u32[]{:S(2)}, u32[]{:S(2)}) collective-permute-start(f32[3,128,512]{2,1,0:T(8,128)} %get-tuple-element.41), channel_id=1, source_target_pairs={{0,1},{1,2},{2,3},{3,0},{4,5},{5,6},{6,7},{7,4},{8,9},{9,10},{10,1... | collective-permute-start | bytes 2359304 | tf_op jit(solution)/shard_map/ppermute | solution.py:266
  261.8 52.9 %collective-permute-start.5 = (f32[3,128,512]{2,1,0:T(8,128)}, f32[3,128,512]{2,1,0:T(8,128)}, u32[]{:S(2)}, u32[]{:S(2)}) collective-permute-start(f32[3,128,512]{2,1,0:T(8,128)} %get-tuple-element.42), channel_id=1, source_target_pairs={{0,3},{1,0},{2,1},{3,2},{4,7},{5,4},{6,5},{7,6},{8,11},{9,8},{10,9... | collective-permute-start | bytes 2359304 | tf_op jit(solution)/shard_map/ppermute | solution.py:266
  275.4 91.4 %collective-permute-start.10 = (f32[4,128,512]{2,1,0:T(8,128)}, f32[4,128,512]{2,1,0:T(8,128)}, u32[]{:S(2)}, u32[]{:S(2)}) collective-permute-start(f32[4,128,512]{2,1,0:T(8,128)} %get-tuple-element.51), channel_id=1, source_target_pairs={{0,3},{1,0},{2,1},{3,2},{4,7},{5,4},{6,5},{7,6},{8,11},{9,8},{10,9... | collective-permute-start | bytes 3145736 | tf_op jit(solution)/shard_map/ppermute | solution.py:266
  277.0 89.8 %collective-permute-start.11 = (f32[4,128,512]{2,1,0:T(8,128)}, f32[4,128,512]{2,1,0:T(8,128)}, u32[]{:S(2)}, u32[]{:S(2)}) collective-permute-start(f32[4,128,512]{2,1,0:T(8,128)} %get-tuple-element.52), channel_id=1, source_target_pairs={{0,2},{1,3},{2,0},{3,1},{4,6},{5,7},{6,4},{7,5},{8,10},{9,11},{10,... | collective-permute-start | bytes 3145736 | tf_op jit(solution)/shard_map/ppermute | solution.py:266
  277.7 92.9 %collective-permute-start.9 = (f32[4,128,512]{2,1,0:T(8,128)}, f32[4,128,512]{2,1,0:T(8,128)}, u32[]{:S(2)}, u32[]{:S(2)}) collective-permute-start(f32[4,128,512]{2,1,0:T(8,128)} %get-tuple-element.50), channel_id=1, source_target_pairs={{0,1},{1,2},{2,3},{3,0},{4,5},{5,6},{6,7},{7,4},{8,9},{9,10},{10,1... | collective-permute-start | bytes 3145736 | tf_op jit(solution)/shard_map/ppermute | solution.py:266
  314.7 123.4 %collective-permute-start = (f32[2,128,512]{2,1,0:T(8,128)}, f32[2,128,512]{2,1,0:T(8,128)}, u32[]{:S(2)}, u32[]{:S(2)}) collective-permute-start(f32[2,128,512]{2,1,0:T(8,128)} %get-tuple-element.32), channel_id=1, source_target_pairs={{0,2},{1,3},{2,0},{3,1},{4,6},{5,7},{6,4},{7,5},{8,10},{9,11},{10,... | collective-permute-start | bytes 1572872 | tf_op jit(solution)/shard_map/ppermute | solution.py:266
  314.7 116.0 %collective-permute-start.3 = (f32[3,128,512]{2,1,0:T(8,128)}, f32[3,128,512]{2,1,0:T(8,128)}, u32[]{:S(2)}, u32[]{:S(2)}) collective-permute-start(f32[3,128,512]{2,1,0:T(8,128)} %get-tuple-element.39), channel_id=1, source_target_pairs={{0,2},{1,3},{2,0},{3,1},{4,6},{5,7},{6,4},{7,5},{8,10},{9,11},{10,... | collective-permute-start | bytes 2359304 | tf_op jit(solution)/shard_map/ppermute | solution.py:266
  366.9 44.4 %collective-permute-start.6 = (f32[4,128,512]{2,1,0:T(8,128)}, f32[4,128,512]{2,1,0:T(8,128)}, u32[]{:S(2)}, u32[]{:S(2)}) collective-permute-start(f32[4,128,512]{2,1,0:T(8,128)} %get-tuple-element.45), channel_id=1, source_target_pairs={{0,1},{1,2},{2,3},{3,0},{4,5},{5,6},{6,7},{7,4},{8,9},{9,10},{10,1... | collective-permute-start | bytes 3145736 | tf_op jit(solution)/shard_map/ppermute | solution.py:266
  366.9 44.4 %collective-permute-start.7 = (f32[4,128,512]{2,1,0:T(8,128)}, f32[4,128,512]{2,1,0:T(8,128)}, u32[]{:S(2)}, u32[]{:S(2)}) collective-permute-start(f32[4,128,512]{2,1,0:T(8,128)} %get-tuple-element.46), channel_id=1, source_target_pairs={{0,3},{1,0},{2,1},{3,2},{4,7},{5,4},{6,5},{7,6},{8,11},{9,8},{10,9... | collective-permute-start | bytes 3145736 | tf_op jit(solution)/shard_map/ppermute | solution.py:266
  370.6 40.7 %collective-permute-start.8 = (f32[4,128,512]{2,1,0:T(8,128)}, f32[4,128,512]{2,1,0:T(8,128)}, u32[]{:S(2)}, u32[]{:S(2)}) collective-permute-start(f32[4,128,512]{2,1,0:T(8,128)} %get-tuple-element.47), channel_id=1, source_target_pairs={{0,2},{1,3},{2,0},{3,1},{4,6},{5,7},{6,4},{7,5},{8,10},{9,11},{10,... | collective-permute-start | bytes 3145736 | tf_op jit(solution)/shard_map/ppermute | solution.py:266

commit v4 on v2

--- a/solution.py
+++ b/solution.py
@@ -8,8 +8,8 @@
 from jax.experimental.pallas import tpu as pltpu
 from jax.sharding import PartitionSpec as P
 
-SIZES = (3, 4, 4, 3, 2)
-STARTS = (0, 8, 12, 3, 6)
+SIZES = (5, 4, 3, 2, 2)
+STARTS = (0, 5, 9, 12, 14)
 Z_COLS = 512
 X_FORM = ((4, 2), (4, 2))
 Y_WIDTH = 512
@@ -41,6 +41,14 @@
 
 def stacked(table):
     return jnp.concatenate(split_table(table), axis=0)
+
+
+def fixed_table(rank, count):
+    turns = rank[:, None] * np.arange(count)[None, :] % count
+    table = np.cos(2.0 * np.pi / count * turns - np.pi / 4) * (2.0 / count) ** 0.5
+    high = table.astype(jnp.bfloat16)
+    low = (table - high.astype(np.float64)).astype(jnp.bfloat16)
+    return jnp.asarray(np.concatenate([high, low]))
 
 
 def small_table(rank, count):
@@ -179,8 +187,6 @@
     group = planes
     rows = group * share
     pairs = planes // group
-    first = start // group
-    assert start % group == 0
     cols = Z_COLS
     operands = [*values, *tables, sxy, symbol_z]
     in_specs = [
@@ -188,7 +194,7 @@
     ] * parts + [
         pl.BlockSpec((n, cols), lambda i, k: (0, i)),
         pl.BlockSpec((n, cols), lambda i, k: (0, i)),
-        pl.BlockSpec((rows, 128), lambda i, k: (first + k, 0)),
+        pl.BlockSpec((pl.Element(rows), pl.Element(128)), lambda i, k: (start * share, 0)),
         pl.BlockSpec((1, cols), lambda i, k: (0, i)),
     ]
     aliases = {}
@@ -200,7 +206,9 @@
         functools.partial(z_kernel, parts),
         grid=(n // cols, pairs),
         in_specs=in_specs,
-        out_specs=pl.BlockSpec((group, share, cols), lambda i, k: (first + k, 0, i)),
+        out_specs=pl.BlockSpec(
+            (pl.Element(group), pl.Element(share), pl.Element(cols)), lambda i, k: (start, 0, i * cols)
+        ),
         out_shape=jax.ShapeDtypeStruct((total, share, n), jnp.float32),
         scratch_shapes=[pltpu.VMEM((pairs, rows, n), jnp.bfloat16)] * 2,
         input_output_aliases=aliases,
@@ -230,11 +238,14 @@
     z_tables = wide_table(outer, jnp.arange(low_count), all_z)
 
     x_parts = []
-    for pick in (range(1), range(1, len(SIZES))):
+    for name, pick in (("x0", range(1)), ("x1", range(1, len(SIZES)))):
         mode = np.concatenate(
             [(np.arange(rows)[:, None] * planes + STARTS[j] + np.arange(SIZES[j])).reshape(-1) for j in pick]
         )
-        x_table = stacked(small_table(jnp.asarray(mode, jnp.int32), xs))
+        if name == "x0":
+            x_table = fixed_table(mode, xs)
+        else:
+            x_table = stacked(small_table(jnp.asarray(mode, jnp.int32), xs))
         x_parts += x_modes(velocity, x_table, [rows * SIZES[j] for j in pick])
 
     out = None

time: 454 us -> 440 us (0.969)
  waiting for transfers between devices: 106 us -> 57.4 us
  blocking collectives: 87.9 us -> 135 us
  starting transfers between devices: 83.1 us -> 73.6 us
    all_to_all x2 -> x3, blocking collectives: 87.9 us -> 135 us  [local(): part = lax.all_to_all(part, 'row', split_axis=0, concat_axis=0, tiled=True)]
    all_to_all x3 -> x2, waiting for transfers between devices: 67.9 us -> 29.7 us  [local(): part = lax.all_to_all(part, 'row', split_axis=0, concat_axis=0, tiled=True)]
    ppermute x15, waiting for transfers between devices: 37.7 us -> 27.7 us  [local(): lax.ppermute(part[d], 'col', [(i, (i + d) % cols) for i in range(cols)])]
    all_to_all x3 -> x2, starting transfers between devices: 17.4 us -> 9.71 us  [local(): part = lax.all_to_all(part, 'row', split_axis=0, concat_axis=0, tiled=True)]
    convert_element_type x3 -> x2, other arithmetic: 9.47 us -> 8.13 us  [split_table(): return (high.astype(jnp.bfloat16), low.astype(jnp.bfloat16))]
  transfers between devices with their start and end apart: 18 -> 17, of which waited for: 8 -> 7; matrix products, arithmetic and copies ran while one was open for 4% -> 3% of each run, Pallas kernels for 27% -> 28%
where the time goes in v4:
time: 440 us; the launch traced here: 439 us
  Pallas kernels  153 us (35%)
  blocking collectives  135 us (31%)
  starting transfers between devices  73.6 us (17%)
  waiting for transfers between devices  57.4 us (13%)
  other arithmetic  15.8 us (4%)
    all_to_all x3, blocking collectives, local(): part = lax.all_to_all(part, 'row', split_axis=0, concat_axis=0, tiled=True)  135 us
    pallas_call x5, Pallas kernels, z_modes(): pl.pallas_call(functools.partial(z_kernel, parts), grid=(n // cols, pairs...  84 us
    ppermute x15, starting transfers between devices, local(): lax.ppermute(part[d], 'col', [(i, (i + d) % cols) for i in range(cols)])  63.9 us
    pallas_call x5, Pallas kernels, y_modes(): pl.pallas_call(y_kernel, grid=(planes, zs // width), in_specs=[pl.BlockSp...  30.1 us
    pallas_call x2, Pallas kernels, x_modes(): pl.pallas_call(functools.partial(x_kernel, group, unroll), grid=(zs // 12...  30.1 us
    all_to_all x2, waiting for transfers between devices, local(): part = lax.all_to_all(part, 'row', split_axis=0, concat_axis=0, tiled=True)  29.7 us
    ppermute x15, waiting for transfers between devices, local(): lax.ppermute(part[d], 'col', [(i, (i + d) % cols) for i in range(cols)])  27.7 us
    all_to_all x2, starting transfers between devices, local(): part = lax.all_to_all(part, 'row', split_axis=0, concat_axis=0, tiled=True)  9.71 us
  transfers between devices with their start and end apart: 17, of which 7 were waited for; matrix products, arithmetic and copies ran while one was open for 3% of the time, Pallas kernels for 28%

profile of v4, /device:TPU:0, one launch (start us, length us, event | category | flops | bytes accessed | tf_op | source)
XLA Modules:
  0.0 439.1 jit_solution(6784653865625014637)
XLA Ops:
  0.0 3.7 reduce-precision_convert_fusion.1
  3.7 0.9 pad_maximum_fusion.1.a_ref
  4.6 16.9 %shard_map.64 = (f32[128,2,8,512]{3,2,1,0:T(8,128)}, f32[96,2,8,512]{3,2,1,0:T(8,128)}, f32[64,2,8,512]{3,2,1,0:T(8,128)}, f32[64,2,8,512]{3,2,1,0:T(8,128)}) custom-call(bf16[704,512]{1,0:T(8,128)(2,1)} %pad_maximum_fusion.1.a_ref, f32[512,2,8,512]{3,2,1,0:T(8,128)} %bitcast.11), custom_call_target="tpu_custom_call" | custom-call | flops 8858370048 | bytes 16777216 | tf_op jit(solution)/shard_map/pallas_call | solution.py:85
  21.5 36.1 %all_to_all.25.v_ref = f32[32,2,16,512]{3,2,1,0:T(8,128)} all-to-all(f32[32,2,16,512]{3,2,1,0:T(8,128)} %bitcast.15), channel_id=1, replica_groups=mesh['row'=32,'col'=4] {'row'}, dimensions={0} | all-to-all | bytes 4194304 | tf_op jit(solution)/shard_map/all_to_all | solution.py:254
  57.6 32.1 %all_to_all.26.v_ref = f32[32,2,16,512]{3,2,1,0:T(8,128)} all-to-all(f32[32,2,16,512]{3,2,1,0:T(8,128)S(1)} %bitcast.14), channel_id=1, replica_groups=mesh['row'=32,'col'=4] {'row'}, dimensions={0} | all-to-all | bytes 4194304 | tf_op jit(solution)/shard_map/all_to_all | solution.py:254
  89.7 4.8 %all-to-all-start.2 = ((f32[32,3,16,512]{3,2,1,0:T(8,128)}), f32[32,3,16,512]{3,2,1,0:T(8,128)}, u32[]{:S(2)}, u32[]{:S(2)}) async-start(f32[32,3,16,512]{3,2,1,0:T(8,128)} %bitcast.6), calls=%async_computation.2 | async-start | bytes 6291456 | tf_op jit(solution)/shard_map/all_to_all | solution.py:254
  94.6 13.2 %shard_map.70 = f32[160,2,8,512]{3,2,1,0:T(8,128)} custom-call(bf16[320,512]{1,0:T(8,128)(2,1)} %constant.122.clone.a_ref, f32[512,2,8,512]{3,2,1,0:T(8,128)} %bitcast.12), custom_call_target="tpu_custom_call" | custom-call | flops 4026531840 | bytes 16777216 | tf_op jit(solution)/shard_map/pallas_call | solution.py:85
  107.8 28.8 %all-to-all-done.2.v_ref = f32[32,3,16,512]{3,2,1,0:T(8,128)} async-done(((f32[32,3,16,512]{3,2,1,0:T(8,128)}), f32[32,3,16,512]{3,2,1,0:T(8,128)}, u32[]{:S(2)}, u32[]{:S(2)}) %all-to-all-start.2) | async-done | bytes 3145760 | tf_op jit(solution)/shard_map/all_to_all | solution.py:254
  136.6 67.0 %all_to_all.27.v_ref = f32[32,5,16,512]{3,2,1,0:T(8,128)} all-to-all(f32[32,5,16,512]{3,2,1,0:T(8,128)} %bitcast.10), channel_id=1, replica_groups=mesh['row'=32,'col'=4] {'row'}, dimensions={0} | all-to-all | bytes 10485760 | tf_op jit(solution)/shard_map/all_to_all | solution.py:254
  203.6 4.9 %all-to-all-start.3 = ((f32[32,4,16,512]{3,2,1,0:T(8,128)}), f32[32,4,16,512]{3,2,1,0:T(8,128)}, u32[]{:S(2)}, u32[]{:S(2)}) async-start(f32[32,4,16,512]{3,2,1,0:T(8,128)} %bitcast.13), calls=%async_computation.3 | async-start | bytes 8388608 | tf_op jit(solution)/shard_map/all_to_all | solution.py:254
  208.5 4.4 %reduce-precision_convert_fusion = (bf16[512,512]{1,0:T(8,128)(2,1)S(1)}, bf16[512,512]{1,0:T(8,128)(2,1)S(1)}) fusion(s32[512]{0:T(512)S(1)} %add_select_fusion.4), kind=kLoop, calls=%fused_computation.4 | loop fusion | flops 5242880 | bytes 1050624 | tf_op jit(solution)/shard_map/convert_element_type | solution.py:39
  212.9 1.1 pad_maximum_fusion.a_ref
  214.0 3.1 fusion.31
  217.1 1.9 sine_multiply_fusion
  219.0 8.4 %shard_map.71 = (f32[5,128,512]{2,1,0:T(8,128)}, f32[5,128,512]{2,1,0:T(8,128)}, f32[5,128,512]{2,1,0:T(8,128)}, f32[5,128,512]{2,1,0:T(8,128)}) custom-call(bf16[1024,512]{1,0:T(8,128)(2,1)} %pad_maximum_fusion.a_ref, f32[32,5,16,512]{3,2,1,0:T(8,128)} %all_to_all.27.v_ref), custom_call_target="tpu_custom_call" | custom-call | flops 4026531840 | bytes 10485760 | tf_op jit(solution)/shard_map/pallas_call | solution.py:112
  227.4 1.9 collective-permute-start.12
  229.3 3.6 collective-permute-start.13
  232.9 1.0 collective-permute-start.14
  233.9 9.2 %shard_map.66 = (bf16[2048,2048]{1,0:T(8,128)(2,1)}, bf16[2048,2048]{1,0:T(8,128)(2,1)}) custom-call(f32[32,2048]{1,0:T(8,128)} %get-tuple-element.62.cos_ref, f32[32,2048]{1,0:T(8,128)} %get-tuple-element.61.sin_ref, f32[64,2048]{1,0:T(8,128)} %get-tuple-element.64.plus_ref, f32[64,2048]{1,0:T(8,128)} %get-tuple-element.63.minus_ref), custom_call_target="tpu_custom_call" | custom-call | flops 10000000000 | bytes 16777216 | tf_op jit(solution)/shard_map/pallas_call | solution.py:148
  243.1 0.8 dynamic_slice.7
  243.8 0.8 dynamic_slice.6
  244.6 0.7 bitcast_add_fusion
  245.3 4.4 %shard_map.65 = (f32[2,128,512]{2,1,0:T(8,128)}, f32[2,128,512]{2,1,0:T(8,128)}, f32[2,128,512]{2,1,0:T(8,128)}, f32[2,128,512]{2,1,0:T(8,128)}) custom-call(bf16[1024,512]{1,0:T(8,128)(2,1)} %pad_maximum_fusion.a_ref, f32[32,2,16,512]{3,2,1,0:T(8,128)} %all_to_all.26.v_ref), custom_call_target="tpu_custom_call" | custom-call | flops 1610612736 | bytes 4194304 | tf_op jit(solution)/shard_map/pallas_call | solution.py:112
  249.7 1.0 collective-permute-start
  250.7 0.4 collective-permute-start.1
  251.2 4.4 %shard_map.67 = (f32[2,128,512]{2,1,0:T(8,128)}, f32[2,128,512]{2,1,0:T(8,128)}, f32[2,128,512]{2,1,0:T(8,128)}, f32[2,128,512]{2,1,0:T(8,128)}) custom-call(bf16[1024,512]{1,0:T(8,128)(2,1)} %pad_maximum_fusion.a_ref, f32[32,2,16,512]{3,2,1,0:T(8,128)} %all_to_all.25.v_ref), custom_call_target="tpu_custom_call" | custom-call | flops 1610612736 | bytes 4194304 | tf_op jit(solution)/shard_map/pallas_call | solution.py:112
  255.6 6.0 %shard_map.68 = (f32[3,128,512]{2,1,0:T(8,128)}, f32[3,128,512]{2,1,0:T(8,128)}, f32[3,128,512]{2,1,0:T(8,128)}, f32[3,128,512]{2,1,0:T(8,128)}) custom-call(bf16[1024,512]{1,0:T(8,128)(2,1)} %pad_maximum_fusion.a_ref, f32[32,3,16,512]{3,2,1,0:T(8,128)} %all-to-all-done.2.v_ref), custom_call_target="tpu_custom_call" | custom-call | flops 2415919104 | bytes 6291456 | tf_op jit(solution)/shard_map/pallas_call | solution.py:112
  261.5 0.9 all-to-all-done.3.v_ref
  262.4 7.0 %shard_map.69 = (f32[4,128,512]{2,1,0:T(8,128)}, f32[4,128,512]{2,1,0:T(8,128)}, f32[4,128,512]{2,1,0:T(8,128)}, f32[4,128,512]{2,1,0:T(8,128)}) custom-call(bf16[1024,512]{1,0:T(8,128)(2,1)} %pad_maximum_fusion.a_ref, f32[32,4,16,512]{3,2,1,0:T(8,128)} %all-to-all-done.3.v_ref), custom_call_target="tpu_custom_call" | custom-call | flops 3221225472 | bytes 8388608 | tf_op jit(solution)/shard_map/pallas_call | solution.py:112
  269.4 19.2 %collective-permute-start.9 = (f32[4,128,512]{2,1,0:T(8,128)}, f32[4,128,512]{2,1,0:T(8,128)}, u32[]{:S(2)}, u32[]{:S(2)}) collective-permute-start(f32[4,128,512]{2,1,0:T(8,128)} %get-tuple-element.50), channel_id=1, source_target_pairs={{0,1},{1,2},{2,3},{3,0},{4,5},{5,6},{6,7},{7,4},{8,9},{9,10},{10,1... | collective-permute-start | bytes 3145736 | tf_op jit(solution)/shard_map/ppermute | solution.py:257
  288.6 2.3 collective-permute-done.13.refs_2_
  291.0 0.4 collective-permute-start.10
  291.3 2.6 collective-permute-start.11
  293.9 2.0 broadcast_in_dim.2.refs_6_
  296.0 23.5 %shard_map.72.refs_8_ = f32[16,128,2048]{2,1,0:T(8,128)} custom-call(f32[5,128,512]{2,1,0:T(8,128)} %get-tuple-element.53.refs_0_, f32[5,128,512]{2,1,0:T(8,128)} %collective-permute-done.12.refs_1_, f32[5,128,512]{2,1,0:T(8,128)} %collective-permute-done.13.refs_2_, f32[5,128,512]{2,1,0:T(8,128)} %collective-permute-done.14.refs_3_, ...), custom_call_target="tpu_custom_call" | custom-call | flops 16106127360 | bytes 27262976 | tf_op jit(solution)/shard_map/pallas_call | solution.py:205
  319.4 14.4 %collective-permute-done.9.refs_1_ = f32[4,128,512]{2,1,0:T(8,128)} collective-permute-done((f32[4,128,512]{2,1,0:T(8,128)}, f32[4,128,512]{2,1,0:T(8,128)}, u32[]{:S(2)}, u32[]{:S(2)}) %collective-permute-start.9) | collective-permute-done | bytes 1048608 | tf_op jit(solution)/shard_map/ppermute | solution.py:257
  333.8 21.0 %collective-permute-start.6 = (f32[3,128,512]{2,1,0:T(8,128)}, f32[3,128,512]{2,1,0:T(8,128)}, u32[]{:S(2)}, u32[]{:S(2)}) collective-permute-start(f32[3,128,512]{2,1,0:T(8,128)} %get-tuple-element.45), channel_id=1, source_target_pairs={{0,1},{1,2},{2,3},{3,0},{4,5},{5,6},{6,7},{7,4},{8,9},{9,10},{10,1... | collective-permute-start | bytes 2359304 | tf_op jit(solution)/shard_map/ppermute | solution.py:257
  354.8 3.7 collective-permute-done.10.refs_2_
  358.5 2.0 collective-permute-start.8
  360.4 19.6 %shard_map.73.refs_8_ = f32[16,128,2048]{2,1,0:T(8,128)} custom-call(f32[4,128,512]{2,1,0:T(8,128)} %get-tuple-element.49.refs_0_, f32[4,128,512]{2,1,0:T(8,128)} %collective-permute-done.9.refs_1_, f32[4,128,512]{2,1,0:T(8,128)} %collective-permute-done.10.refs_2_, f32[4,128,512]{2,1,0:T(8,128)} %collective-permute-done.11.refs_3_, ...), custom_call_target="tpu_custom_call", output_to_operand_aliasing={{}: (8, {})} | custom-call | flops 12884901888 | bytes 25165824 | tf_op jit(solution)/shard_map/pallas_call | solution.py:205
  380.0 6.6 %collective-permute-start.3 = (f32[2,128,512]{2,1,0:T(8,128)}, f32[2,128,512]{2,1,0:T(8,128)}, u32[]{:S(2)}, u32[]{:S(2)}) collective-permute-start(f32[2,128,512]{2,1,0:T(8,128)} %get-tuple-element.40), channel_id=1, source_target_pairs={{0,1},{1,2},{2,3},{3,0},{4,5},{5,6},{6,7},{7,4},{8,9},{9,10},{10,1... | collective-permute-start | bytes 1572872 | tf_op jit(solution)/shard_map/ppermute | solution.py:257
  386.6 6.8 %collective-permute-done.7.refs_2_ = f32[3,128,512]{2,1,0:T(8,128)} collective-permute-done((f32[3,128,512]{2,1,0:T(8,128)}, f32[3,128,512]{2,1,0:T(8,128)}, u32[]{:S(2)}, u32[]{:S(2)}) %collective-permute-start.7) | collective-permute-done | bytes 786464 | tf_op jit(solution)/shard_map/ppermute | solution.py:257
  393.4 0.5 collective-permute-start.4
  393.9 15.7 %shard_map.74.refs_8_ = f32[16,128,2048]{2,1,0:T(8,128)} custom-call(f32[3,128,512]{2,1,0:T(8,128)} %get-tuple-element.44.refs_0_, f32[3,128,512]{2,1,0:T(8,128)} %collective-permute-done.6.refs_1_, f32[3,128,512]{2,1,0:T(8,128)} %collective-permute-done.7.refs_2_, f32[3,128,512]{2,1,0:T(8,128)} %collective-permute-done.8.refs_3_, ...), custom_call_target="tpu_custom_call", output_to_operand_aliasing={{}: (8, {})} | custom-call | flops 9663676416 | bytes 23068672 | tf_op jit(solution)/shard_map/pallas_call | solution.py:205
  409.6 3.6 collective-permute-start.2
  413.3 0.5 collective-permute-done.4.refs_2_
  413.8 12.6 %shard_map.75.refs_8_ = f32[16,128,2048]{2,1,0:T(8,128)} custom-call(f32[2,128,512]{2,1,0:T(8,128)} %get-tuple-element.39.refs_0_, f32[2,128,512]{2,1,0:T(8,128)} %collective-permute-done.3.refs_1_, f32[2,128,512]{2,1,0:T(8,128)} %collective-permute-done.4.refs_2_, f32[2,128,512]{2,1,0:T(8,128)} %collective-permute-done.5.refs_3_, ...), custom_call_target="tpu_custom_call", output_to_operand_aliasing={{}: (8, {})} | custom-call | flops 6442450944 | bytes 20971520 | tf_op jit(solution)/shard_map/pallas_call | solution.py:205
  426.5 12.7 %shard_map.76 = f32[16,128,2048]{2,1,0:T(8,128)} custom-call(f32[2,128,512]{2,1,0:T(8,128)} %get-tuple-element.32.refs_0_, f32[2,128,512]{2,1,0:T(8,128)} %collective-permute-done.refs_1_, f32[2,128,512]{2,1,0:T(8,128)} %collective-permute-done.1.refs_2_, f32[2,128,512]{2,1,0:T(8,128)} %collective-permute-done.2.refs_3_, ...), custom_call_target="tpu_custom_call", output_to_operand_aliasing={{}: (8, {})} | custom-call | flops 6442450944 | bytes 20971520 | tf_op jit(solution)/shard_map/pallas_call | solution.py:205
  (17 shorter events, 0.1 us)
Async XLA Ops:
  21.5 36.1 %copy-start = (f32[64,2,8,512]{3,2,1,0:T(8,128)S(1)}, f32[64,2,8,512]{3,2,1,0:T(8,128)}, u32[]{:S(2)}) copy-start(f32[64,2,8,512]{3,2,1,0:T(8,128)} %get-tuple-element.31) | copy-start | bytes 6291460
  89.7 46.8 %all-to-all-start.2 = ((f32[32,3,16,512]{3,2,1,0:T(8,128)}), f32[32,3,16,512]{3,2,1,0:T(8,128)}, u32[]{:S(2)}, u32[]{:S(2)}) async-start(f32[32,3,16,512]{3,2,1,0:T(8,128)} %bitcast.6), calls=%async_computation.2 | async-start | bytes 6291456 | tf_op jit(solution)/shard_map/all_to_all | solution.py:254
  203.6 58.8 %all-to-all-start.3 = ((f32[32,4,16,512]{3,2,1,0:T(8,128)}), f32[32,4,16,512]{3,2,1,0:T(8,128)}, u32[]{:S(2)}, u32[]{:S(2)}) async-start(f32[32,4,16,512]{3,2,1,0:T(8,128)} %bitcast.13), calls=%async_computation.3 | async-start | bytes 8388608 | tf_op jit(solution)/shard_map/all_to_all | solution.py:254
  227.4 42.0 %collective-permute-start.12 = (f32[5,128,512]{2,1,0:T(8,128)}, f32[5,128,512]{2,1,0:T(8,128)}, u32[]{:S(2)}, u32[]{:S(2)}) collective-permute-start(f32[5,128,512]{2,1,0:T(8,128)} %get-tuple-element.54), channel_id=1, source_target_pairs={{0,1},{1,2},{2,3},{3,0},{4,5},{5,6},{6,7},{7,4},{8,9},{9,10},{10,1... | collective-permute-start | bytes 3932168 | tf_op jit(solution)/shard_map/ppermute | solution.py:257
  229.3 61.7 %collective-permute-start.13 = (f32[5,128,512]{2,1,0:T(8,128)}, f32[5,128,512]{2,1,0:T(8,128)}, u32[]{:S(2)}, u32[]{:S(2)}) collective-permute-start(f32[5,128,512]{2,1,0:T(8,128)} %get-tuple-element.55), channel_id=1, source_target_pairs={{0,2},{1,3},{2,0},{3,1},{4,6},{5,7},{6,4},{7,5},{8,10},{9,11},{10,... | collective-permute-start | bytes 3932168 | tf_op jit(solution)/shard_map/ppermute | solution.py:257
  232.9 58.4 %collective-permute-start.14 = (f32[5,128,512]{2,1,0:T(8,128)}, f32[5,128,512]{2,1,0:T(8,128)}, u32[]{:S(2)}, u32[]{:S(2)}) collective-permute-start(f32[5,128,512]{2,1,0:T(8,128)} %get-tuple-element.56), channel_id=1, source_target_pairs={{0,3},{1,0},{2,1},{3,2},{4,7},{5,4},{6,5},{7,6},{8,11},{9,8},{10,9... | collective-permute-start | bytes 3932168 | tf_op jit(solution)/shard_map/ppermute | solution.py:257
  249.7 176.7 %collective-permute-start = (f32[2,128,512]{2,1,0:T(8,128)}, f32[2,128,512]{2,1,0:T(8,128)}, u32[]{:S(2)}, u32[]{:S(2)}) collective-permute-start(f32[2,128,512]{2,1,0:T(8,128)} %get-tuple-element.33), channel_id=1, source_target_pairs={{0,1},{1,2},{2,3},{3,0},{4,5},{5,6},{6,7},{7,4},{8,9},{9,10},{10,1... | collective-permute-start | bytes 1572872 | tf_op jit(solution)/shard_map/ppermute | solution.py:257
  250.7 175.7 %collective-permute-start.1 = (f32[2,128,512]{2,1,0:T(8,128)}, f32[2,128,512]{2,1,0:T(8,128)}, u32[]{:S(2)}, u32[]{:S(2)}) collective-permute-start(f32[2,128,512]{2,1,0:T(8,128)} %get-tuple-element.34), channel_id=1, source_target_pairs={{0,2},{1,3},{2,0},{3,1},{4,6},{5,7},{6,4},{7,5},{8,10},{9,11},{10,... | collective-permute-start | bytes 1572872 | tf_op jit(solution)/shard_map/ppermute | solution.py:257
  269.4 64.4 %collective-permute-start.9 = (f32[4,128,512]{2,1,0:T(8,128)}, f32[4,128,512]{2,1,0:T(8,128)}, u32[]{:S(2)}, u32[]{:S(2)}) collective-permute-start(f32[4,128,512]{2,1,0:T(8,128)} %get-tuple-element.50), channel_id=1, source_target_pairs={{0,1},{1,2},{2,3},{3,0},{4,5},{5,6},{6,7},{7,4},{8,9},{9,10},{10,1... | collective-permute-start | bytes 3145736 | tf_op jit(solution)/shard_map/ppermute | solution.py:257
  291.0 67.5 %collective-permute-start.10 = (f32[4,128,512]{2,1,0:T(8,128)}, f32[4,128,512]{2,1,0:T(8,128)}, u32[]{:S(2)}, u32[]{:S(2)}) collective-permute-start(f32[4,128,512]{2,1,0:T(8,128)} %get-tuple-element.51), channel_id=1, source_target_pairs={{0,2},{1,3},{2,0},{3,1},{4,6},{5,7},{6,4},{7,5},{8,10},{9,11},{10,... | collective-permute-start | bytes 3145736 | tf_op jit(solution)/shard_map/ppermute | solution.py:257
  291.3 67.1 %collective-permute-start.11 = (f32[4,128,512]{2,1,0:T(8,128)}, f32[4,128,512]{2,1,0:T(8,128)}, u32[]{:S(2)}, u32[]{:S(2)}) collective-permute-start(f32[4,128,512]{2,1,0:T(8,128)} %get-tuple-element.52), channel_id=1, source_target_pairs={{0,3},{1,0},{2,1},{3,2},{4,7},{5,4},{6,5},{7,6},{8,11},{9,8},{10,9... | collective-permute-start | bytes 3145736 | tf_op jit(solution)/shard_map/ppermute | solution.py:257
  333.8 46.2 %collective-permute-start.6 = (f32[3,128,512]{2,1,0:T(8,128)}, f32[3,128,512]{2,1,0:T(8,128)}, u32[]{:S(2)}, u32[]{:S(2)}) collective-permute-start(f32[3,128,512]{2,1,0:T(8,128)} %get-tuple-element.45), channel_id=1, source_target_pairs={{0,1},{1,2},{2,3},{3,0},{4,5},{5,6},{6,7},{7,4},{8,9},{9,10},{10,1... | collective-permute-start | bytes 2359304 | tf_op jit(solution)/shard_map/ppermute | solution.py:257
  358.5 35.0 %collective-permute-start.7 = (f32[3,128,512]{2,1,0:T(8,128)}, f32[3,128,512]{2,1,0:T(8,128)}, u32[]{:S(2)}, u32[]{:S(2)}) collective-permute-start(f32[3,128,512]{2,1,0:T(8,128)} %get-tuple-element.46), channel_id=1, source_target_pairs={{0,2},{1,3},{2,0},{3,1},{4,6},{5,7},{6,4},{7,5},{8,10},{9,11},{10,... | collective-permute-start | bytes 2359304 | tf_op jit(solution)/shard_map/ppermute | solution.py:257
  358.5 35.5 %collective-permute-start.8 = (f32[3,128,512]{2,1,0:T(8,128)}, f32[3,128,512]{2,1,0:T(8,128)}, u32[]{:S(2)}, u32[]{:S(2)}) collective-permute-start(f32[3,128,512]{2,1,0:T(8,128)} %get-tuple-element.47), channel_id=1, source_target_pairs={{0,3},{1,0},{2,1},{3,2},{4,7},{5,4},{6,5},{7,6},{8,11},{9,8},{10,9... | collective-permute-start | bytes 2359304 | tf_op jit(solution)/shard_map/ppermute | solution.py:257
  380.0 29.6 %collective-permute-start.3 = (f32[2,128,512]{2,1,0:T(8,128)}, f32[2,128,512]{2,1,0:T(8,128)}, u32[]{:S(2)}, u32[]{:S(2)}) collective-permute-start(f32[2,128,512]{2,1,0:T(8,128)} %get-tuple-element.40), channel_id=1, source_target_pairs={{0,1},{1,2},{2,3},{3,0},{4,5},{5,6},{6,7},{7,4},{8,9},{9,10},{10,1... | collective-permute-start | bytes 1572872 | tf_op jit(solution)/shard_map/ppermute | solution.py:257
  393.4 20.4 %collective-permute-start.4 = (f32[2,128,512]{2,1,0:T(8,128)}, f32[2,128,512]{2,1,0:T(8,128)}, u32[]{:S(2)}, u32[]{:S(2)}) collective-permute-start(f32[2,128,512]{2,1,0:T(8,128)} %get-tuple-element.41), channel_id=1, source_target_pairs={{0,2},{1,3},{2,0},{3,1},{4,6},{5,7},{6,4},{7,5},{8,10},{9,11},{10,... | collective-permute-start | bytes 1572872 | tf_op jit(solution)/shard_map/ppermute | solution.py:257
  393.9 19.9 %collective-permute-start.5 = (f32[2,128,512]{2,1,0:T(8,128)}, f32[2,128,512]{2,1,0:T(8,128)}, u32[]{:S(2)}, u32[]{:S(2)}) collective-permute-start(f32[2,128,512]{2,1,0:T(8,128)} %get-tuple-element.42), channel_id=1, source_target_pairs={{0,3},{1,0},{2,1},{3,2},{4,7},{5,4},{6,5},{7,6},{8,11},{9,8},{10,9... | collective-permute-start | bytes 1572872 | tf_op jit(solution)/shard_map/ppermute | solution.py:257
  409.6 16.8 %collective-permute-start.2 = (f32[2,128,512]{2,1,0:T(8,128)}, f32[2,128,512]{2,1,0:T(8,128)}, u32[]{:S(2)}, u32[]{:S(2)}) collective-permute-start(f32[2,128,512]{2,1,0:T(8,128)} %get-tuple-element.35), channel_id=1, source_target_pairs={{0,3},{1,0},{2,1},{3,2},{4,7},{5,4},{6,5},{7,6},{8,11},{9,8},{10,9... | collective-permute-start | bytes 1572872 | tf_op jit(solution)/shard_map/ppermute | solution.py:257

commit v5 on v4

--- a/solution.py
+++ b/solution.py
@@ -135,48 +135,58 @@
         low_ref[k * inner : (k + 1) * inner] = low
 
 
-def wide_table(outer, inner, count):
-    rank = jnp.arange(count)
+def wide_table(outer, inner, rank, count):
+    width = len(rank)
     unit = 2.0 * jnp.pi / count
     a = unit * (outer[:, None] * rank[None, :] % count).astype(jnp.float32)
     b = unit * (inner[:, None] * rank[None, :] % count).astype(jnp.float32)
     scale = count ** (-0.5)
     cos_b, sin_b = jnp.cos(b), jnp.sin(b)
-    lines = pl.BlockSpec((len(outer), count), lambda i: (0, 0))
-    whole = pl.BlockSpec((len(inner), count), lambda i: (0, 0))
-    block = pl.BlockSpec((4 * len(inner), count), lambda i: (i, 0))
+    lines = pl.BlockSpec((len(outer), width), lambda i: (0, 0))
+    whole = pl.BlockSpec((len(inner), width), lambda i: (0, 0))
+    block = pl.BlockSpec((4 * len(inner), width), lambda i: (i, 0))
+    shape = jax.ShapeDtypeStruct((len(outer) * len(inner), width), jnp.bfloat16)
     return pl.pallas_call(
         table_kernel,
         grid=(len(outer) // 4,),
         in_specs=[lines, lines, whole, whole],
         out_specs=[block, block],
-        out_shape=[jax.ShapeDtypeStruct((count, count), jnp.bfloat16)] * 2,
-        compiler_params=pltpu.CompilerParams(vmem_limit_bytes=VMEM),
-        cost_estimate=pl.CostEstimate(flops=10**10, bytes_accessed=4 * count * count, transcendentals=0),
+        out_shape=[shape, shape],
+        compiler_params=pltpu.CompilerParams(vmem_limit_bytes=VMEM),
+        cost_estimate=pl.CostEstimate(flops=10**10, bytes_accessed=2 * count * count, transcendentals=0),
     )(jnp.cos(a) * scale, jnp.sin(a) * scale, cos_b + sin_b, cos_b - sin_b)
 
 
 def z_kernel(parts, *refs):
-    v_refs, (h_ref, l_ref, sxy_ref, sz_ref) = refs[:parts], refs[parts : parts + 4]
+    v_refs = refs[:parts]
+    he_ref, ho_ref, le_ref, lo_ref, sxy_ref, sz_ref = refs[parts : parts + 6]
     o_ref, high_s, low_s = refs[-3:]
     planes, share, zs = v_refs[0].shape
     rows = planes * share
-    pair = pl.program_id(1)
 
     @pl.when(pl.program_id(0) == 0)
     def _():
-        for p, v_ref in enumerate(v_refs):
-            high, low = halves(v_ref[...].reshape(rows, zs))
-            high_s[pair, :, p * zs : (p + 1) * zs] = high
-            low_s[pair, :, p * zs : (p + 1) * zs] = low
-
-    high = high_s[pair]
-    hr = h_ref[...]
-    out = mm(high, hr) + mm(low_s[pair], hr) + mm(high, l_ref[...])
+        for p in range(parts // 2):
+            near, far = v_refs[p][...].reshape(rows, zs), v_refs[p + parts // 2][...].reshape(rows, zs)
+            for k, mixed in enumerate((near + far, near - far)):
+                high, low = halves(mixed)
+                high_s[k, :, p * zs : (p + 1) * zs] = high
+                low_s[k, :, p * zs : (p + 1) * zs] = low
+
+    both = []
+    for k, (h_ref, l_ref) in enumerate(((he_ref, le_ref), (ho_ref, lo_ref))):
+        high, hr = high_s[k], h_ref[...]
+        both.append(mm(high, hr) + mm(low_s[k], hr) + mm(high, l_ref[...]))
+    even, odd = both
     sxy = sxy_ref[...]
-    for c in range(0, out.shape[1], 128):
+    lane = lax.broadcasted_iota(jnp.int32, (rows, 128), 1)
+    for c in range(0, o_ref.shape[2], 128):
+        g = c // 256 * 128
+        pick = lane // 2 + c // 128 % 2 * 64
+        here = [jnp.take_along_axis(t[:, g : g + 128], pick, axis=1, mode="promise_in_bounds") for t in (even, odd)]
+        out = jnp.where(lane % 2 == 0, *here)
         step = 0.2 * (sxy + sz_ref[:, c : c + 128])
-        done = out[:, c : c + 128] * ((1.0 - step) / (1.0 + step))
+        done = out * ((1.0 - step) / (1.0 + step))
         o_ref[:, :, c : c + 128] = done.reshape(planes, share, 128)
 
 
@@ -184,18 +194,18 @@
     parts = len(values)
     planes, share, zs = values[0].shape
     n = parts * zs
-    group = planes
-    rows = group * share
-    pairs = planes // group
+    rows = planes * share
     cols = Z_COLS
-    operands = [*values, *tables, sxy, symbol_z]
-    in_specs = [
-        pl.BlockSpec((group, share, zs), lambda i, k: (jnp.where(i == 0, k, pairs - 1), 0, 0))
-    ] * parts + [
-        pl.BlockSpec((n, cols), lambda i, k: (0, i)),
-        pl.BlockSpec((n, cols), lambda i, k: (0, i)),
-        pl.BlockSpec((pl.Element(rows), pl.Element(128)), lambda i, k: (start * share, 0)),
-        pl.BlockSpec((1, cols), lambda i, k: (0, i)),
+    steps = n // cols
+    high, low = tables
+    table_specs = [
+        pl.BlockSpec((n // 2, cols // 2), lambda i: (0, i)),
+        pl.BlockSpec((n // 2, cols // 2), lambda i: (0, steps + i)),
+    ]
+    operands = [*values, high, high, low, low, sxy, symbol_z]
+    in_specs = [pl.BlockSpec((planes, share, zs), lambda i: (0, 0, 0))] * parts + table_specs * 2 + [
+        pl.BlockSpec((pl.Element(rows), pl.Element(128)), lambda i: (start * share, 0)),
+        pl.BlockSpec((1, cols), lambda i: (0, i)),
     ]
     aliases = {}
     if previous is not None:
@@ -204,16 +214,16 @@
         in_specs.append(pl.BlockSpec(memory_space=pl.ANY))
     return pl.pallas_call(
         functools.partial(z_kernel, parts),
-        grid=(n // cols, pairs),
+        grid=(steps,),
         in_specs=in_specs,
         out_specs=pl.BlockSpec(
-            (pl.Element(group), pl.Element(share), pl.Element(cols)), lambda i, k: (start, 0, i * cols)
+            (pl.Element(planes), pl.Element(share), pl.Element(cols)), lambda i: (start, 0, i * cols)
         ),
         out_shape=jax.ShapeDtypeStruct((total, share, n), jnp.float32),
-        scratch_shapes=[pltpu.VMEM((pairs, rows, n), jnp.bfloat16)] * 2,
+        scratch_shapes=[pltpu.VMEM((2, rows, n // 2), jnp.bfloat16)] * 2,
         input_output_aliases=aliases,
         compiler_params=pltpu.CompilerParams(vmem_limit_bytes=VMEM),
-        cost_estimate=pl.CostEstimate(flops=6 * planes * share * n * n, bytes_accessed=4 * n * n + 8 * planes * share * n, transcendentals=0),
+        cost_estimate=pl.CostEstimate(flops=3 * rows * n * n, bytes_accessed=2 * n * n + 8 * rows * n, transcendentals=0),
     )(*operands)
 
 
@@ -233,9 +243,11 @@
     y_rank = (jnp.arange(all_y) + me * share_y) % all_y
     y_table = stacked(small_table(y_rank, all_y))
     low_count = 64
-    outer = jnp.arange(all_z // low_count) * low_count
+    outer = jnp.arange(all_z // 2 // low_count) * low_count
     outer = (me + cols - outer // zs) % cols * zs + outer % zs
-    z_tables = wide_table(outer, jnp.arange(low_count), all_z)
+    lane = jnp.arange(all_z)
+    half = all_z // 2
+    z_tables = wide_table(outer, jnp.arange(low_count), lane % half * 2 + lane // half, all_z)
 
     x_parts = []
     for name, pick in (("x0", range(1)), ("x1", range(1, len(SIZES)))):

time: 440 us -> 447 us (1.016)
  waiting for transfers between devices: 57.4 us -> 140 us
  blocking collectives: 135 us -> 68.2 us
  Pallas kernels: 153 us -> 130 us
  starting transfers between devices: 73.6 us -> 89.8 us
    all_to_all x2 -> x3, waiting for transfers between devices: 29.7 us -> 101 us  [local(): part = lax.all_to_all(part, 'row', split_axis=0, concat_axis=0, tiled=True)]
    all_to_all x3 -> x2, blocking collectives: 135 us -> 68.2 us  [local(): part = lax.all_to_all(part, 'row', split_axis=0, concat_axis=0, tiled=True)]
    pallas_call x5, Pallas kernels: 84 us -> 63.8 us  [z_modes(): pl.pallas_call(functools.partial(z_kernel, parts), grid=(steps,), in_spec...]
    ppermute x15, starting transfers between devices: 63.9 us -> 75.2 us  [local(): lax.ppermute(part[d], 'col', [(i, (i + d) % cols) for i in range(cols)])]
    ppermute x15, waiting for transfers between devices: 27.7 us -> 38.5 us  [local(): lax.ppermute(part[d], 'col', [(i, (i + d) % cols) for i in range(cols)])]
    all_to_all x2 -> x3, starting transfers between devices: 9.71 us -> 14.6 us  [local(): part = lax.all_to_all(part, 'row', split_axis=0, concat_axis=0, tiled=True)]
  transfers between devices with their start and end apart: 17 -> 18, of which waited for: 7 -> 6; matrix products, arithmetic and copies ran while one was open for 3% -> 3% of each run, Pallas kernels for 28% -> 23%
where the time goes in v5:
time: 447 us; the launch traced here: 446 us
  waiting for transfers between devices  140 us (31%)
  Pallas kernels  130 us (29%)
  starting transfers between devices  89.8 us (20%)
  blocking collectives  68.2 us (15%)
  other arithmetic  15.2 us (3%)
    all_to_all x3, waiting for transfers between devices, local(): part = lax.all_to_all(part, 'row', split_axis=0, concat_axis=0, tiled=True)  101 us
    ppermute x15, starting transfers between devices, local(): lax.ppermute(part[d], 'col', [(i, (i + d) % cols) for i in range(cols)])  75.2 us
    all_to_all x2, blocking collectives, local(): part = lax.all_to_all(part, 'row', split_axis=0, concat_axis=0, tiled=True)  68.2 us
    pallas_call x5, Pallas kernels, z_modes(): pl.pallas_call(functools.partial(z_kernel, parts), grid=(steps,), in_spec...  63.8 us
    ppermute x15, waiting for transfers between devices, local(): lax.ppermute(part[d], 'col', [(i, (i + d) % cols) for i in range(cols)])  38.5 us
    pallas_call x5, Pallas kernels, y_modes(): pl.pallas_call(y_kernel, grid=(planes, zs // width), in_specs=[pl.BlockSp...  30.2 us
    pallas_call x2, Pallas kernels, x_modes(): pl.pallas_call(functools.partial(x_kernel, group, unroll), grid=(zs // 12...  30.1 us
    all_to_all x3, starting transfers between devices, local(): part = lax.all_to_all(part, 'row', split_axis=0, concat_axis=0, tiled=True)  14.6 us
  transfers between devices with their start and end apart: 18, of which 6 were waited for; matrix products, arithmetic and copies ran while one was open for 3% of the time, Pallas kernels for 23%

profile of v5, /device:TPU:0, one launch (start us, length us, event | category | flops | bytes accessed | tf_op | source)
XLA Modules:
  0.0 446.1 jit_solution(3901124041198336566)
XLA Ops:
  0.0 3.7 reduce-precision_convert_fusion.1
  3.7 0.9 pad_maximum_fusion.1.a_ref
  4.6 16.9 %shard_map.64 = (f32[128,2,8,512]{3,2,1,0:T(8,128)}, f32[96,2,8,512]{3,2,1,0:T(8,128)}, f32[64,2,8,512]{3,2,1,0:T(8,128)}, f32[64,2,8,512]{3,2,1,0:T(8,128)}) custom-call(bf16[704,512]{1,0:T(8,128)(2,1)} %pad_maximum_fusion.1.a_ref, f32[512,2,8,512]{3,2,1,0:T(8,128)} %bitcast.11), custom_call_target="tpu_custom_call" | custom-call | flops 8858370048 | bytes 16777216 | tf_op jit(solution)/shard_map/pallas_call | solution.py:85
  21.5 36.1 %all_to_all.25.v_ref = f32[32,2,16,512]{3,2,1,0:T(8,128)} all-to-all(f32[32,2,16,512]{3,2,1,0:T(8,128)} %bitcast.15), channel_id=1, replica_groups=mesh['row'=32,'col'=4] {'row'}, dimensions={0} | all-to-all | bytes 4194304 | tf_op jit(solution)/shard_map/all_to_all | solution.py:266
  57.6 32.1 %all_to_all.26.v_ref = f32[32,2,16,512]{3,2,1,0:T(8,128)} all-to-all(f32[32,2,16,512]{3,2,1,0:T(8,128)S(1)} %bitcast.14), channel_id=1, replica_groups=mesh['row'=32,'col'=4] {'row'}, dimensions={0} | all-to-all | bytes 4194304 | tf_op jit(solution)/shard_map/all_to_all | solution.py:266
  89.7 4.9 %all-to-all-start.3 = ((f32[32,4,16,512]{3,2,1,0:T(8,128)}), f32[32,4,16,512]{3,2,1,0:T(8,128)}, u32[]{:S(2)}, u32[]{:S(2)}) async-start(f32[32,4,16,512]{3,2,1,0:T(8,128)} %bitcast.13), calls=%async_computation.3 | async-start | bytes 8388608 | tf_op jit(solution)/shard_map/all_to_all | solution.py:266
  94.6 13.2 %shard_map.70 = f32[160,2,8,512]{3,2,1,0:T(8,128)} custom-call(bf16[320,512]{1,0:T(8,128)(2,1)} %constant.152.clone.a_ref, f32[512,2,8,512]{3,2,1,0:T(8,128)} %bitcast.12), custom_call_target="tpu_custom_call" | custom-call | flops 4026531840 | bytes 16777216 | tf_op jit(solution)/shard_map/pallas_call | solution.py:85
  107.9 40.7 %all-to-all-done.3.v_ref = f32[32,4,16,512]{3,2,1,0:T(8,128)} async-done(((f32[32,4,16,512]{3,2,1,0:T(8,128)}), f32[32,4,16,512]{3,2,1,0:T(8,128)}, u32[]{:S(2)}, u32[]{:S(2)}) %all-to-all-start.3) | async-done | bytes 4194336 | tf_op jit(solution)/shard_map/all_to_all | solution.py:266
  148.6 4.9 %all-to-all-start.4 = ((f32[32,5,16,512]{3,2,1,0:T(8,128)}), f32[32,5,16,512]{3,2,1,0:T(8,128)}, u32[]{:S(2)}, u32[]{:S(2)}) async-start(f32[32,5,16,512]{3,2,1,0:T(8,128)} %bitcast.10), calls=%async_computation.4 | async-start | bytes 10485760 | tf_op jit(solution)/shard_map/all_to_all | solution.py:266
  153.5 4.4 reduce-precision_convert_fusion
  158.0 1.1 pad_maximum_fusion.a_ref
  159.0 60.3 %all-to-all-done.4.v_ref = f32[32,5,16,512]{3,2,1,0:T(8,128)} async-done(((f32[32,5,16,512]{3,2,1,0:T(8,128)}), f32[32,5,16,512]{3,2,1,0:T(8,128)}, u32[]{:S(2)}, u32[]{:S(2)}) %all-to-all-start.4) | async-done | bytes 5242912 | tf_op jit(solution)/shard_map/all_to_all | solution.py:266
  219.3 4.8 %all-to-all-start.2 = ((f32[32,3,16,512]{3,2,1,0:T(8,128)}), f32[32,3,16,512]{3,2,1,0:T(8,128)}, u32[]{:S(2)}, u32[]{:S(2)}) async-start(f32[32,3,16,512]{3,2,1,0:T(8,128)} %bitcast.6), calls=%async_computation.2 | async-start | bytes 6291456 | tf_op jit(solution)/shard_map/all_to_all | solution.py:266
  224.2 1.3 sine_multiply_fusion
  225.5 3.1 fusion.28
  228.6 4.4 shard_map.67
  233.0 1.9 collective-permute-start.3
  234.9 7.0 %shard_map.69 = (f32[4,128,512]{2,1,0:T(8,128)}, f32[4,128,512]{2,1,0:T(8,128)}, f32[4,128,512]{2,1,0:T(8,128)}, f32[4,128,512]{2,1,0:T(8,128)}) custom-call(bf16[1024,512]{1,0:T(8,128)(2,1)} %pad_maximum_fusion.a_ref, f32[32,4,16,512]{3,2,1,0:T(8,128)} %all-to-all-done.3.v_ref), custom_call_target="tpu_custom_call" | custom-call | flops 3221225472 | bytes 8388608 | tf_op jit(solution)/shard_map/pallas_call | solution.py:112
  241.9 1.9 collective-permute-start.9
  243.8 8.4 %shard_map.71 = (f32[5,128,512]{2,1,0:T(8,128)}, f32[5,128,512]{2,1,0:T(8,128)}, f32[5,128,512]{2,1,0:T(8,128)}, f32[5,128,512]{2,1,0:T(8,128)}) custom-call(bf16[1024,512]{1,0:T(8,128)(2,1)} %pad_maximum_fusion.a_ref, f32[32,5,16,512]{3,2,1,0:T(8,128)} %all-to-all-done.4.v_ref), custom_call_target="tpu_custom_call" | custom-call | flops 4026531840 | bytes 10485760 | tf_op jit(solution)/shard_map/pallas_call | solution.py:112
  252.2 1.6 collective-permute-start.12
  253.9 1.2 collective-permute-start.13
  255.0 1.7 collective-permute-start.14
  256.8 5.6 %shard_map.66 = (bf16[1024,2048]{1,0:T(8,128)(2,1)}, bf16[1024,2048]{1,0:T(8,128)(2,1)}) custom-call(f32[16,2048]{1,0:T(8,128)} %get-tuple-element.58.cos_ref, f32[16,2048]{1,0:T(8,128)} %get-tuple-element.57.sin_ref, f32[64,2048]{1,0:T(8,128)} %get-tuple-element.60.plus_ref, f32[64,2048]{1,0:T(8,128)} %get-tuple-element.59.minus_ref), custom_call_target="tpu_custom_call" | custom-call | flops 10000000000 | bytes 8388608 | tf_op jit(solution)/shard_map/pallas_call | solution.py:149
  262.4 0.8 dynamic_slice.7
  263.1 0.8 dynamic_slice.6
  263.9 0.7 bitcast_add_fusion
  264.6 1.6 collective-permute-start.10
  266.2 6.4 %collective-permute-done.9.refs_1_ = f32[4,128,512]{2,1,0:T(8,128)} collective-permute-done((f32[4,128,512]{2,1,0:T(8,128)}, f32[4,128,512]{2,1,0:T(8,128)}, u32[]{:S(2)}, u32[]{:S(2)}) %collective-permute-start.9) | collective-permute-done | bytes 1048608 | tf_op jit(solution)/shard_map/ppermute | solution.py:269
  272.6 2.0 collective-permute-start.11
  274.6 4.4 shard_map.65
  279.1 5.9 %shard_map.68 = (f32[3,128,512]{2,1,0:T(8,128)}, f32[3,128,512]{2,1,0:T(8,128)}, f32[3,128,512]{2,1,0:T(8,128)}, f32[3,128,512]{2,1,0:T(8,128)}) custom-call(bf16[1024,512]{1,0:T(8,128)(2,1)} %pad_maximum_fusion.a_ref, f32[32,3,16,512]{3,2,1,0:T(8,128)} %all-to-all-done.2.v_ref), custom_call_target="tpu_custom_call" | custom-call | flops 2415919104 | bytes 6291456 | tf_op jit(solution)/shard_map/pallas_call | solution.py:112
  285.0 15.1 %collective-permute-done.12.refs_1_ = f32[5,128,512]{2,1,0:T(8,128)} collective-permute-done((f32[5,128,512]{2,1,0:T(8,128)}, f32[5,128,512]{2,1,0:T(8,128)}, u32[]{:S(2)}, u32[]{:S(2)}) %collective-permute-start.12) | collective-permute-done | bytes 1310752 | tf_op jit(solution)/shard_map/ppermute | solution.py:269
  300.1 49.4 %collective-permute-start.6 = (f32[3,128,512]{2,1,0:T(8,128)}, f32[3,128,512]{2,1,0:T(8,128)}, u32[]{:S(2)}, u32[]{:S(2)}) collective-permute-start(f32[3,128,512]{2,1,0:T(8,128)} %get-tuple-element.45), channel_id=1, source_target_pairs={{0,1},{1,2},{2,3},{3,0},{4,5},{5,6},{6,7},{7,4},{8,9},{9,10},{10,1... | collective-permute-start | bytes 2359304 | tf_op jit(solution)/shard_map/ppermute | solution.py:269
  349.5 3.0 collective-permute-start.7
  352.5 2.6 collective-permute-start.8
  355.1 2.0 broadcast_in_dim.2.refs_8_
  357.1 17.6 %shard_map.72.refs_10_ = f32[16,128,2048]{2,1,0:T(8,128)} custom-call(f32[5,128,512]{2,1,0:T(8,128)} %get-tuple-element.53.refs_0_, f32[5,128,512]{2,1,0:T(8,128)} %collective-permute-done.12.refs_1_, f32[5,128,512]{2,1,0:T(8,128)} %collective-permute-done.13.refs_2_, f32[5,128,512]{2,1,0:T(8,128)} %collective-permute-done.14.refs_3_, ...), custom_call_target="tpu_custom_call" | custom-call | flops 8053063680 | bytes 18874368 | tf_op jit(solution)/shard_map/pallas_call | solution.py:215
  374.8 2.1 collective-permute-start.5
  376.9 14.8 %shard_map.73.refs_10_ = f32[16,128,2048]{2,1,0:T(8,128)} custom-call(f32[4,128,512]{2,1,0:T(8,128)} %get-tuple-element.49.refs_0_, f32[4,128,512]{2,1,0:T(8,128)} %collective-permute-done.9.refs_1_, f32[4,128,512]{2,1,0:T(8,128)} %collective-permute-done.10.refs_2_, ...), custom_call_target="tpu_custom_call", output_to_operand_aliasing={{}: (10, {})} | custom-call | flops 6442450944 | bytes 16777216 | tf_op jit(solution)/shard_map/pallas_call | solution.py:215
  391.8 0.4 collective-permute-start
  392.1 3.2 collective-permute-start.1
  395.3 2.5 collective-permute-start.2
  397.8 12.0 %shard_map.74.refs_10_ = f32[16,128,2048]{2,1,0:T(8,128)} custom-call(f32[3,128,512]{2,1,0:T(8,128)} %get-tuple-element.44.refs_0_, f32[3,128,512]{2,1,0:T(8,128)} %collective-permute-done.6.refs_1_, f32[3,128,512]{2,1,0:T(8,128)} %collective-permute-done.7.refs_2_, f32[3,128,512]{2,1,0:T(8,128)} %collective-permute-done.8.refs_3_, ...), custom_call_target="tpu_custom_call", output_to_operand_aliasing={{}: (10, {})} | custom-call | flops 4831838208 | bytes 14680064 | tf_op jit(solution)/shard_map/pallas_call | solution.py:215
  409.8 5.8 %collective-permute-done.5.refs_3_ = f32[2,128,512]{2,1,0:T(8,128)} collective-permute-done((f32[2,128,512]{2,1,0:T(8,128)}, f32[2,128,512]{2,1,0:T(8,128)}, u32[]{:S(2)}, u32[]{:S(2)}) %collective-permute-start.5) | collective-permute-done | bytes 524320 | tf_op jit(solution)/shard_map/ppermute | solution.py:269
  415.7 9.6 %shard_map.75.refs_10_ = f32[16,128,2048]{2,1,0:T(8,128)} custom-call(f32[2,128,512]{2,1,0:T(8,128)} %get-tuple-element.39.refs_0_, f32[2,128,512]{2,1,0:T(8,128)} %collective-permute-done.3.refs_1_, f32[2,128,512]{2,1,0:T(8,128)} %collective-permute-done.4.refs_2_, f32[2,128,512]{2,1,0:T(8,128)} %collective-permute-done.5.refs_3_, ...), custom_call_target="tpu_custom_call", output_to_operand_aliasing={{}: (10, {})} | custom-call | flops 3221225472 | bytes 12582912 | tf_op jit(solution)/shard_map/pallas_call | solution.py:215
  425.3 11.2 %collective-permute-done.2.refs_3_ = f32[2,128,512]{2,1,0:T(8,128)} collective-permute-done((f32[2,128,512]{2,1,0:T(8,128)}, f32[2,128,512]{2,1,0:T(8,128)}, u32[]{:S(2)}, u32[]{:S(2)}) %collective-permute-start.2) | collective-permute-done | bytes 524320 | tf_op jit(solution)/shard_map/ppermute | solution.py:269
  436.5 9.6 %shard_map.76 = f32[16,128,2048]{2,1,0:T(8,128)} custom-call(f32[2,128,512]{2,1,0:T(8,128)} %get-tuple-element.32.refs_0_, f32[2,128,512]{2,1,0:T(8,128)} %collective-permute-done.refs_1_, f32[2,128,512]{2,1,0:T(8,128)} %collective-permute-done.1.refs_2_, f32[2,128,512]{2,1,0:T(8,128)} %collective-permute-done.2.refs_3_, ...), custom_call_target="tpu_custom_call", output_to_operand_aliasing={{}: (10, {})} | custom-call | flops 3221225472 | bytes 12582912 | tf_op jit(solution)/shard_map/pallas_call | solution.py:215
  (19 shorter events, 0.2 us)
Async XLA Ops:
  21.5 36.1 %copy-start = (f32[64,2,8,512]{3,2,1,0:T(8,128)S(1)}, f32[64,2,8,512]{3,2,1,0:T(8,128)}, u32[]{:S(2)}) copy-start(f32[64,2,8,512]{3,2,1,0:T(8,128)} %get-tuple-element.31) | copy-start | bytes 6291460
  89.7 58.8 %all-to-all-start.3 = ((f32[32,4,16,512]{3,2,1,0:T(8,128)}), f32[32,4,16,512]{3,2,1,0:T(8,128)}, u32[]{:S(2)}, u32[]{:S(2)}) async-start(f32[32,4,16,512]{3,2,1,0:T(8,128)} %bitcast.13), calls=%async_computation.3 | async-start | bytes 8388608 | tf_op jit(solution)/shard_map/all_to_all | solution.py:266
  148.6 70.8 %all-to-all-start.4 = ((f32[32,5,16,512]{3,2,1,0:T(8,128)}), f32[32,5,16,512]{3,2,1,0:T(8,128)}, u32[]{:S(2)}, u32[]{:S(2)}) async-start(f32[32,5,16,512]{3,2,1,0:T(8,128)} %bitcast.10), calls=%async_computation.4 | async-start | bytes 10485760 | tf_op jit(solution)/shard_map/all_to_all | solution.py:266
  219.3 59.7 %all-to-all-start.2 = ((f32[32,3,16,512]{3,2,1,0:T(8,128)}), f32[32,3,16,512]{3,2,1,0:T(8,128)}, u32[]{:S(2)}, u32[]{:S(2)}) async-start(f32[32,3,16,512]{3,2,1,0:T(8,128)} %bitcast.6), calls=%async_computation.2 | async-start | bytes 6291456 | tf_op jit(solution)/shard_map/all_to_all | solution.py:266
  233.0 31.6 %collective-permute-start.3 = (f32[2,128,512]{2,1,0:T(8,128)}, f32[2,128,512]{2,1,0:T(8,128)}, u32[]{:S(2)}, u32[]{:S(2)}) collective-permute-start(f32[2,128,512]{2,1,0:T(8,128)} %get-tuple-element.40), channel_id=1, source_target_pairs={{0,1},{1,2},{2,3},{3,0},{4,5},{5,6},{6,7},{7,4},{8,9},{9,10},{10,1... | collective-permute-start | bytes 1572872 | tf_op jit(solution)/shard_map/ppermute | solution.py:269
  241.9 30.7 %collective-permute-start.9 = (f32[4,128,512]{2,1,0:T(8,128)}, f32[4,128,512]{2,1,0:T(8,128)}, u32[]{:S(2)}, u32[]{:S(2)}) collective-permute-start(f32[4,128,512]{2,1,0:T(8,128)} %get-tuple-element.50), channel_id=1, source_target_pairs={{0,1},{1,2},{2,3},{3,0},{4,5},{5,6},{6,7},{7,4},{8,9},{9,10},{10,1... | collective-permute-start | bytes 3145736 | tf_op jit(solution)/shard_map/ppermute | solution.py:269
  252.2 47.9 %collective-permute-start.12 = (f32[5,128,512]{2,1,0:T(8,128)}, f32[5,128,512]{2,1,0:T(8,128)}, u32[]{:S(2)}, u32[]{:S(2)}) collective-permute-start(f32[5,128,512]{2,1,0:T(8,128)} %get-tuple-element.54), channel_id=1, source_target_pairs={{0,1},{1,2},{2,3},{3,0},{4,5},{5,6},{6,7},{7,4},{8,9},{9,10},{10,1... | collective-permute-start | bytes 3932168 | tf_op jit(solution)/shard_map/ppermute | solution.py:269
  253.9 95.6 %collective-permute-start.13 = (f32[5,128,512]{2,1,0:T(8,128)}, f32[5,128,512]{2,1,0:T(8,128)}, u32[]{:S(2)}, u32[]{:S(2)}) collective-permute-start(f32[5,128,512]{2,1,0:T(8,128)} %get-tuple-element.55), channel_id=1, source_target_pairs={{0,2},{1,3},{2,0},{3,1},{4,6},{5,7},{6,4},{7,5},{8,10},{9,11},{10,... | collective-permute-start | bytes 3932168 | tf_op jit(solution)/shard_map/ppermute | solution.py:269
  255.0 97.5 %collective-permute-start.14 = (f32[5,128,512]{2,1,0:T(8,128)}, f32[5,128,512]{2,1,0:T(8,128)}, u32[]{:S(2)}, u32[]{:S(2)}) collective-permute-start(f32[5,128,512]{2,1,0:T(8,128)} %get-tuple-element.56), channel_id=1, source_target_pairs={{0,3},{1,0},{2,1},{3,2},{4,7},{5,4},{6,5},{7,6},{8,11},{9,8},{10,9... | collective-permute-start | bytes 3932168 | tf_op jit(solution)/shard_map/ppermute | solution.py:269
  264.6 110.2 %collective-permute-start.10 = (f32[4,128,512]{2,1,0:T(8,128)}, f32[4,128,512]{2,1,0:T(8,128)}, u32[]{:S(2)}, u32[]{:S(2)}) collective-permute-start(f32[4,128,512]{2,1,0:T(8,128)} %get-tuple-element.51), channel_id=1, source_target_pairs={{0,2},{1,3},{2,0},{3,1},{4,6},{5,7},{6,4},{7,5},{8,10},{9,11},{10,... | collective-permute-start | bytes 3145736 | tf_op jit(solution)/shard_map/ppermute | solution.py:269
  272.6 102.2 %collective-permute-start.11 = (f32[4,128,512]{2,1,0:T(8,128)}, f32[4,128,512]{2,1,0:T(8,128)}, u32[]{:S(2)}, u32[]{:S(2)}) collective-permute-start(f32[4,128,512]{2,1,0:T(8,128)} %get-tuple-element.52), channel_id=1, source_target_pairs={{0,3},{1,0},{2,1},{3,2},{4,7},{5,4},{6,5},{7,6},{8,11},{9,8},{10,9... | collective-permute-start | bytes 3145736 | tf_op jit(solution)/shard_map/ppermute | solution.py:269
  300.1 91.7 %collective-permute-start.6 = (f32[3,128,512]{2,1,0:T(8,128)}, f32[3,128,512]{2,1,0:T(8,128)}, u32[]{:S(2)}, u32[]{:S(2)}) collective-permute-start(f32[3,128,512]{2,1,0:T(8,128)} %get-tuple-element.45), channel_id=1, source_target_pairs={{0,1},{1,2},{2,3},{3,0},{4,5},{5,6},{6,7},{7,4},{8,9},{9,10},{10,1... | collective-permute-start | bytes 2359304 | tf_op jit(solution)/shard_map/ppermute | solution.py:269
  349.5 42.7 %collective-permute-start.7 = (f32[3,128,512]{2,1,0:T(8,128)}, f32[3,128,512]{2,1,0:T(8,128)}, u32[]{:S(2)}, u32[]{:S(2)}) collective-permute-start(f32[3,128,512]{2,1,0:T(8,128)} %get-tuple-element.46), channel_id=1, source_target_pairs={{0,2},{1,3},{2,0},{3,1},{4,6},{5,7},{6,4},{7,5},{8,10},{9,11},{10,... | collective-permute-start | bytes 2359304 | tf_op jit(solution)/shard_map/ppermute | solution.py:269
  352.5 42.8 %collective-permute-start.8 = (f32[3,128,512]{2,1,0:T(8,128)}, f32[3,128,512]{2,1,0:T(8,128)}, u32[]{:S(2)}, u32[]{:S(2)}) collective-permute-start(f32[3,128,512]{2,1,0:T(8,128)} %get-tuple-element.47), channel_id=1, source_target_pairs={{0,3},{1,0},{2,1},{3,2},{4,7},{5,4},{6,5},{7,6},{8,11},{9,8},{10,9... | collective-permute-start | bytes 2359304 | tf_op jit(solution)/shard_map/ppermute | solution.py:269
  374.7 35.1 %collective-permute-start.4 = (f32[2,128,512]{2,1,0:T(8,128)}, f32[2,128,512]{2,1,0:T(8,128)}, u32[]{:S(2)}, u32[]{:S(2)}) collective-permute-start(f32[2,128,512]{2,1,0:T(8,128)} %get-tuple-element.41), channel_id=1, source_target_pairs={{0,2},{1,3},{2,0},{3,1},{4,6},{5,7},{6,4},{7,5},{8,10},{9,11},{10,... | collective-permute-start | bytes 1572872 | tf_op jit(solution)/shard_map/ppermute | solution.py:269
  374.8 40.8 %collective-permute-start.5 = (f32[2,128,512]{2,1,0:T(8,128)}, f32[2,128,512]{2,1,0:T(8,128)}, u32[]{:S(2)}, u32[]{:S(2)}) collective-permute-start(f32[2,128,512]{2,1,0:T(8,128)} %get-tuple-element.42), channel_id=1, source_target_pairs={{0,3},{1,0},{2,1},{3,2},{4,7},{5,4},{6,5},{7,6},{8,11},{9,8},{10,9... | collective-permute-start | bytes 1572872 | tf_op jit(solution)/shard_map/ppermute | solution.py:269
  391.8 33.5 %collective-permute-start = (f32[2,128,512]{2,1,0:T(8,128)}, f32[2,128,512]{2,1,0:T(8,128)}, u32[]{:S(2)}, u32[]{:S(2)}) collective-permute-start(f32[2,128,512]{2,1,0:T(8,128)} %get-tuple-element.33), channel_id=1, source_target_pairs={{0,1},{1,2},{2,3},{3,0},{4,5},{5,6},{6,7},{7,4},{8,9},{9,10},{10,1... | collective-permute-start | bytes 1572872 | tf_op jit(solution)/shard_map/ppermute | solution.py:269
  392.1 33.2 %collective-permute-start.1 = (f32[2,128,512]{2,1,0:T(8,128)}, f32[2,128,512]{2,1,0:T(8,128)}, u32[]{:S(2)}, u32[]{:S(2)}) collective-permute-start(f32[2,128,512]{2,1,0:T(8,128)} %get-tuple-element.34), channel_id=1, source_target_pairs={{0,2},{1,3},{2,0},{3,1},{4,6},{5,7},{6,4},{7,5},{8,10},{9,11},{10,... | collective-permute-start | bytes 1572872 | tf_op jit(solution)/shard_map/ppermute | solution.py:269
  395.3 41.1 %collective-permute-start.2 = (f32[2,128,512]{2,1,0:T(8,128)}, f32[2,128,512]{2,1,0:T(8,128)}, u32[]{:S(2)}, u32[]{:S(2)}) collective-permute-start(f32[2,128,512]{2,1,0:T(8,128)} %get-tuple-element.35), channel_id=1, source_target_pairs={{0,3},{1,0},{2,1},{3,2},{4,7},{5,4},{6,5},{7,6},{8,11},{9,8},{10,9... | collective-permute-start | bytes 1572872 | tf_op jit(solution)/shard_map/ppermute | solution.py:269

commit v6 on v5

--- a/solution.py
+++ b/solution.py
@@ -8,11 +8,8 @@
 from jax.experimental.pallas import tpu as pltpu
 from jax.sharding import PartitionSpec as P
 
-SIZES = (5, 4, 3, 2, 2)
-STARTS = (0, 5, 9, 12, 14)
+CHUNKS = ((0, 8, 0, 2), (0, 8, 1, 2), (8, 4, 0, 1), (12, 3, 0, 1), (15, 1, 0, 1))
 Z_COLS = 512
-X_FORM = ((4, 2), (4, 2))
-Y_WIDTH = 512
 VMEM = 67043328
 
 
@@ -56,41 +53,41 @@
     return jnp.cos(2.0 * jnp.pi / count * turns - jnp.pi / 4) * (2.0 / count) ** 0.5
 
 
-def x_kernel(group, unroll, a_ref, v_ref, *o_refs):
+def x_kernel(a_ref, v_ref, *o_refs):
     xs, _, tile, lanes = v_ref.shape
     v_ref = v_ref.reshape(xs * tile, lanes)
     o_refs = [o_ref.reshape(o_ref.shape[0] * tile, lanes) for o_ref in o_refs]
     a = a_ref[...]
 
     def body(s, _):
-        y = s * group
-        lines = [v_ref[pl.ds(y + k, xs, stride=tile), :] for k in range(group)]
+        y = s * 4
+        lines = [v_ref[pl.ds(y + k, xs, stride=tile), :] for k in range(4)]
         out = mm3(a, jnp.concatenate(lines, axis=1))
         first = 0
         for o_ref in o_refs:
             modes = o_ref.shape[0] // tile
-            for k in range(group):
+            for k in range(4):
                 o_ref[pl.ds(y + k, modes, stride=tile), :] = out[first : first + modes, lanes * k : lanes * (k + 1)]
             first += modes
         return 0
 
-    lax.fori_loop(0, tile // group, body, 0, unroll=unroll)
-
-
-def x_modes(velocity, table, shares):
+    lax.fori_loop(0, tile // 4, body, 0)
+
+
+def x_modes(velocity, table, shares, part=0, parts=1):
     xs, ys, zs = velocity.shape
     modes = table.shape[0] // 2
     tile = 8
-    group, unroll = X_FORM[modes < 256]
-    return pl.pallas_call(
-        functools.partial(x_kernel, group, unroll),
-        grid=(zs // 128, ys // tile),
+    blocks = zs // 128 // parts
+    return pl.pallas_call(
+        x_kernel,
+        grid=(blocks, ys // tile),
         in_specs=[
             pl.BlockSpec((2 * modes, xs), lambda i, k: (0, 0)),
-            pl.BlockSpec((xs, 1, tile, 128), lambda i, k: (0, k, 0, i)),
+            pl.BlockSpec((xs, 1, tile, 128), lambda i, k: (0, k, 0, part * blocks + i)),
         ],
         out_specs=[pl.BlockSpec((m, 1, tile, 128), lambda i, k: (0, k, 0, i)) for m in shares],
-        out_shape=[jax.ShapeDtypeStruct((m, ys // tile, tile, zs), jnp.float32) for m in shares],
+        out_shape=[jax.ShapeDtypeStruct((m, ys // tile, tile, zs // parts), jnp.float32) for m in shares],
         compiler_params=pltpu.CompilerParams(vmem_limit_bytes=VMEM),
         cost_estimate=pl.CostEstimate(flops=6 * modes * xs * ys * zs, bytes_accessed=4 * xs * ys * zs, transcendentals=0),
     )(table, velocity.reshape(xs, ys // tile, tile, zs))
@@ -108,7 +105,7 @@
 def y_modes(values, table, parts):
     blocks, planes, ys, zs = values.shape
     n = blocks * ys
-    width = Y_WIDTH
+    width = zs
     return pl.pallas_call(
         y_kernel,
         grid=(planes, zs // width),
@@ -250,24 +247,30 @@
     z_tables = wide_table(outer, jnp.arange(low_count), lane % half * 2 + lane // half, all_z)
 
     x_parts = []
-    for name, pick in (("x0", range(1)), ("x1", range(1, len(SIZES)))):
+    for name, picked in (("x0", CHUNKS[:1]), ("x1", CHUNKS[1:2]), ("x2", CHUNKS[2:])):
         mode = np.concatenate(
-            [(np.arange(rows)[:, None] * planes + STARTS[j] + np.arange(SIZES[j])).reshape(-1) for j in pick]
+            [(np.arange(rows)[:, None] * planes + start + np.arange(size)).reshape(-1) for start, size, _, _ in picked]
         )
-        if name == "x0":
+        if name == "x2":
+            x_table = stacked(small_table(jnp.asarray(mode, jnp.int32), xs))
+        elif name == "x0":
             x_table = fixed_table(mode, xs)
-        else:
-            x_table = stacked(small_table(jnp.asarray(mode, jnp.int32), xs))
-        x_parts += x_modes(velocity, x_table, [rows * SIZES[j] for j in pick])
-
+        x_parts += x_modes(velocity, x_table, [rows * size for _, size, _, _ in picked], *picked[0][2:])
+
+    waiting = []
     out = None
-    for j, (size, start) in enumerate(zip(SIZES, STARTS)):
-        part = x_parts[j].reshape(rows, size, ys, zs)
+    for j, (start, size, piece, pieces) in enumerate(CHUNKS):
+        part = x_parts[j].reshape(rows, size, ys, zs // pieces)
         part = lax.all_to_all(part, "row", split_axis=0, concat_axis=0, tiled=True)
         part = y_modes(part, y_table, cols)
         part = [part[0]] + [
             lax.ppermute(part[d], "col", [(i, (i + d) % cols) for i in range(cols)]) for d in range(1, cols)
         ]
+        waiting.append(part)
+        if piece + 1 < pieces:
+            continue
+        part = [piece[d] for d in range(cols) for piece in waiting]
+        waiting = []
         out = z_modes(part, z_tables, sxy, symbol_z, start, planes, out)
     return out
 

time: 447 us -> 451 us (level)
  waiting for transfers between devices: 140 us -> 175 us
  starting transfers between devices: 89.8 us -> 64.8 us
  blocking collectives: 68.2 us -> 55.7 us
  Pallas kernels: 130 us -> 135 us
    ppermute x15, waiting for transfers between devices: 38.5 us -> 75.8 us  [local(): lax.ppermute(part[d], 'col', [(i, (i + d) % cols) for i in range(cols)])]
    ppermute x15, starting transfers between devices: 75.2 us -> 42.7 us  [local(): lax.ppermute(part[d], 'col', [(i, (i + d) % cols) for i in range(cols)])]
    all_to_all x2 -> x1, blocking collectives: 68.2 us -> 55.7 us  [local(): part = lax.all_to_all(part, 'row', split_axis=0, concat_axis=0, tiled=True)]
    all_to_all x3 -> x4, starting transfers between devices: 14.6 us -> 22.1 us  [local(): part = lax.all_to_all(part, 'row', split_axis=0, concat_axis=0, tiled=True)]
    pallas_call x2 -> x3, Pallas kernels: 30.1 us -> 34.8 us  [x_modes(): pl.pallas_call(x_kernel, grid=(blocks, ys // tile), in_specs=[pl.BlockSpe...]
    pallas_call x5 -> x4, Pallas kernels: 63.8 us -> 60.8 us  [z_modes(): pl.pallas_call(functools.partial(z_kernel, parts), grid=(steps,), in_spec...]
    all_to_all x3 -> x4, waiting for transfers between devices: 101 us -> 99 us  [local(): part = lax.all_to_all(part, 'row', split_axis=0, concat_axis=0, tiled=True)]
  transfers between devices with their start and end apart: 18 -> 19, of which waited for: 6 -> 8; matrix products, arithmetic and copies ran while one was open for 3% -> 3% of each run, Pallas kernels for 23% -> 25%
where the time goes in v6:
time: 451 us; the launch traced here: 449 us
  waiting for transfers between devices  175 us (39%)
  Pallas kernels  135 us (30%)
  starting transfers between devices  64.8 us (14%)
  blocking collectives  55.7 us (12%)
  other arithmetic  15.6 us (3%)
    all_to_all x4, waiting for transfers between devices, local(): part = lax.all_to_all(part, 'row', split_axis=0, concat_axis=0, tiled=True)  99 us
    ppermute x15, waiting for transfers between devices, local(): lax.ppermute(part[d], 'col', [(i, (i + d) % cols) for i in range(cols)])  75.8 us
    pallas_call x4, Pallas kernels, z_modes(): pl.pallas_call(functools.partial(z_kernel, parts), grid=(steps,), in_spec...  60.8 us
    all_to_all x1, blocking collectives, local(): part = lax.all_to_all(part, 'row', split_axis=0, concat_axis=0, tiled=True)  55.7 us
    ppermute x15, starting transfers between devices, local(): lax.ppermute(part[d], 'col', [(i, (i + d) % cols) for i in range(cols)])  42.7 us
    pallas_call x3, Pallas kernels, x_modes(): pl.pallas_call(x_kernel, grid=(blocks, ys // tile), in_specs=[pl.BlockSpe...  34.8 us
    pallas_call x5, Pallas kernels, y_modes(): pl.pallas_call(y_kernel, grid=(planes, zs // width), in_specs=[pl.BlockSp...  33.4 us
    all_to_all x4, starting transfers between devices, local(): part = lax.all_to_all(part, 'row', split_axis=0, concat_axis=0, tiled=True)  22.1 us
  transfers between devices with their start and end apart: 19, of which 8 were waited for; matrix products, arithmetic and copies ran while one was open for 3% of the time, Pallas kernels for 25%

profile of v6, /device:TPU:0, one launch (start us, length us, event | category | flops | bytes accessed | tf_op | source)
XLA Modules:
  0.0 449.2 jit_solution(13637077316144560258)
XLA Ops:
  0.0 2.9 reduce-precision_convert_fusion.1
  2.9 0.8 pad_maximum_fusion.1.a_ref
  3.7 16.3 %shard_map.64 = (f32[128,2,8,512]{3,2,1,0:T(8,128)}, f32[96,2,8,512]{3,2,1,0:T(8,128)}, f32[32,2,8,512]{3,2,1,0:T(8,128)}) custom-call(bf16[512,512]{1,0:T(8,128)(2,1)} %pad_maximum_fusion.1.a_ref, f32[512,2,8,512]{3,2,1,0:T(8,128)} %bitcast.19), custom_call_target="tpu_custom_call" | custom-call | flops 6442450944 | bytes 16777216 | tf_op jit(solution)/shard_map/pallas_call | solution.py:82
  20.0 7.5 %all-to-all-start = ((f32[32,1,16,512]{3,2,1,0:T(8,128)}), f32[32,1,16,512]{3,2,1,0:T(8,128)}, u32[]{:S(2)}, u32[]{:S(2)}) async-start(f32[32,1,16,512]{3,2,1,0:T(8,128)} %bitcast.13), calls=%async_computation | async-start | bytes 2097152 | tf_op jit(solution)/shard_map/all_to_all | solution.py:264
  27.5 9.3 %shard_map.71 = f32[256,2,8,256]{3,2,1,0:T(8,128)} custom-call(bf16[512,512]{1,0:T(8,128)(2,1)} %constant.152.clone.a_ref, f32[512,2,8,512]{3,2,1,0:T(8,128)} %bitcast.20), custom_call_target="tpu_custom_call" | custom-call | flops 6442450944 | bytes 16777216 | tf_op jit(solution)/shard_map/pallas_call | solution.py:82
  36.8 7.9 %all-to-all-done.v_ref = f32[32,1,16,512]{3,2,1,0:T(8,128)} async-done(((f32[32,1,16,512]{3,2,1,0:T(8,128)}), f32[32,1,16,512]{3,2,1,0:T(8,128)}, u32[]{:S(2)}, u32[]{:S(2)}) %all-to-all-start) | async-done | bytes 1048608 | tf_op jit(solution)/shard_map/all_to_all | solution.py:264
  44.7 4.9 %all-to-all-start.4 = ((f32[32,8,16,256]{3,2,1,0:T(8,128)}), f32[32,8,16,256]{3,2,1,0:T(8,128)}, u32[]{:S(2)}, u32[]{:S(2)}) async-start(f32[32,8,16,256]{3,2,1,0:T(8,128)} %bitcast.11), calls=%async_computation.4 | async-start | bytes 8388608 | tf_op jit(solution)/shard_map/all_to_all | solution.py:264
  49.6 9.2 %shard_map.69 = f32[256,2,8,256]{3,2,1,0:T(8,128)} custom-call(bf16[512,512]{1,0:T(8,128)(2,1)} %constant.152.clone.a_ref, f32[512,2,8,512]{3,2,1,0:T(8,128)} %bitcast.21), custom_call_target="tpu_custom_call" | custom-call | flops 6442450944 | bytes 16777216 | tf_op jit(solution)/shard_map/pallas_call | solution.py:82
  58.8 44.7 %all-to-all-done.4.v_ref = f32[32,8,16,256]{3,2,1,0:T(8,128)} async-done(((f32[32,8,16,256]{3,2,1,0:T(8,128)}), f32[32,8,16,256]{3,2,1,0:T(8,128)}, u32[]{:S(2)}, u32[]{:S(2)}) %all-to-all-start.4) | async-done | bytes 4194336 | tf_op jit(solution)/shard_map/all_to_all | solution.py:264
  103.5 55.7 %all_to_all.25.v_ref = f32[32,8,16,256]{3,2,1,0:T(8,128)} all-to-all(f32[32,8,16,256]{3,2,1,0:T(8,128)} %bitcast.12), channel_id=1, replica_groups=mesh['row'=32,'col'=4] {'row'}, dimensions={0} | all-to-all | bytes 8388608 | tf_op jit(solution)/shard_map/all_to_all | solution.py:264
  159.3 4.9 %all-to-all-start.2 = ((f32[32,4,16,512]{3,2,1,0:T(8,128)}), f32[32,4,16,512]{3,2,1,0:T(8,128)}, u32[]{:S(2)}, u32[]{:S(2)}) async-start(f32[32,4,16,512]{3,2,1,0:T(8,128)} %bitcast.10), calls=%async_computation.2 | async-start | bytes 8388608 | tf_op jit(solution)/shard_map/all_to_all | solution.py:264
  164.2 0.8 dynamic_slice.7
  164.9 0.8 dynamic_slice.6
  165.7 0.5 fusion.43
  166.2 4.4 reduce-precision_convert_fusion
  170.7 1.1 pad_maximum_fusion.a_ref
  171.8 46.3 %all-to-all-done.2.v_ref = f32[32,4,16,512]{3,2,1,0:T(8,128)} async-done(((f32[32,4,16,512]{3,2,1,0:T(8,128)}), f32[32,4,16,512]{3,2,1,0:T(8,128)}, u32[]{:S(2)}, u32[]{:S(2)}) %all-to-all-start.2) | async-done | bytes 4194336 | tf_op jit(solution)/shard_map/all_to_all | solution.py:264
  218.1 4.8 %all-to-all-start.1 = ((f32[32,3,16,512]{3,2,1,0:T(8,128)}), f32[32,3,16,512]{3,2,1,0:T(8,128)}, u32[]{:S(2)}, u32[]{:S(2)}) async-start(f32[32,3,16,512]{3,2,1,0:T(8,128)} %bitcast.5), calls=%async_computation.1 | async-start | bytes 6291456 | tf_op jit(solution)/shard_map/all_to_all | solution.py:264
  223.0 0.7 bitcast_add_fusion
  223.6 3.1 fusion.28
  226.7 8.5 %shard_map.72 = (f32[8,128,256]{2,1,0:T(8,128)}, f32[8,128,256]{2,1,0:T(8,128)}, f32[8,128,256]{2,1,0:T(8,128)}, f32[8,128,256]{2,1,0:T(8,128)}) custom-call(bf16[1024,512]{1,0:T(8,128)(2,1)} %pad_maximum_fusion.a_ref, f32[32,8,16,256]{3,2,1,0:T(8,128)} %all-to-all-done.4.v_ref), custom_call_target="tpu_custom_call" | custom-call | flops 3221225472 | bytes 8388608 | tf_op jit(solution)/shard_map/pallas_call | solution.py:109
  235.3 1.9 collective-permute-start.10
  237.2 3.6 collective-permute-start.12
  240.8 2.0 sine_multiply_fusion
  242.8 1.0 collective-permute-start.14
  243.8 8.6 %shard_map.70 = (f32[8,128,256]{2,1,0:T(8,128)}, f32[8,128,256]{2,1,0:T(8,128)}, f32[8,128,256]{2,1,0:T(8,128)}, f32[8,128,256]{2,1,0:T(8,128)}) custom-call(bf16[1024,512]{1,0:T(8,128)(2,1)} %pad_maximum_fusion.a_ref, f32[32,8,16,256]{3,2,1,0:T(8,128)} %all_to_all.25.v_ref), custom_call_target="tpu_custom_call" | custom-call | flops 3221225472 | bytes 8388608 | tf_op jit(solution)/shard_map/pallas_call | solution.py:109
  252.4 1.0 collective-permute-start.9
  253.4 0.5 collective-permute-start.11
  253.8 7.0 %shard_map.68 = (f32[4,128,512]{2,1,0:T(8,128)}, f32[4,128,512]{2,1,0:T(8,128)}, f32[4,128,512]{2,1,0:T(8,128)}, f32[4,128,512]{2,1,0:T(8,128)}) custom-call(bf16[1024,512]{1,0:T(8,128)(2,1)} %pad_maximum_fusion.a_ref, f32[32,4,16,512]{3,2,1,0:T(8,128)} %all-to-all-done.2.v_ref), custom_call_target="tpu_custom_call" | custom-call | flops 3221225472 | bytes 8388608 | tf_op jit(solution)/shard_map/pallas_call | solution.py:109
  260.8 3.1 collective-permute-done.10.refs_3_
  263.9 1.7 collective-permute-start.13
  265.6 22.0 %collective-permute-done.12.refs_5_ = f32[8,128,256]{2,1,0:T(8,128)} collective-permute-done((f32[8,128,256]{2,1,0:T(8,128)}, f32[8,128,256]{2,1,0:T(8,128)}, u32[]{:S(2)}, u32[]{:S(2)}) %collective-permute-start.12) | collective-permute-done | bytes 1048608 | tf_op jit(solution)/shard_map/ppermute | solution.py:267
  287.6 5.7 %shard_map.66 = (bf16[1024,2048]{1,0:T(8,128)(2,1)}, bf16[1024,2048]{1,0:T(8,128)(2,1)}) custom-call(f32[16,2048]{1,0:T(8,128)} %get-tuple-element.56.cos_ref, f32[16,2048]{1,0:T(8,128)} %get-tuple-element.55.sin_ref, f32[64,2048]{1,0:T(8,128)} %get-tuple-element.58.plus_ref, f32[64,2048]{1,0:T(8,128)} %get-tuple-element.57.minus_ref), custom_call_target="tpu_custom_call" | custom-call | flops 10000000000 | bytes 8388608 | tf_op jit(solution)/shard_map/pallas_call | solution.py:146
  293.3 3.4 shard_map.65
  296.7 5.9 %shard_map.67 = (f32[3,128,512]{2,1,0:T(8,128)}, f32[3,128,512]{2,1,0:T(8,128)}, f32[3,128,512]{2,1,0:T(8,128)}, f32[3,128,512]{2,1,0:T(8,128)}) custom-call(bf16[1024,512]{1,0:T(8,128)(2,1)} %pad_maximum_fusion.a_ref, f32[32,3,16,512]{3,2,1,0:T(8,128)} %all-to-all-done.1.v_ref), custom_call_target="tpu_custom_call" | custom-call | flops 2415919104 | bytes 6291456 | tf_op jit(solution)/shard_map/pallas_call | solution.py:109
  303.0 5.8 %collective-permute-done.9.refs_2_ = f32[8,128,256]{2,1,0:T(8,128)} collective-permute-done((f32[8,128,256]{2,1,0:T(8,128)}, f32[8,128,256]{2,1,0:T(8,128)}, u32[]{:S(2)}, u32[]{:S(2)}) %collective-permute-start.9) | collective-permute-done | bytes 1048608 | tf_op jit(solution)/shard_map/ppermute | solution.py:267
  308.8 24.1 %collective-permute-start.4 = (f32[3,128,512]{2,1,0:T(8,128)}, f32[3,128,512]{2,1,0:T(8,128)}, u32[]{:S(2)}, u32[]{:S(2)}) collective-permute-start(f32[3,128,512]{2,1,0:T(8,128)} %get-tuple-element.40), channel_id=1, source_target_pairs={{0,2},{1,3},{2,0},{3,1},{4,6},{5,7},{6,4},{7,5},{8,10},{9,11},{10,... | collective-permute-start | bytes 2359304 | tf_op jit(solution)/shard_map/ppermute | solution.py:267
  332.9 2.1 collective-permute-start.7
  335.1 18.4 %collective-permute-done.6.refs_1_ = f32[4,128,512]{2,1,0:T(8,128)} collective-permute-done((f32[4,128,512]{2,1,0:T(8,128)}, f32[4,128,512]{2,1,0:T(8,128)}, u32[]{:S(2)}, u32[]{:S(2)}) %collective-permute-start.6) | collective-permute-done | bytes 1048608 | tf_op jit(solution)/shard_map/ppermute | solution.py:267
  353.5 2.1 collective-permute-start.8
  355.6 2.0 broadcast_in_dim.2.refs_12_.refs_8_
  357.7 26.2 %shard_map.73.refs_10_ = f32[16,128,2048]{2,1,0:T(8,128)} custom-call(f32[8,128,256]{2,1,0:T(8,128)} %get-tuple-element.47.refs_0_, f32[8,128,256]{2,1,0:T(8,128)} %get-tuple-element.48.refs_1_, f32[8,128,256]{2,1,0:T(8,128)} %collective-permute-done.9.refs_2_, f32[8,128,256]{2,1,0:T(8,128)} %collective-permute-done.10.refs_3_, ...), custom_call_target="tpu_custom_call" | custom-call | flops 12884901888 | bytes 25165824 | tf_op jit(solution)/shard_map/pallas_call | solution.py:212
  383.9 26.5 %collective-permute-done.7.refs_2_ = f32[4,128,512]{2,1,0:T(8,128)} collective-permute-done((f32[4,128,512]{2,1,0:T(8,128)}, f32[4,128,512]{2,1,0:T(8,128)}, u32[]{:S(2)}, u32[]{:S(2)}) %collective-permute-start.7) | collective-permute-done | bytes 1048608 | tf_op jit(solution)/shard_map/ppermute | solution.py:267
  410.4 2.3 collective-permute-start.1
  412.6 15.0 %shard_map.74.refs_10_ = f32[16,128,2048]{2,1,0:T(8,128)} custom-call(f32[4,128,512]{2,1,0:T(8,128)} %get-tuple-element.43.refs_0_, f32[4,128,512]{2,1,0:T(8,128)} %collective-permute-done.6.refs_1_, f32[4,128,512]{2,1,0:T(8,128)} %collective-permute-done.7.refs_2_, f32[4,128,512]{2,1,0:T(8,128)} %collective-permute-done.8.refs_3_, ...), custom_call_target="tpu_custom_call", output_to_operand_aliasing={{}: (10, {})} | custom-call | flops 6442450944 | bytes 16777216 | tf_op jit(solution)/shard_map/pallas_call | solution.py:212
  427.6 2.0 collective-permute-start.2
  429.6 12.1 %shard_map.75.refs_10_ = f32[16,128,2048]{2,1,0:T(8,128)} custom-call(f32[3,128,512]{2,1,0:T(8,128)} %get-tuple-element.38.refs_0_, f32[3,128,512]{2,1,0:T(8,128)} %collective-permute-done.3.refs_1_, f32[3,128,512]{2,1,0:T(8,128)} %collective-permute-done.4.refs_2_, f32[3,128,512]{2,1,0:T(8,128)} %collective-permute-done.5.refs_3_, ...), custom_call_target="tpu_custom_call", output_to_operand_aliasing={{}: (10, {})} | custom-call | flops 4831838208 | bytes 14680064 | tf_op jit(solution)/shard_map/pallas_call | solution.py:212
  441.8 7.5 %shard_map.76 = f32[16,128,2048]{2,1,0:T(8,128)} custom-call(f32[1,128,512]{2,1,0:T(8,128)} %get-tuple-element.31.refs_0_, f32[1,128,512]{2,1,0:T(8,128)} %collective-permute-done.refs_1_, f32[1,128,512]{2,1,0:T(8,128)} %collective-permute-done.1.refs_2_, f32[1,128,512]{2,1,0:T(8,128)} %collective-permute-done.2.refs_3_, ...), custom_call_target="tpu_custom_call", output_to_operand_aliasing={{}: (10, {})} | custom-call | flops 1610612736 | bytes 10485760 | tf_op jit(solution)/shard_map/pallas_call | solution.py:212
  (20 shorter events, 0.4 us)
Async XLA Ops:
  20.0 24.7 %all-to-all-start = ((f32[32,1,16,512]{3,2,1,0:T(8,128)}), f32[32,1,16,512]{3,2,1,0:T(8,128)}, u32[]{:S(2)}, u32[]{:S(2)}) async-start(f32[32,1,16,512]{3,2,1,0:T(8,128)} %bitcast.13), calls=%async_computation | async-start | bytes 2097152 | tf_op jit(solution)/shard_map/all_to_all | solution.py:264
  44.7 58.8 %all-to-all-start.4 = ((f32[32,8,16,256]{3,2,1,0:T(8,128)}), f32[32,8,16,256]{3,2,1,0:T(8,128)}, u32[]{:S(2)}, u32[]{:S(2)}) async-start(f32[32,8,16,256]{3,2,1,0:T(8,128)} %bitcast.11), calls=%async_computation.4 | async-start | bytes 8388608 | tf_op jit(solution)/shard_map/all_to_all | solution.py:264
  159.3 58.8 %all-to-all-start.2 = ((f32[32,4,16,512]{3,2,1,0:T(8,128)}), f32[32,4,16,512]{3,2,1,0:T(8,128)}, u32[]{:S(2)}, u32[]{:S(2)}) async-start(f32[32,4,16,512]{3,2,1,0:T(8,128)} %bitcast.10), calls=%async_computation.2 | async-start | bytes 8388608 | tf_op jit(solution)/shard_map/all_to_all | solution.py:264
  166.2 57.4 %copy-start = (s32[2048]{0:T(1024)}, s32[2048]{0:T(1024)S(1)}, u32[]{:S(2)}) copy-start(s32[2048]{0:T(1024)S(1)} %fusion.39) | copy-start | bytes 24580
  218.1 78.6 %all-to-all-start.1 = ((f32[32,3,16,512]{3,2,1,0:T(8,128)}), f32[32,3,16,512]{3,2,1,0:T(8,128)}, u32[]{:S(2)}, u32[]{:S(2)}) async-start(f32[32,3,16,512]{3,2,1,0:T(8,128)} %bitcast.5), calls=%async_computation.1 | async-start | bytes 6291456 | tf_op jit(solution)/shard_map/all_to_all | solution.py:264
  235.3 28.6 %collective-permute-start.10 = (f32[8,128,256]{2,1,0:T(8,128)}, f32[8,128,256]{2,1,0:T(8,128)}, u32[]{:S(2)}, u32[]{:S(2)}) collective-permute-start(f32[8,128,256]{2,1,0:T(8,128)} %get-tuple-element.50), channel_id=1, source_target_pairs={{0,1},{1,2},{2,3},{3,0},{4,5},{5,6},{6,7},{7,4},{8,9},{9,10},{10,1... | collective-permute-start | bytes 3145736 | tf_op jit(solution)/shard_map/ppermute | solution.py:267
  237.2 50.4 %collective-permute-start.12 = (f32[8,128,256]{2,1,0:T(8,128)}, f32[8,128,256]{2,1,0:T(8,128)}, u32[]{:S(2)}, u32[]{:S(2)}) collective-permute-start(f32[8,128,256]{2,1,0:T(8,128)} %get-tuple-element.52), channel_id=1, source_target_pairs={{0,2},{1,3},{2,0},{3,1},{4,6},{5,7},{6,4},{7,5},{8,10},{9,11},{10,... | collective-permute-start | bytes 3145736 | tf_op jit(solution)/shard_map/ppermute | solution.py:267
  242.8 59.9 %collective-permute-start.14 = (f32[8,128,256]{2,1,0:T(8,128)}, f32[8,128,256]{2,1,0:T(8,128)}, u32[]{:S(2)}, u32[]{:S(2)}) collective-permute-start(f32[8,128,256]{2,1,0:T(8,128)} %get-tuple-element.54), channel_id=1, source_target_pairs={{0,3},{1,0},{2,1},{3,2},{4,7},{5,4},{6,5},{7,6},{8,11},{9,8},{10,9... | collective-permute-start | bytes 3145736 | tf_op jit(solution)/shard_map/ppermute | solution.py:267
  252.4 56.5 %collective-permute-start.9 = (f32[8,128,256]{2,1,0:T(8,128)}, f32[8,128,256]{2,1,0:T(8,128)}, u32[]{:S(2)}, u32[]{:S(2)}) collective-permute-start(f32[8,128,256]{2,1,0:T(8,128)} %get-tuple-element.49), channel_id=1, source_target_pairs={{0,1},{1,2},{2,3},{3,0},{4,5},{5,6},{6,7},{7,4},{8,9},{9,10},{10,1... | collective-permute-start | bytes 3145736 | tf_op jit(solution)/shard_map/ppermute | solution.py:267
  253.4 79.5 %collective-permute-start.11 = (f32[8,128,256]{2,1,0:T(8,128)}, f32[8,128,256]{2,1,0:T(8,128)}, u32[]{:S(2)}, u32[]{:S(2)}) collective-permute-start(f32[8,128,256]{2,1,0:T(8,128)} %get-tuple-element.51), channel_id=1, source_target_pairs={{0,2},{1,3},{2,0},{3,1},{4,6},{5,7},{6,4},{7,5},{8,10},{9,11},{10,... | collective-permute-start | bytes 3145736 | tf_op jit(solution)/shard_map/ppermute | solution.py:267
  263.9 69.0 %collective-permute-start.13 = (f32[8,128,256]{2,1,0:T(8,128)}, f32[8,128,256]{2,1,0:T(8,128)}, u32[]{:S(2)}, u32[]{:S(2)}) collective-permute-start(f32[8,128,256]{2,1,0:T(8,128)} %get-tuple-element.53), channel_id=1, source_target_pairs={{0,3},{1,0},{2,1},{3,2},{4,7},{5,4},{6,5},{7,6},{8,11},{9,8},{10,9... | collective-permute-start | bytes 3145736 | tf_op jit(solution)/shard_map/ppermute | solution.py:267
  287.6 65.9 %collective-permute-start.6 = (f32[4,128,512]{2,1,0:T(8,128)}, f32[4,128,512]{2,1,0:T(8,128)}, u32[]{:S(2)}, u32[]{:S(2)}) collective-permute-start(f32[4,128,512]{2,1,0:T(8,128)} %get-tuple-element.44), channel_id=1, source_target_pairs={{0,1},{1,2},{2,3},{3,0},{4,5},{5,6},{6,7},{7,4},{8,9},{9,10},{10,1... | collective-permute-start | bytes 3145736 | tf_op jit(solution)/shard_map/ppermute | solution.py:267
  302.6 125.0 %collective-permute-start.3 = (f32[3,128,512]{2,1,0:T(8,128)}, f32[3,128,512]{2,1,0:T(8,128)}, u32[]{:S(2)}, u32[]{:S(2)}) collective-permute-start(f32[3,128,512]{2,1,0:T(8,128)} %get-tuple-element.39), channel_id=1, source_target_pairs={{0,1},{1,2},{2,3},{3,0},{4,5},{5,6},{6,7},{7,4},{8,9},{9,10},{10,1... | collective-permute-start | bytes 2359304 | tf_op jit(solution)/shard_map/ppermute | solution.py:267
  308.8 120.8 %collective-permute-start.4 = (f32[3,128,512]{2,1,0:T(8,128)}, f32[3,128,512]{2,1,0:T(8,128)}, u32[]{:S(2)}, u32[]{:S(2)}) collective-permute-start(f32[3,128,512]{2,1,0:T(8,128)} %get-tuple-element.40), channel_id=1, source_target_pairs={{0,2},{1,3},{2,0},{3,1},{4,6},{5,7},{6,4},{7,5},{8,10},{9,11},{10,... | collective-permute-start | bytes 2359304 | tf_op jit(solution)/shard_map/ppermute | solution.py:267
  332.9 96.7 %collective-permute-start.5 = (f32[3,128,512]{2,1,0:T(8,128)}, f32[3,128,512]{2,1,0:T(8,128)}, u32[]{:S(2)}, u32[]{:S(2)}) collective-permute-start(f32[3,128,512]{2,1,0:T(8,128)} %get-tuple-element.41), channel_id=1, source_target_pairs={{0,3},{1,0},{2,1},{3,2},{4,7},{5,4},{6,5},{7,6},{8,11},{9,8},{10,9... | collective-permute-start | bytes 2359304 | tf_op jit(solution)/shard_map/ppermute | solution.py:267
  332.9 77.4 %collective-permute-start.7 = (f32[4,128,512]{2,1,0:T(8,128)}, f32[4,128,512]{2,1,0:T(8,128)}, u32[]{:S(2)}, u32[]{:S(2)}) collective-permute-start(f32[4,128,512]{2,1,0:T(8,128)} %get-tuple-element.45), channel_id=1, source_target_pairs={{0,2},{1,3},{2,0},{3,1},{4,6},{5,7},{6,4},{7,5},{8,10},{9,11},{10,... | collective-permute-start | bytes 3145736 | tf_op jit(solution)/shard_map/ppermute | solution.py:267
  353.5 56.9 %collective-permute-start.8 = (f32[4,128,512]{2,1,0:T(8,128)}, f32[4,128,512]{2,1,0:T(8,128)}, u32[]{:S(2)}, u32[]{:S(2)}) collective-permute-start(f32[4,128,512]{2,1,0:T(8,128)} %get-tuple-element.46), channel_id=1, source_target_pairs={{0,3},{1,0},{2,1},{3,2},{4,7},{5,4},{6,5},{7,6},{8,11},{9,8},{10,9... | collective-permute-start | bytes 3145736 | tf_op jit(solution)/shard_map/ppermute | solution.py:267
  410.4 31.4 %collective-permute-start = (f32[1,128,512]{2,1,0:T(8,128)}, f32[1,128,512]{2,1,0:T(8,128)}, u32[]{:S(2)}, u32[]{:S(2)}) collective-permute-start(f32[1,128,512]{2,1,0:T(8,128)} %get-tuple-element.32), channel_id=1, source_target_pairs={{0,1},{1,2},{2,3},{3,0},{4,5},{5,6},{6,7},{7,4},{8,9},{9,10},{10,1... | collective-permute-start | bytes 786440 | tf_op jit(solution)/shard_map/ppermute | solution.py:267
  410.4 31.4 %collective-permute-start.1 = (f32[1,128,512]{2,1,0:T(8,128)}, f32[1,128,512]{2,1,0:T(8,128)}, u32[]{:S(2)}, u32[]{:S(2)}) collective-permute-start(f32[1,128,512]{2,1,0:T(8,128)} %get-tuple-element.33), channel_id=1, source_target_pairs={{0,2},{1,3},{2,0},{3,1},{4,6},{5,7},{6,4},{7,5},{8,10},{9,11},{10,... | collective-permute-start | bytes 786440 | tf_op jit(solution)/shard_map/ppermute | solution.py:267
  427.6 14.1 %collective-permute-start.2 = (f32[1,128,512]{2,1,0:T(8,128)}, f32[1,128,512]{2,1,0:T(8,128)}, u32[]{:S(2)}, u32[]{:S(2)}) collective-permute-start(f32[1,128,512]{2,1,0:T(8,128)} %get-tuple-element.34), channel_id=1, source_target_pairs={{0,3},{1,0},{2,1},{3,2},{4,7},{5,4},{6,5},{7,6},{8,11},{9,8},{10,9... | collective-permute-start | bytes 786440 | tf_op jit(solution)/shard_map/ppermute | solution.py:267
